TPU v7x, 8 devices: a whole 2x2x1 slice. The times are simulated.
8 devices in a mesh: dp: 2 (over z, y), fsdp: 4 (over x, core).
Axes of the slice: x: 2, y: 2, z: 1, core: 2. Of those that a mesh axis runs over, the one named last changes fastest.
Arguments:
- x_in: bfloat16 [128, 256, 512], P(('dp', 'fsdp'))
- grad_y: bfloat16 [128, 256, 512], P(('dp', 'fsdp'))
- norm_scale: bfloat16 [2, 512], P(None, 'fsdp')
- w_in: bfloat16 [2, 512, 4736], P(None, 'fsdp')
- w_out: bfloat16 [2, 2560, 512], P(None, 'fsdp')
Outputs:
- output 1: bfloat16 [128, 256, 512], P(('dp', 'fsdp'))
- output 2: bfloat16 [128, 256, 512], P(('dp', 'fsdp'))
- output 3: float32 [2, 512], P(None, 'fsdp')
- output 4: float32 [2, 512, 4736], P(None, 'fsdp')
- output 5: float32 [2, 2560, 512], P(None, 'fsdp')
All inputs are finite; a program needn't handle non-finite values.
Results may differ from a plain program's by a relative error of at most 0.0145983.
Values are sent between devices in bfloat16 or wider.
A program may use at most 1 GiB of HBM per device.

v0:
```python
import functools
import jax
import jax.numpy as jnp
from jax import lax
from jax.sharding import PartitionSpec as P


def rotary_tables(seq_len, head_dim):
    half_dim = head_dim // 2
    inv_freq = 10000.0 ** (-(jnp.arange(half_dim, dtype=jnp.float32) * 2.0 / head_dim))
    angles = jnp.arange(seq_len, dtype=jnp.float32)[:, None] * inv_freq[None, :]
    return jnp.cos(angles), jnp.sin(angles)


def rotate(vectors, cos_tab, sin_tab):
    half_dim = vectors.shape[-1] // 2
    lo_half = vectors[..., :half_dim]
    hi_half = vectors[..., half_dim:]
    return jnp.concatenate([lo_half * cos_tab - hi_half * sin_tab, hi_half * cos_tab + lo_half * sin_tab], axis=-1)


def layer_norm(hidden, gain_vec):
    hid_f32 = hidden.astype(jnp.float32)
    centered = hid_f32 - jnp.mean(hid_f32, axis=-1, keepdims=True)
    variance = jnp.mean(centered * centered, axis=-1, keepdims=True)
    return (centered * lax.rsqrt(variance + 1e-6) * gain_vec).astype(jnp.bfloat16)


def mix_block(projected, model_dim, ff_dim, head_dim):
    n_batch, seq_len, _ = projected.shape
    n_heads = model_dim // head_dim
    kv_end = model_dim + 2 * head_dim
    queries = projected[..., :model_dim].reshape(n_batch, seq_len, n_heads, head_dim).astype(jnp.float32) * head_dim ** -0.5
    key_vec = projected[..., model_dim:model_dim + head_dim].astype(jnp.float32)
    val_vec = projected[..., model_dim + head_dim:kv_end]
    gate_act = projected[..., kv_end:kv_end + ff_dim].astype(jnp.float32)
    up_act = projected[..., kv_end + ff_dim:].astype(jnp.float32)
    cos_tab, sin_tab = rotary_tables(seq_len, head_dim)
    q_rot = rotate(queries, cos_tab[:, None, :], sin_tab[:, None, :]).astype(jnp.bfloat16)
    k_rot = rotate(key_vec, cos_tab, sin_tab).astype(jnp.bfloat16)
    scores = jnp.einsum("crie,cle->cirl", q_rot, k_rot, preferred_element_type=jnp.float32)
    positions = jnp.arange(seq_len)
    scores = jnp.where(positions[:, None] >= positions[None, :], scores, -1e30)
    attn_probs = jax.nn.softmax(scores, axis=-1).astype(jnp.bfloat16)
    attn_out = jnp.einsum("cirl,cle->crie", attn_probs, val_vec, preferred_element_type=jnp.float32)
    attn_out = attn_out.astype(jnp.bfloat16).reshape(n_batch, seq_len, model_dim)
    mlp_out = (jax.nn.silu(gate_act) * up_act).astype(jnp.bfloat16)
    return jnp.concatenate([attn_out, mlp_out], axis=-1)


def solution(mesh):
    fsdp_size = mesh.shape["fsdp"]
    batch_spec = P(("dp", "fsdp"), None, None)
    scale_spec = P(None, "fsdp")
    weight_spec = P(None, "fsdp", None)

    def gather_layer(norm_scale, w_in, w_out, layer_idx):
        scale_full = lax.all_gather(norm_scale[layer_idx], "fsdp", axis=0, tiled=True).astype(jnp.float32)
        w_in_full = lax.all_gather(w_in[layer_idx], "fsdp", axis=0, tiled=True)
        w_out_full = lax.all_gather(w_out[layer_idx], "fsdp", axis=0, tiled=True)
        return scale_full, w_in_full, w_out_full

    def reduce_grad(part_sum):
        shard_sum = lax.psum_scatter(part_sum, "fsdp", scatter_dimension=0, tiled=True)
        return lax.psum(shard_sum, "dp")

    def device_step(x_in, grad_y, norm_scale, w_in, w_out):
        n_layers = w_in.shape[0]
        model_dim = x_in.shape[-1]
        ff_dim = w_out.shape[1] * fsdp_size - model_dim
        head_dim = (w_in.shape[2] - model_dim - 2 * ff_dim) // 2
        mix_fn = functools.partial(mix_block, model_dim=model_dim, ff_dim=ff_dim, head_dim=head_dim)
        saved_acts = []
        hidden = x_in
        for layer_idx in range(n_layers):
            scale_full, w_in_full, w_out_full = gather_layer(norm_scale, w_in, w_out, layer_idx)
            normed = layer_norm(hidden, scale_full)
            projected = jnp.einsum("bsd,de->bse", normed, w_in_full, preferred_element_type=jnp.float32).astype(jnp.bfloat16)
            mixed_out = mix_fn(projected)
            block_out = jnp.einsum("bsf,fd->bsd", mixed_out, w_out_full, preferred_element_type=jnp.float32)
            saved_acts.append((hidden, normed, projected, mixed_out))
            hidden = (hidden.astype(jnp.float32) + block_out).astype(jnp.bfloat16)
        grad_hidden = grad_y
        scale_grads = []
        in_grads = []
        out_grads = []
        for layer_idx in reversed(range(n_layers)):
            layer_in, normed, projected, mixed_out = saved_acts[layer_idx]
            scale_full, w_in_full, w_out_full = gather_layer(norm_scale, w_in, w_out, layer_idx)
            part_w_out = jnp.einsum("bsf,bsd->fd", mixed_out, grad_hidden, preferred_element_type=jnp.float32)
            grad_mixed = jnp.einsum("bsd,fd->bsf", grad_hidden, w_out_full, preferred_element_type=jnp.float32).astype(jnp.bfloat16)
            grad_proj = jax.vjp(mix_fn, projected)[1](grad_mixed)[0]
            part_w_in = jnp.einsum("bsd,bse->de", normed, grad_proj, preferred_element_type=jnp.float32)
            grad_normed = jnp.einsum("bse,de->bsd", grad_proj, w_in_full, preferred_element_type=jnp.float32).astype(jnp.bfloat16)
            grad_in, part_scale = jax.vjp(layer_norm, layer_in, scale_full)[1](grad_normed)
            grad_hidden = (grad_hidden.astype(jnp.float32) + grad_in.astype(jnp.float32)).astype(jnp.bfloat16)
            scale_grads.append(reduce_grad(part_scale))
            in_grads.append(reduce_grad(part_w_in))
            out_grads.append(reduce_grad(part_w_out))
        return (hidden, grad_hidden, jnp.stack(scale_grads[::-1]), jnp.stack(in_grads[::-1]), jnp.stack(out_grads[::-1]))

    return jax.shard_map(
        device_step,
        mesh=mesh,
        in_specs=(batch_spec, batch_spec, scale_spec, weight_spec, weight_spec),
        out_specs=(batch_spec, batch_spec, scale_spec, weight_spec, weight_spec),
        check_vma=False,
    )
```

profile of v0, /device:TPU:0, one launch (start us, length us, event | category | flops | bytes accessed | tf_op | source)
XLA Modules:
  0.0 1003.7 jit_solution(2824752309040292870)
XLA Ops:
  37.0 17.7 %convolution_convert_fusion.3 = bf16[16,256,2560]{1,2,0:T(8,128)(2,1)} fusion(bf16[16,256,512]{2,1,0:T(8,128)(2,1)} %param.6, bf16[1,2560,512]{2,1,0:T(8,128)(2,1)} %all-gather.17.cloned.1.call-done), kind=kOutput, calls=%fused_computation.63 | convolution fusion | flops 10747904000 | bytes 27787264 | tf_op jit(solution)/shard_map/bsd,fd->bsf/dot_general | solution.py:91
  59.4 13.8 %all-gather.11.cloned.1.call-done = bf16[1,512,4736]{2,1,0:T(8,128)(2,1)} async-done(((bf16[1,128,4736]{2,1,0:T(8,128)(2,1)}), bf16[1,512,4736]{2,1,0:T(8,128)(2,1)}) %all-gather.11.cloned.1.call-update) | async-done | bytes 4849680 | tf_op jit(solution)/shard_map/all_gather | solution.py:59
  73.2 28.0 %convolution_convert_fusion.1 = bf16[16,256,4736]{1,2,0:T(8,128)(2,1)} fusion(bf16[1,512,4736]{2,1,0:T(8,128)(2,1)} %all-gather.11.cloned.1.call-done, bf16[16,256,512]{2,1,0:T(8,128)(2,1)} %param.5, f32[512]{0:T(512)S(1)} %bitcast.222, f32[16,256]{1,0:T(8,128)S(1)} %fusion.96, f32[16,256]{1,0:T(8,128)S(1)} %broadcast_multiply_fusion.1), kind=kOutput, calls=%fused_computation.21 | convolution fusion | flops 19894108160 | bytes 47876096 | tf_op jit(solution)/shard_map/bsd,de->bse/dot_general | solution.py:78
  105.8 21.8 %fusion = bf16[16,256,2048]{1,2,0:T(8,128)(2,1)} fusion(bf16[16,256,4736]{1,2,0:T(8,128)(2,1)} %convolution_convert_fusion.1), kind=kLoop, calls=%fused_computation.22 | loop fusion | flops 67108864 | bytes 50331648 | tf_op jit(solution)/shard_map/convert_element_type | solution.py:47
  129.3 13.3 %fusion.28 = (f32[16,8,256]{2,1,0:T(8,128)S(1)}, f32[16,256,256,8]{2,1,3,0:T(8,128)}) fusion(pred[256,256]{0,1:T(8,128)(4,1)S(1)} %iota_compare_fusion.1, bf16[16,256,8,32]{1,3,2,0:T(8,128)(2,1)S(1)} %get-tuple-element.31, bf16[16,256,8,32]{1,3,2,0:T(8,128)(2,1)S(1)} %get-tuple-element.30, bf16[16,256,32]{1,2,0:T(8,128)(2,1)S(1)} %get-tuple-element.43, ...), kind=kOutput, calls=%fused_computation.56 | convolution fusion | flops 1099923456 | bytes 38469632 | tf_op jit(solution)/shard_map/crie,cle->cirl/dot_general | solution.py:41
  142.6 14.3 %fusion.30 = f32[16,8,256]{2,1,0:T(8,128)S(1)} fusion(f32[16,256,256,8]{2,1,3,0:T(8,128)} %get-tuple-element.49, f32[16,8,256]{2,1,0:T(8,128)S(1)} %get-tuple-element.48, pred[256,256]{0,1:T(8,128)(4,1)S(1)} %iota_compare_fusion.1), kind=kLoop, calls=%fused_computation.58 | loop fusion | flops 25133056 | bytes 33882112 | tf_op jit(solution)/shard_map/reduce_sum | solution.py:44
  173.1 11.0 %convolution_convert_fusion.7 = bf16[16,64,8,256]{3,1,2,0:T(8,128)(2,1)} fusion(bf16[16,8,256,256]{2,3,1,0:T(8,128)(2,1)} %divide_convert_fusion.1, bf16[16,256,4736]{1,2,0:T(8,128)(2,1)} %convolution_convert_fusion.1), kind=kOutput, calls=%fused_computation.144 | convolution fusion | flops 1075838976 | bytes 21495808 | tf_op jit(solution)/shard_map/cirl,cle->crie/dot_general | solution.py:45
  184.2 18.5 %convert_reduce_fusion = (f32[16,256]{1,0:T(8,128)S(1)}, bf16[16,256,512]{2,1,0:T(8,128)(2,1)}) fusion(bf16[1,2560,512]{2,1,0:T(8,128)(2,1)} %all-gather.13.cloned.1.call-done, bf16[16,256,2048]{1,2,0:T(8,128)(2,1)} %fusion, bf16[16,256,512]{1,2,0:T(8,128)(2,1)} %bitcast.200, bf16[16,256,512]{2,1,0:T(8,128)(2,1)} %param.5), kind=kOutput, calls=%fused_computation.72 | convolution fusion | flops 10789842944 | bytes 31997952 | tf_op jit(solution)/shard_map/bsf,fd->bsd/dot_general | solution.py:80
  206.0 28.3 %convolution_convert_fusion = bf16[16,256,4736]{1,2,0:T(8,128)(2,1)} fusion(bf16[1,512,4736]{2,1,0:T(8,128)(2,1)} %all-gather.15.cloned.1.call-done, bf16[16,256,512]{2,1,0:T(8,128)(2,1)} %get-tuple-element.51, f32[512]{0:T(512)S(1)} %bitcast.227, f32[16,256]{1,0:T(8,128)S(1)} %fusion.97, f32[16,256]{1,0:T(8,128)S(1)} %broadcast_multiply_fusion), kind=kOutput, calls=%fused_computation.20 | convolution fusion | flops 19894108160 | bytes 47876096 | tf_op jit(solution)/shard_map/bsd,de->bse/dot_general | solution.py:78
  240.1 13.3 %fusion.29 = (f32[16,8,256]{2,1,0:T(8,128)S(1)}, f32[16,256,256,8]{2,1,3,0:T(8,128)}) fusion(pred[256,256]{0,1:T(8,128)(4,1)S(1)} %iota_compare_fusion.1, bf16[16,256,8,32]{1,3,2,0:T(8,128)(2,1)S(1)} %get-tuple-element.29, bf16[16,256,8,32]{1,3,2,0:T(8,128)(2,1)S(1)} %get-tuple-element.28, bf16[16,256,32]{1,2,0:T(8,128)(2,1)S(1)} %get-tuple-element.41, ...), kind=kOutput, calls=%fused_computation.57 | convolution fusion | flops 1099923456 | bytes 38469632 | tf_op jit(solution)/shard_map/crie,cle->cirl/dot_general | solution.py:41
  253.4 13.9 %fusion.31 = f32[16,8,256]{2,1,0:T(8,128)S(1)} fusion(f32[16,256,256,8]{2,1,3,0:T(8,128)} %get-tuple-element.53, f32[16,8,256]{2,1,0:T(8,128)S(1)} %get-tuple-element.52, pred[256,256]{0,1:T(8,128)(4,1)S(1)} %iota_compare_fusion.1), kind=kLoop, calls=%fused_computation.59 | loop fusion | flops 25133056 | bytes 33882112 | tf_op jit(solution)/shard_map/reduce_sum | solution.py:44
  267.3 26.1 %fusion.9 = (f32[16,8,256]{2,1,0:T(8,128)S(1)}, bf16[16,8,256,256]{2,3,1,0:T(8,128)(2,1)}, bf16[16,8,256,256]{2,3,1,0:T(8,128)(2,1)}) fusion(f32[16,256,256,8]{2,1,3,0:T(8,128)} %get-tuple-element.53, f32[16,8,256]{2,1,0:T(8,128)S(1)} %multiply_divide_fusion.1, f32[16,8,256]{2,1,0:T(8,128)S(1)} %get-tuple-element.52, ...), kind=kOutput, calls=%fused_computation.31 | convolution fusion | flops 1149206528 | bytes 72417280 | tf_op jit(solution)/shard_map/transpose(jvp(cirl,cle->crie))/dot_general | solution.py:45
  293.5 18.8 %fusion.91 = f32[16,256,64]{1,2,0:T(8,128)S(1)} fusion(bf16[16,256,8,32]{1,3,2,0:T(8,128)(2,1)S(1)} %get-tuple-element.29, bf16[16,256,8,32]{1,3,2,0:T(8,128)(2,1)S(1)} %get-tuple-element.28, bf16[16,8,256,256]{2,3,1,0:T(8,128)(2,1)} %get-tuple-element.54, f32[16,256,256,8]{2,1,3,0:T(8,128)} %get-tuple-element.53, f32[16,256,8]{1,2,0:T(8,128)S(1)} %bitcast.218, ...), kind=kOutput, calls=%fused_computation.157 | convolution fusion | flops 1141374976 | bytes 56033280 | tf_op jit(solution)/shard_map/transpose(jvp(crie,cle->cirl))/dot_general | solution.py:41
  312.2 23.1 %convert_convert_fusion.1 = f32[16,256,8,64]{1,3,2,0:T(8,128)} fusion(bf16[16,256,32]{1,2,0:T(8,128)(2,1)S(1)} %get-tuple-element.41, bf16[16,256,32]{1,2,0:T(8,128)(2,1)S(1)} %get-tuple-element.40, bf16[16,8,256,256]{2,3,1,0:T(8,128)(2,1)} %get-tuple-element.54, f32[16,256,256,8]{2,1,3,0:T(8,128)} %get-tuple-element.53, f32[16,256,8]{1,2,0:T(8,128)S(1)} %bitcast.219, ...), kind=kOutput, calls=%fused_computation.132 | convolution fusion | flops 1137704960 | bytes 59703296 | tf_op jit(solution)/shard_map/transpose(jvp(crie,cle->cirl))/dot_general | solution.py:41
  335.4 41.9 %fusion.2 = (bf16[16,256,2048]{1,2,0:T(8,128)(2,1)}, bf16[16,256,2048]{1,2,0:T(8,128)(2,1)}, bf16[16,256,2048]{1,2,0:T(8,128)(2,1)}) fusion(bf16[16,256,2560]{1,2,0:T(8,128)(2,1)} %convolution_convert_fusion.3, bf16[16,256,4736]{1,2,0:T(8,128)(2,1)} %convolution_convert_fusion), kind=kLoop, calls=%fused_computation.24 | loop fusion | flops 159383552 | bytes 100663296 | tf_op jit(solution)/shard_map/transpose(jvp())/convert_element_type | solution.py:37
  386.1 11.2 %convolution_convert_fusion.6 = bf16[16,64,8,256]{3,1,2,0:T(8,128)(2,1)} fusion(bf16[16,8,256,256]{2,3,1,0:T(8,128)(2,1)} %get-tuple-element.23, bf16[16,256,4736]{1,2,0:T(8,128)(2,1)} %convolution_convert_fusion), kind=kOutput, calls=%fused_computation.143 | convolution fusion | flops 1075838976 | bytes 21495808 | tf_op jit(solution)/shard_map/cirl,cle->crie/dot_general | solution.py:45
  404.6 27.4 %fusion.56 = (f32[16,256]{1,0:T(8,128)S(1)}, bf16[16,256,512]{2,1,0:T(8,128)(2,1)S(1)}) fusion(bf16[16,256,512]{2,1,0:T(8,128)(2,1)S(1)} %copy-done.3, f32[512]{0:T(512)S(1)} %bitcast.228, f32[16,256]{1,0:T(8,128)S(1)} %copy-done.40, bf16[1,512,4736]{2,1,0:T(8,128)(2,1)} %all-gather.15.cloned.1.call-done, bf16[16,256,512]{1,2,0:T(8,128)(2,1)S(1)} %bitcast.202, ...), kind=kOutput, calls=%fused_computation.102 | convolution fusion | flops 20072886272 | bytes 52070400 | tf_op jit(solution)/shard_map/bse,de->bsd/dot_general | solution.py:94
  444.5 16.7 %fusion.60 = f32[2560,512]{1,0:T(8,128)} fusion(bf16[16,256,512]{2,1,0:T(8,128)(2,1)S(1)} %add_convert_fusion.2, bf16[16,256,2048]{1,2,0:T(8,128)(2,1)} %fusion, bf16[16,256,512]{1,2,0:T(8,128)(2,1)} %bitcast.201), kind=kOutput, calls=%fused_computation.116 | convolution fusion | flops 10779361280 | bytes 30408704 | tf_op jit(solution)/shard_map/bsf,bsd->fd/dot_general | solution.py:90
  461.3 18.1 %convolution_convert_fusion.2 = bf16[16,256,2560]{1,2,0:T(8,128)(2,1)} fusion(bf16[16,256,512]{2,1,0:T(8,128)(2,1)} %copy-done.5, bf16[1,2560,512]{2,1,0:T(8,128)(2,1)} %all-gather.13.cloned.1.call-done), kind=kOutput, calls=%fused_computation.62 | convolution fusion | flops 10747904000 | bytes 27787264 | tf_op jit(solution)/shard_map/bsd,fd->bsf/dot_general | solution.py:91
  482.0 21.3 %fusion.15 = (f32[16,8,256]{2,1,0:T(8,128)S(1)}, bf16[16,8,256,256]{2,3,1,0:T(8,128)(2,1)}) fusion(f32[16,256,256,8]{2,1,3,0:T(8,128)} %get-tuple-element.49, f32[16,8,256]{2,1,0:T(8,128)S(1)} %multiply_divide_fusion, f32[16,8,256]{2,1,0:T(8,128)S(1)} %copy-done.27, pred[256,256]{0,1:T(8,128)(4,1)S(1)} %copy-done.13, ...), kind=kOutput, calls=%fused_computation.37 | convolution fusion | flops 1132429312 | bytes 55508992 | tf_op jit(solution)/shard_map/transpose(jvp(cirl,cle->crie))/dot_general | solution.py:45
  503.4 18.6 %fusion.93 = f32[16,256,64]{1,2,0:T(8,128)S(1)} fusion(bf16[16,256,8,32]{1,3,2,0:T(8,128)(2,1)S(1)} %copy-done.11, bf16[16,256,8,32]{1,3,2,0:T(8,128)(2,1)S(1)} %copy-done.9, bf16[16,8,256,256]{2,3,1,0:T(8,128)(2,1)} %get-tuple-element.58, f32[16,256,256,8]{2,1,3,0:T(8,128)} %get-tuple-element.49, f32[16,256,8]{1,2,0:T(8,128)S(1)} %bitcast.214, ...), kind=kOutput, calls=%fused_computation.159 | convolution fusion | flops 1141374976 | bytes 56033280 | tf_op jit(solution)/shard_map/transpose(jvp(crie,cle->cirl))/dot_general | solution.py:41
  522.1 22.9 %convert_convert_fusion = f32[16,256,8,64]{1,3,2,0:T(8,128)} fusion(bf16[16,256,32]{1,2,0:T(8,128)(2,1)S(1)} %copy-done.34, bf16[16,256,32]{1,2,0:T(8,128)(2,1)S(1)} %copy-done.32, bf16[16,8,256,256]{2,3,1,0:T(8,128)(2,1)} %get-tuple-element.58, f32[16,256,256,8]{2,1,3,0:T(8,128)} %get-tuple-element.49, f32[16,256,8]{1,2,0:T(8,128)S(1)} %bitcast.215, ...), kind=kOutput, calls=%fused_computation.129 | convolution fusion | flops 1137704960 | bytes 59703296 | tf_op jit(solution)/shard_map/transpose(jvp(crie,cle->cirl))/dot_general | solution.py:41
  545.1 19.0 %fusion.61 = f32[2560,512]{1,0:T(8,128)} fusion(bf16[16,256,512]{2,1,0:T(8,128)(2,1)} %param.6, bf16[16,256,2048]{1,2,0:T(8,128)(2,1)} %get-tuple-element.21, bf16[16,256,512]{1,2,0:T(8,128)(2,1)} %bitcast.198), kind=kOutput, calls=%fused_computation.117 | convolution fusion | flops 10779361280 | bytes 30408704 | tf_op jit(solution)/shard_map/bsf,bsd->fd/dot_general | solution.py:90
  573.2 34.5 %fusion.3 = (bf16[16,256,2048]{1,2,0:T(8,128)(2,1)}, bf16[16,256,2048]{1,2,0:T(8,128)(2,1)}) fusion(bf16[16,256,2560]{1,2,0:T(8,128)(2,1)} %convolution_convert_fusion.2, bf16[16,256,4736]{1,2,0:T(8,128)(2,1)} %convolution_convert_fusion.1), kind=kLoop, calls=%fused_computation.25 | loop fusion | flops 142606336 | bytes 83886080 | tf_op jit(solution)/shard_map/transpose(jvp())/convert_element_type | solution.py:37
  613.4 10.9 %fusion.89 = bf16[16,256,64]{1,2,0:T(8,128)(2,1)S(1)} fusion(bf16[16,8,256,256]{2,3,1,0:T(8,128)(2,1)} %divide_convert_fusion.1, bf16[16,64,8,256]{3,1,2,0:T(8,128)(2,1)S(1)} %bitcast.209), kind=kOutput, calls=%fused_computation.155 | convolution fusion | flops 1074003968 | bytes 21495808 | tf_op jit(solution)/shard_map/transpose(jvp(cirl,cle->crie))/dot_general | solution.py:45
  624.4 36.9 %convolution_bitcast_fusion.1 = f32[512,4736]{1,0:T(8,128)} fusion(bf16[16,256,512]{2,1,0:T(8,128)(2,1)S(1)} %copy-done.1, f32[512]{0:T(512)S(1)} %bitcast.223, f32[16,256]{1,0:T(8,128)S(1)} %copy-done.47, f32[16,256]{1,0:T(8,128)S(1)} %copy-done.38, bf16[16,256,512]{1,2,0:T(8,128)(2,1)S(1)} %bitcast.204, bf16[16,256,64]{1,2,0:T(8,128)(2,1)S(1)} %add_convert_fusion.6, ...), kind=kOutput, calls=%fused_computation.113 | convolution fusion | flops 20068696064 | bytes 52725760 | tf_op jit(solution)/shard_map/bsd,bse->de/dot_general | solution.py:93
  662.5 38.2 %convolution_bitcast_fusion = f32[512,4736]{1,0:T(8,128)} fusion(bf16[16,256,512]{2,1,0:T(8,128)(2,1)} %get-tuple-element.51, f32[512]{0:T(512)S(1)} %bitcast.231, f32[16,256]{1,0:T(8,128)S(1)} %copy-done.51, f32[16,256]{1,0:T(8,128)S(1)} %copy-done.41, bf16[16,256,512]{1,2,0:T(8,128)(2,1)} %bitcast.203, bf16[16,256,64]{1,2,0:T(8,128)(2,1)S(1)} %copy-done.36, ...), kind=kOutput, calls=%fused_computation.112 | convolution fusion | flops 20068696064 | bytes 52725760 | tf_op jit(solution)/shard_map/bsd,bse->de/dot_general | solution.py:93
  702.7 33.3 %reduce-scatter.5.cloned.1.call-done = f32[128,4736]{1,0:T(8,128)} async-done(((f32[512,4736]{1,0:T(8,128)}), f32[128,4736]{1,0:T(8,128)}) %reduce-scatter.5.cloned.1.call-update) | async-done | bytes 2424848 | tf_op jit(solution)/shard_map/reduce_scatter | solution.py:64
  736.0 76.6 %reduce-scatter.7.cloned.1.call-done = f32[128,4736]{1,0:T(8,128)} async-done(((f32[512,4736]{1,0:T(8,128)}), f32[128,4736]{1,0:T(8,128)}) %reduce-scatter.7.cloned.1.call-update) | async-done | bytes 2424848 | tf_op jit(solution)/shard_map/reduce_scatter | solution.py:64
  812.6 27.3 %fusion.53 = (f32[16,256]{1,0:T(8,128)S(1)}, bf16[16,256,512]{2,1,0:T(8,128)(2,1)S(1)}) fusion(bf16[16,256,512]{2,1,0:T(8,128)(2,1)} %param.5, f32[512]{0:T(512)S(1)} %bitcast.224, f32[16,256]{1,0:T(8,128)S(1)} %copy-done.38, bf16[1,512,4736]{2,1,0:T(8,128)(2,1)} %all-gather.11.cloned.1.call-done, bf16[16,256,512]{1,2,0:T(8,128)(2,1)} %bitcast.205, ...), kind=kOutput, calls=%fused_computation.99 | convolution fusion | flops 20072886272 | bytes 52070400 | tf_op jit(solution)/shard_map/bse,de->bsd/dot_general | solution.py:94
  865.5 17.5 %fusion.57 = bf16[16,256,512]{2,1,0:T(8,128)(2,1)} fusion(bf16[16,256,512]{2,1,0:T(8,128)(2,1)S(1)} %copy-done.4, bf16[16,256,2048]{1,2,0:T(8,128)(2,1)} %get-tuple-element.21, bf16[16,256,512]{1,2,0:T(8,128)(2,1)} %bitcast.199, bf16[1,2560,512]{2,1,0:T(8,128)(2,1)} %all-gather.17.cloned.1.call-done), kind=kOutput, calls=%fused_computation.103 | convolution fusion | flops 10785652736 | bytes 31981568 | tf_op jit(solution)/shard_map/bsf,fd->bsd/dot_general | solution.py:80
  883.0 105.5 %all-reduce.25.cloned.1.call-done = (f32[1,128,4736]{2,1,0:T(8,128)}, f32[1,128,4736]{2,1,0:T(8,128)}, f32[1,640,512]{2,1,0:T(8,128)}, f32[1,640,512]{2,1,0:T(8,128)}) async-done(((f32[1,128,4736]{2,1,0:T(8,128)}, f32[1,128,4736]{2,1,0:T(8,128)}, f32[1,640,512]{2,1,0:T(8,128)}, f32[1,640,512]{2,1,0:T(8,128)}), (f32[1,128,4736]{2,1,0:T(8,128)}, f32[1,128,4736]{2,1,0:T(8,128)}, f32[1,640,512]{2,1,0:T(8,128)}, ...) | async-done | bytes 7471120 | tf_op jit(solution)/shard_map/psum | solution.py:65
  (208 shorter events, 147.9 us)
Async XLA Ops:
  7.2 29.9 %all-gather.17.cloned.1.call-start = ((), (), s32[]{:S(2)}) async-start(), calls=%async_computation.11 | async-start | bytes 3276800 | tf_op jit(solution)/shard_map/all_gather | solution.py:60
  9.7 63.5 %all-gather.11.cloned.1.call-start = ((), (), s32[]{:S(2)}) async-start(), calls=%async_computation.8 | async-start | bytes 6062080 | tf_op jit(solution)/shard_map/all_gather | solution.py:59
  13.0 171.2 %all-gather.13.cloned.1.call-start = ((), (), s32[]{:S(2)}) async-start(), calls=%async_computation.9 | async-start | bytes 3276800 | tf_op jit(solution)/shard_map/all_gather | solution.py:60
  13.7 192.2 %all-gather.15.cloned.1.call-start = ((), (), s32[]{:S(2)}) async-start(), calls=%async_computation.10 | async-start | bytes 6062080 | tf_op jit(solution)/shard_map/all_gather | solution.py:59
  14.3 688.4 %reduce-scatter.9.cloned.1.call-start = ((), (), s32[]{:S(2)}) async-start(), calls=%async_computation.6 | async-start | bytes 6553600 | tf_op jit(solution)/shard_map/reduce_scatter | solution.py:64
  14.4 252.9 %copy-start.12 = (pred[256,256]{0,1:T(8,128)(4,1)}, pred[256,256]{0,1:T(8,128)(4,1)S(1)}, u32[]{:S(2)}) copy-start(pred[256,256]{0,1:T(8,128)(4,1)S(1)} %iota_compare_fusion.1) | copy-start | bytes 196612
  18.2 55.0 %copy-start.37 = (f32[16,256]{1,0:T(8,128)}, f32[16,256]{1,0:T(8,128)S(1)}, u32[]{:S(2)}) copy-start(f32[16,256]{1,0:T(8,128)S(1)} %broadcast_multiply_fusion.1) | copy-start | bytes 49156
  21.5 33.3 %copy-start.42 = (f32[16,256]{1,0:T(8,128)}, f32[16,256]{1,0:T(8,128)S(1)}, u32[]{:S(2)}) copy-start(f32[16,256]{1,0:T(8,128)S(1)} %fusion.52) | copy-start | bytes 49156
  21.6 51.6 %copy-start.46 = (f32[16,256]{1,0:T(8,128)}, f32[16,256]{1,0:T(8,128)S(1)}, u32[]{:S(2)}) copy-start(f32[16,256]{1,0:T(8,128)S(1)} %fusion.96) | copy-start | bytes 49156
  30.2 43.0 %copy-start.54 = (f32[1,512]{1,0:T(1,128)}, f32[1,512]{1,0:T(1,128)S(1)}, u32[]{:S(2)}) copy-start(f32[1,512]{1,0:T(1,128)S(1)} %convert_element_type.306) | copy-start | bytes 6148
  30.5 209.5 %copy-start.20 = (f32[256,32]{0,1:T(8,128)}, f32[256,32]{0,1:T(8,128)S(1)}, u32[]{:S(2)}) copy-start(f32[256,32]{0,1:T(8,128)S(1)} %get-tuple-element.46) | copy-start | bytes 98308
  30.5 209.5 %copy-start.23 = (f32[256,32]{0,1:T(8,128)}, f32[256,32]{0,1:T(8,128)S(1)}, u32[]{:S(2)}) copy-start(f32[256,32]{0,1:T(8,128)S(1)} %get-tuple-element.47) | copy-start | bytes 98308
  184.2 21.8 %copy-start.56 = (f32[1,512]{1,0:T(1,128)S(1)}, f32[1,512]{1,0:T(1,128)}, u32[]{:S(2)}) copy-start(f32[1,512]{1,0:T(1,128)} %convert_element_type.307) | copy-start | bytes 6148
  202.6 31.6 %copy-start.39 = (f32[16,256]{1,0:T(8,128)}, f32[16,256]{1,0:T(8,128)S(1)}, u32[]{:S(2)}) copy-start(f32[16,256]{1,0:T(8,128)S(1)} %broadcast_multiply_fusion) | copy-start | bytes 49156
  205.9 28.4 %copy-start.44 = (f32[16,256]{1,0:T(8,128)}, f32[16,256]{1,0:T(8,128)S(1)}, u32[]{:S(2)}) copy-start(f32[16,256]{1,0:T(8,128)S(1)} %fusion.55) | copy-start | bytes 49156
  205.9 28.4 %copy-start.49 = (f32[16,256]{1,0:T(8,128)}, f32[16,256]{1,0:T(8,128)S(1)}, u32[]{:S(2)}) copy-start(f32[16,256]{1,0:T(8,128)S(1)} %fusion.97) | copy-start | bytes 49156
  267.3 26.1 %copy-start.52 = (pred[256,256]{1,0:T(8,128)(4,1)S(1)}, pred[256,256]{1,0:T(8,128)(4,1)}, u32[]{:S(2)}) copy-start(pred[256,256]{1,0:T(8,128)(4,1)} %iota_compare_fusion) | copy-start | bytes 196612
  335.4 41.9 %copy-start.17 = (bf16[16,256,512]{1,2,0:T(8,128)(2,1)S(1)}, bf16[16,256,512]{1,2,0:T(8,128)(2,1)}, u32[]{:S(2)}) copy-start(bf16[16,256,512]{1,2,0:T(8,128)(2,1)} %split.49) | copy-start | bytes 12582916
  402.3 29.8 %copy-start.35 = (bf16[16,256,64]{1,2,0:T(8,128)(2,1)}, bf16[16,256,64]{1,2,0:T(8,128)(2,1)S(1)}, u32[]{:S(2)}) copy-start(bf16[16,256,64]{1,2,0:T(8,128)(2,1)S(1)} %add_convert_fusion.7) | copy-start | bytes 1572868
  403.7 28.3 %copy-start.15 = (bf16[16,256,8,64]{1,3,2,0:T(8,128)(2,1)}, bf16[16,256,8,64]{1,3,2,0:T(8,128)(2,1)S(1)}, u32[]{:S(2)}) copy-start(bf16[16,256,8,64]{1,3,2,0:T(8,128)(2,1)S(1)} %multiply_convert_fusion.1) | copy-start | bytes 12582916
  404.6 27.5 %copy-start.45 = (f32[16,256]{1,0:T(8,128)S(1)}, f32[16,256]{1,0:T(8,128)}, u32[]{:S(2)}) copy-start(f32[16,256]{1,0:T(8,128)} %copy-done.44) | copy-start | bytes 49156
  404.6 27.5 %copy-start.50 = (f32[16,256]{1,0:T(8,128)S(1)}, f32[16,256]{1,0:T(8,128)}, u32[]{:S(2)}) copy-start(f32[16,256]{1,0:T(8,128)} %copy-done.49) | copy-start | bytes 49156
  481.9 21.4 %copy-start.18 = (bf16[16,256,512]{1,2,0:T(8,128)(2,1)}, bf16[16,256,512]{1,2,0:T(8,128)(2,1)S(1)}, u32[]{:S(2)}) copy-start(bf16[16,256,512]{1,2,0:T(8,128)(2,1)S(1)} %split.55) | copy-start | bytes 12582916
  482.0 21.4 %copy-start.9 = (bf16[16,256,8,32]{1,3,2,0:T(8,128)(2,1)S(1)}, bf16[16,256,8,32]{1,3,2,0:T(8,128)(2,1)}, u32[]{:S(2)}) copy-start(bf16[16,256,8,32]{1,3,2,0:T(8,128)(2,1)} %copy-done.8) | copy-start | bytes 6291460
  482.0 21.4 %copy-start.11 = (bf16[16,256,8,32]{1,3,2,0:T(8,128)(2,1)S(1)}, bf16[16,256,8,32]{1,3,2,0:T(8,128)(2,1)}, u32[]{:S(2)}) copy-start(bf16[16,256,8,32]{1,3,2,0:T(8,128)(2,1)} %copy-done.10) | copy-start | bytes 6291460
  545.0 157.7 %reduce-scatter.11.cloned.1.call-start = ((), (), s32[]{:S(2)}) async-start(), calls=%async_computation.7 | async-start | bytes 6553600 | tf_op jit(solution)/shard_map/reduce_scatter | solution.py:64
  607.8 128.2 %reduce-scatter.5.cloned.1.call-start = ((), (), s32[]{:S(2)}) async-start(), calls=%async_computation.4 | async-start | bytes 12124160 | tf_op jit(solution)/shard_map/reduce_scatter | solution.py:64
  661.3 151.2 %reduce-scatter.7.cloned.1.call-start = ((), (), s32[]{:S(2)}) async-start(), calls=%async_computation.5 | async-start | bytes 12124160 | tf_op jit(solution)/shard_map/reduce_scatter | solution.py:64
  700.8 287.8 %all-reduce.25.cloned.1.call-start = ((), (), s32[]{:S(2)}) async-start(), calls=%async_computation.12 | async-start | bytes 14942208 | tf_op jit(solution)/shard_map/psum | solution.py:65
  812.6 27.4 %copy-start.43 = (f32[16,256]{1,0:T(8,128)S(1)}, f32[16,256]{1,0:T(8,128)}, u32[]{:S(2)}) copy-start(f32[16,256]{1,0:T(8,128)} %copy-done.42) | copy-start | bytes 49156
  812.6 27.4 %copy-start.2 = (bf16[16,256,512]{2,1,0:T(8,128)(2,1)S(1)}, bf16[16,256,512]{2,1,0:T(8,128)(2,1)}, u32[]{:S(2)}) copy-start(bf16[16,256,512]{2,1,0:T(8,128)(2,1)} %param.5) | copy-start | bytes 12582916
  812.6 27.4 %copy-start.48 = (f32[16,256]{1,0:T(8,128)S(1)}, f32[16,256]{1,0:T(8,128)}, u32[]{:S(2)}) copy-start(f32[16,256]{1,0:T(8,128)} %copy-done.46) | copy-start | bytes 49156
  (41 other events, 389.6 us)
Sparse Core Ops, SparseCore 0:
  10.1 25.5 all-gather.16
  37.8 35.3 all-gather.10
  75.3 22.7 all-gather.12
  99.5 35.3 all-gather.14
  545.2 46.1 reduce-scatter.8
  607.9 46.0 reduce-scatter.10
  661.4 74.4 reduce-scatter.4
  738.5 73.9 reduce-scatter.6
  815.2 173.3 all-reduce.24
where the time goes:
time: 1010 us; the launch traced here: 1000 us
  matrix products  493 us (49%)
  waiting for transfers between devices  231 us (23%)
  other arithmetic  214 us (21%)
  blocking collectives  25.9 us (3%)
  local copies, waits for them, and re-layouts  24.2 us (2%)
  between operations  15.8 us (2%)
    dot_general x6, matrix products, mix_block(): jnp.einsum('crie,cle->cirl', q_rot, k_rot, preferred_element_type=jnp.flo...  110 us
    reduce_scatter x4, waiting for transfers between devices, reduce_grad(): lax.psum_scatter(part_sum, 'fsdp', scatter_dimension=0, tiled=True)  110 us
    psum x1, waiting for transfers between devices, reduce_grad(): return lax.psum(shard_sum, 'dp')  106 us
    dot_general x6, matrix products, mix_block(): jnp.einsum('cirl,cle->crie', attn_probs, val_vec, preferred_element_type=...  89.4 us
    convert_element_type x2, other arithmetic, mix_block(): up_act = projected[..., kv_end + ff_dim:].astype(jnp.float32)  76.4 us
    dot_general x2, matrix products, device_step(): jnp.einsum('bsd,bse->de', normed, grad_proj, preferred_element_type=jnp.f...  75.1 us
    dot_general x2, matrix products, device_step(): jnp.einsum('bsd,de->bse', normed, w_in_full, preferred_element_type=jnp.f...  56.3 us
    dot_general x2, matrix products, device_step(): jnp.einsum('bse,de->bsd', grad_proj, w_in_full, preferred_element_type=jn...  54.7 us
  transfers between devices with their start and end apart: 9, of which 4 were waited for; matrix products, arithmetic and copies ran while one was open for 37% of the time, Pallas kernels for 0%

commit v1 on v0

v1 whole, which is shorter than its diff:
```python
import functools
import jax
import jax.numpy as jnp
from jax import lax
from jax.experimental import pallas as pl
from jax.experimental.pallas import tpu as pltpu
from jax.sharding import PartitionSpec as P

F32 = jnp.float32
BF16 = jnp.bfloat16
SEQ = 256
HD = 64
D = 512
FF = 2048
QKV = D + 2 * HD
NEG = -1e30
VMEM_LIMIT = 60 * 1024 * 1024

TOK = 512


def dot(a, b):
    return jnp.dot(a, b, preferred_element_type=F32)


def dot_nt(a, b):
    return lax.dot_general(a, b, (((1,), (1,)), ((), ())), preferred_element_type=F32)


def dot_tn(a, b):
    return lax.dot_general(a, b, (((0,), (0,)), ((), ())), preferred_element_type=F32)


def owners():
    me = lax.axis_index("fsdp")
    x = me // 2
    c = me - 2 * x
    return [2 * x + c, 2 * x + (1 - c), 2 * (1 - x) + c, 2 * (1 - x) + (1 - c)]


def load_rows(groups, sem):
    own = owners()
    copies = []
    for pieces, dst in groups:
        rows = pieces[0].shape[0]
        for r in range(4):
            start = pl.multiple_of(own[r] * rows, rows)
            src = pieces[r].at[:, pl.ds(0, dst.shape[1])]
            cp = pltpu.make_async_copy(src, dst.at[pl.ds(start, rows), :], sem.at[len(copies)])
            cp.start()
            copies.append(cp)
    for cp in copies:
        cp.wait()


def lane_iota(shape):
    return lax.broadcasted_iota(jnp.int32, shape, len(shape) - 1)


def half_swap(z):
    n = z.shape[-1]
    lo = lax.rem(lane_iota(z.shape), HD) < HD // 2
    return jnp.where(lo, pltpu.roll(z, n - HD // 2, 1), pltpu.roll(z, HD // 2, 1))


HALF = SEQ // 2


def kv_tiles(kv):
    lo = lane_iota(kv.shape) < HD
    rolled = pltpu.roll(kv, HD, 1)
    zero = jnp.zeros_like(kv)
    return (jnp.where(lo, kv, zero), jnp.where(lo, zero, rolled),
            jnp.where(lo, rolled, zero), jnp.where(lo, zero, kv))


def tri_mask(n):
    key = lax.broadcasted_iota(jnp.int32, (HALF, n), 0)
    query = lax.rem(lax.broadcasted_iota(jnp.int32, (HALF, n), 1), HALF)
    return query >= key


def softmax_keys(s, n_keys, tri):
    out = []
    for i in range(2):
        sh = s[i * n_keys:(i + 1) * n_keys]
        sh = [sh[k * HALF:(k + 1) * HALF] for k in range(n_keys // HALF)]
        sh[-1] = jnp.where(tri, sh[-1], NEG)
        m = jnp.max(sh[-1], axis=0, keepdims=True)
        for t in sh[:-1]:
            m = jnp.maximum(m, jnp.max(t, axis=0, keepdims=True))
        e = [jnp.exp(t - m) for t in sh]
        l = jnp.sum(e[0], axis=0, keepdims=True)
        for t in e[1:]:
            l = l + jnp.sum(t, axis=0, keepdims=True)
        inv = 1.0 / l
        out.append([t * inv for t in e])
    return out


def fwd_attn_kernel(x_ref, gain_ref, c_ref, s_ref, w0, w1, w2, w3, h_ref, qkv_ref, o_ref, w_ref, sem):
    @pl.when(pl.program_id(0) == 0)
    def _():
        load_rows([((w0, w1, w2, w3), w_ref)], sem)

    x = x_ref[...].astype(F32)
    cen = x - jnp.mean(x, axis=-1, keepdims=True)
    var = jnp.mean(cen * cen, axis=-1, keepdims=True)
    h = (cen * lax.rsqrt(var + 1e-6) * gain_ref[...]).astype(BF16)
    h_ref[...] = h
    z_all = dot(h, w_ref[...]).astype(BF16)
    tri = tri_mask(128)
    for b in range(TOK // SEQ):
        r0 = b * SEQ
        zt = []
        for j in range(5):
            t = z_all[r0:r0 + SEQ, j * 128:(j + 1) * 128].astype(F32)
            tc = slice(0, 128) if j < 4 else slice(128, 256)
            t = (t * c_ref[:, tc] + half_swap(t) * s_ref[:, tc]).astype(BF16)
            qkv_ref[r0:r0 + SEQ, j * 128:(j + 1) * 128] = t
            zt.append(t)
        k0, k1, v0, v1 = kv_tiles(zt[4].astype(F32))
        k0, k1 = k0.astype(BF16), k1.astype(BF16)
        v0, v1 = v0.T.astype(BF16), v1.T.astype(BF16)
        for blk in range(2):
            nk = (blk + 1) * HALF
            rows = slice(blk * HALF, (blk + 1) * HALF)
            k_st = jnp.concatenate([k0[:nk], k1[:nk]], axis=0)
            v_t = jnp.concatenate([v0[:, :nk], v1[:, :nk]], axis=1)
            for g in range(2):
                q = jnp.concatenate([zt[2 * g + i][rows] for i in range(2)], axis=0)
                s = dot_nt(k_st, q)
                trib = jnp.concatenate([tri] * 2, axis=1)
                p = softmax_keys(s, nk, trib)
                pb = jnp.concatenate([t.astype(BF16) for ph in p for t in ph], axis=0)
                o = dot(v_t, pb).T.astype(BF16)
                for i in range(2):
                    j = 2 * g + i
                    o_ref[r0 + blk * HALF:r0 + (blk + 1) * HALF, j * 128:(j + 1) * 128] = o[i * HALF:(i + 1) * HALF]


def fwd_mlp_kernel(x_ref, h_ref, o_ref, g0, g1, g2, g3, u0, u1, u2, u3, z_ref, m_ref, y_ref, w_ref, wo_ref, sem):
    @pl.when(pl.program_id(0) == 0)
    def _():
        load_rows([((g0, g1, g2, g3), w_ref), ((u0, u1, u2, u3), wo_ref)], sem)

    h = h_ref[...]
    cw = 512
    acc = dot(o_ref[...], wo_ref[0:D, :])
    for c in range(FF // cw):
        gc = slice(c * cw, (c + 1) * cw)
        uc = slice(FF + c * cw, FF + (c + 1) * cw)
        g = dot(h, w_ref[:, gc]).astype(BF16)
        u = dot(h, w_ref[:, uc]).astype(BF16)
        z_ref[:, gc] = g
        z_ref[:, uc] = u
        g = g.astype(F32)
        m = (g * jax.nn.sigmoid(g) * u.astype(F32)).astype(BF16)
        m_ref[:, gc] = m
        acc = acc + dot(m, wo_ref[D + c * cw:D + (c + 1) * cw, :])
    y_ref[...] = (x_ref[...].astype(F32) + acc).astype(BF16)


def store_grad_rows(acc, width, own_ref, xp_ref, send_ref, sem, by_cols):
    move_grad_rows(acc, width, own_ref, xp_ref, send_ref, sem, by_cols, False)


def move_grad_rows(acc, width, own_ref, xp_ref, send_ref, sem, by_cols, inward):
    own = owners()
    copies = []
    for r, dst in enumerate((own_ref, send_ref.at[0], xp_ref, send_ref.at[1])):
        start = pl.multiple_of(own[r] * width, 128)
        src = acc.at[:, pl.ds(start, width)] if by_cols else acc.at[pl.ds(start, width), :]
        if inward:
            src, dst = dst, src
        cp = pltpu.make_async_copy(src, dst, sem.at[r])
        cp.start()
        copies.append(cp)
    for cp in copies:
        cp.wait()


def dwo_kernel(dy_ref, o_ref, m_ref, own_ref, xp_ref, send_ref, acc, sem):
    step = pl.program_id(0)

    @pl.when(step == 0)
    def _():
        acc[...] = jnp.zeros_like(acc)

    dy = dy_ref[...]
    acc[:, 0:D] += dot_tn(dy, o_ref[...])
    cw = 512
    for c in range(FF // cw):
        acc[:, D + c * cw:D + (c + 1) * cw] += dot_tn(dy, m_ref[:, c * cw:(c + 1) * cw])

    @pl.when(step == pl.num_programs(0) - 1)
    def _():
        store_grad_rows(acc, (D + FF) // 4, own_ref, xp_ref, send_ref, sem, True)


def bmlp_kernel(half, dy_ref, h_ref, zg_ref, zu_ref, w0, w1, w2, w3, dzg_ref, dzu_ref, own_ref, xp_ref, send_ref,
                wo_ref, acc, sem):
    step = pl.program_id(0)
    hw = FF // 2

    @pl.when(step == 0)
    def _():
        load_rows([((w0, w1, w2, w3), wo_ref)], sem)
        acc[...] = jnp.zeros_like(acc)

    dy = dy_ref[...]
    cw = 256
    h_t = h_ref[...].T
    n = hw // cw

    def dm_of(c):
        row0 = D + half * hw + c * cw
        return dot_nt(dy, wo_ref[row0:row0 + cw, :]).astype(BF16)

    for c in range(n):
        cols = slice(c * cw, (c + 1) * cw)
        dm = dm_of(c).astype(F32)
        g = zg_ref[:, cols].astype(F32)
        u = zu_ref[:, cols].astype(F32)
        sig = jax.nn.sigmoid(g)
        sl = g * sig
        dzu_ref[:, cols] = (dm * sl).astype(BF16)
        dzg_ref[:, cols] = (dm * u * (sig + sl * (1.0 - sig))).astype(BF16)
    acc[:, 0:hw] += dot(h_t, dzg_ref[...])
    acc[:, hw:2 * hw] += dot(h_t, dzu_ref[...])

    @pl.when(step == pl.num_programs(0) - 1)
    def _():
        store_grad_rows(acc, D // 4, own_ref, xp_ref, send_ref, sem, False)


def battn_kernel(chained, *refs):
    if chained:
        (dy_ref, h_ref, qkv_ref, c_ref, s_ref, w0, w1, w2, w3, _, in_own, in_xp, in_send,
         dz_ref, own_ref, xp_ref, send_ref, wo_ref, acc, sem) = refs
    else:
        (dy_ref, h_ref, qkv_ref, c_ref, s_ref, w0, w1, w2, w3,
         dz_ref, own_ref, xp_ref, send_ref, wo_ref, acc, sem) = refs
    step = pl.program_id(0)

    @pl.when(step == 0)
    def _():
        load_rows([((w0, w1, w2, w3), wo_ref)], sem)
        if chained:
            move_grad_rows(acc, D // 4, in_own, in_xp, in_send, sem, False, True)
        else:
            acc[...] = jnp.zeros_like(acc)

    do_all = dot_nt(dy_ref[...], wo_ref[0:D, :]).astype(BF16)
    lo = lane_iota((SEQ, 2 * HD)) < HD
    tri = tri_mask(128)
    trib = jnp.concatenate([tri] * 2, axis=1)
    for b in range(TOK // SEQ):
        r0 = b * SEQ
        zb = qkv_ref[r0:r0 + SEQ, :]
        do = do_all[r0:r0 + SEQ]
        k0, k1, v0, v1 = kv_tiles(zb[:, D:].astype(F32))
        kt0, kt1 = k0.T.astype(BF16), k1.T.astype(BF16)
        k0, k1, v0, v1 = [t.astype(BF16) for t in (k0, k1, v0, v1)]
        dk = [[None, None], [None, None]]
        dv = [[None, None], [None, None]]
        dq = [[None] * 4, [None] * 4]
        for blk in range(2):
            nk = (blk + 1) * HALF
            rows = slice(blk * HALF, (blk + 1) * HALF)
            k_st = jnp.concatenate([k0[:nk], k1[:nk]], axis=0)
            v_st = jnp.concatenate([v0[:nk], v1[:nk]], axis=0)
            k_t = jnp.concatenate([kt0[:, :nk], kt1[:, :nk]], axis=1)
            dk_b = dv_b = None
            for g in range(2):
                q = jnp.concatenate([zb[rows, (2 * g + i) * 128:(2 * g + i + 1) * 128] for i in range(2)], axis=0)
                dog = jnp.concatenate([do[rows, (2 * g + i) * 128:(2 * g + i + 1) * 128] for i in range(2)], axis=0)
                p = softmax_keys(dot_nt(k_st, q), nk, trib)
                dp = dot_nt(v_st, dog).astype(BF16)
                ds = []
                for i in range(2):
                    dph = [dp[i * nk + k * HALF:i * nk + (k + 1) * HALF].astype(F32) for k in range(nk // HALF)]
                    delta = sum(jnp.sum(a * c, axis=0, keepdims=True) for a, c in zip(dph, p[i]))
                    ds += [(c * (a - delta)).astype(BF16) for a, c in zip(dph, p[i])]
                ds = jnp.concatenate(ds, axis=0)
                pb = jnp.concatenate([t.astype(BF16) for ph in p for t in ph], axis=0)
                dv_g = dot(pb, dog)
                dk_g = dot(ds, q)
                dv_b = dv_g if dv_b is None else dv_b + dv_g
                dk_b = dk_g if dk_b is None else dk_b + dk_g
                dq_t = dot(k_t, ds).T
                for i in range(2):
                    dq[blk][2 * g + i] = dq_t[i * HALF:(i + 1) * HALF]
            for i in range(2):
                for k in range(nk // HALF):
                    sl = slice(i * nk + k * HALF, i * nk + (k + 1) * HALF)
                    dk[i][k] = dk_b[sl] if dk[i][k] is None else dk[i][k] + dk_b[sl]
                    dv[i][k] = dv_b[sl] if dv[i][k] is None else dv[i][k] + dv_b[sl]
        dk0, dk1, dv0, dv1 = [jnp.concatenate(t, axis=0) for t in (dk[0], dk[1], dv[0], dv[1])]
        kpart = dk0 + pltpu.roll(dk1, HD, 1)
        vpart = pltpu.roll(dv0, HD, 1) + dv1
        parts = [jnp.concatenate([dq[0][j], dq[1][j]], axis=0) for j in range(4)]
        parts.append(jnp.where(lo, kpart, vpart))
        for j in range(5):
            tc = slice(0, 128) if j < 4 else slice(128, 256)
            dr = parts[j].astype(BF16).astype(F32)
            dz_ref[r0:r0 + SEQ, j * 128:(j + 1) * 128] = (
                dr * c_ref[:, tc] - half_swap(dr) * s_ref[:, tc]).astype(BF16)
    acc[...] += dot_tn(h_ref[...], dz_ref[...])

    @pl.when(step == pl.num_programs(0) - 1)
    def _():
        store_grad_rows(acc, D // 4, own_ref, xp_ref, send_ref, sem, False)


def dx_kernel(x_ref, gain_ref, dy_ref, dzq_ref, dg0_ref, du0_ref, dg1_ref, du1_ref,
              q0, q1, q2, q3, w0, w1, w2, w3, *rest):
    dx_ref, dgain_ref, wq_ref, w_ref, sem = rest[-5:]
    step = pl.program_id(0)
    hw = FF // 2

    @pl.when(step == 0)
    def _():
        load_rows([((q0, q1, q2, q3), wq_ref), ((w0, w1, w2, w3), w_ref)], sem)
        dgain_ref[...] = jnp.zeros_like(dgain_ref)

    dh = dot_nt(dzq_ref[...], wq_ref[...])
    dh += dot_nt(dg0_ref[...], w_ref[:, 0:hw])
    dh += dot_nt(dg1_ref[...], w_ref[:, hw:2 * hw])
    dh += dot_nt(du0_ref[...], w_ref[:, 2 * hw:3 * hw])
    dh += dot_nt(du1_ref[...], w_ref[:, 3 * hw:4 * hw])
    dh = dh.astype(BF16).astype(F32)
    x = x_ref[...].astype(F32)
    cen = x - jnp.mean(x, axis=-1, keepdims=True)
    var = jnp.mean(cen * cen, axis=-1, keepdims=True)
    rstd = lax.rsqrt(var + 1e-6)
    xhat = cen * rstd
    dgain_ref[...] += jnp.sum(dh * xhat, axis=0, keepdims=True)
    dxh = dh * gain_ref[...]
    dx = rstd * (dxh - jnp.mean(dxh, axis=-1, keepdims=True)
                 - xhat * jnp.mean(dxh * xhat, axis=-1, keepdims=True))
    dx_ref[...] = (dy_ref[...].astype(F32) + dx.astype(BF16).astype(F32)).astype(BF16)


ANY = pl.BlockSpec(memory_space=pl.ANY)


def tok_spec(width, block=0, first=0):
    return pl.BlockSpec((TOK, width), lambda i: (i + first, block))


def full_spec(shape):
    return pl.BlockSpec(shape, lambda i: (0,) * len(shape))


def call(kernel, n_tok, in_specs, outs, out_specs, scratch, flops, nbytes, aliases=None):
    return pl.pallas_call(
        kernel,
        grid=(n_tok // TOK,),
        in_specs=in_specs,
        out_specs=out_specs,
        out_shape=[jax.ShapeDtypeStruct(s, t) for s, t in outs],
        scratch_shapes=scratch,
        input_output_aliases=aliases or {},
        compiler_params=pltpu.CompilerParams(
            dimension_semantics=("arbitrary",), vmem_limit_bytes=VMEM_LIMIT),
        cost_estimate=pl.CostEstimate(flops=int(flops), bytes_accessed=int(nbytes), transcendentals=0),
    )


def solution(mesh):
    batch_spec = P(("dp", "fsdp"), None, None)
    scale_spec = P(None, "fsdp")
    weight_spec = P(None, "fsdp", None)

    core_perm = [(0, 1), (1, 0), (2, 3), (3, 2)]
    x_perm = [(0, 2), (2, 0), (1, 3), (3, 1)]
    y_perm = [(0, 1), (1, 0)]

    def pp_core(a):
        return lax.ppermute(a, "fsdp", core_perm)

    def pp_x(a):
        return lax.ppermute(a, "fsdp", x_perm)

    def pp_y(a):
        return lax.ppermute(a, "dp", y_perm)

    def gather4(a):
        far = pp_x(a)
        return (a, pp_core(a), far, pp_core(far))

    def reduce4(own, xp, send):
        recv = pp_core(send)
        far = pp_x(xp + recv[1])
        mine = own + recv[0] + far
        return mine + pp_y(mine)

    def inner_step(x_in, grad_y, norm_scale, w_in, w_out):
        n_layers = w_in.shape[0]
        n_batch = x_in.shape[0]
        n_tok = n_batch * SEQ

        half = HD // 2
        inv_freq = 10000.0 ** (-(jnp.arange(half, dtype=F32) * 2.0 / HD))
        angles = jnp.arange(SEQ, dtype=F32)[:, None] * inv_freq[None, :]
        cos, sin = jnp.cos(angles), jnp.sin(angles)
        cos2 = jnp.concatenate([cos, cos], axis=1)
        sin2 = jnp.concatenate([-sin, sin], axis=1)
        qs = HD ** -0.5
        ones, zeros = jnp.ones_like(cos2), jnp.zeros_like(cos2)
        c_tab = jnp.concatenate([cos2 * qs, cos2 * qs, cos2, ones], axis=1)
        s_tab = jnp.concatenate([sin2 * qs, sin2 * qs, sin2, zeros], axis=1)

        q_pieces, g_pieces, o_pieces = [], [], []
        for l in range(n_layers):
            wq_l = w_in[l, :, :QKV]
            if l == 0:
                gcols = jnp.pad(norm_scale.T, ((0, 0), (0, 128 - n_layers)))
                wq_l = jnp.concatenate([wq_l, gcols], axis=1)
            q_pieces.append(gather4(wq_l))
            g_pieces.append(gather4(w_in[l, :, QKV:]))
            o_pieces.append(gather4(w_out[l]))
        gp = [a[:, QKV:QKV + n_layers].T for a in q_pieces[0]]
        own = owners()
        slot = jnp.arange(4)[None, :, None]
        gain = sum(jnp.where(slot == own[r], gp[r][:, None, :].astype(F32), 0.0) for r in range(4))
        gain = gain.reshape(n_layers, 1, D)

        x = x_in.reshape(n_tok, D)
        mm = 2.0 * n_tok * D
        saved = []
        sem = pltpu.SemaphoreType.DMA
        for l in range(n_layers):
            h, qkv, o = call(
                fwd_attn_kernel, n_tok,
                [tok_spec(D), full_spec((1, D)), full_spec((SEQ, 256)), full_spec((SEQ, 256))] + [ANY] * 4,
                [((n_tok, D), BF16), ((n_tok, QKV), BF16), ((n_tok, D), BF16)],
                [tok_spec(D), tok_spec(QKV), tok_spec(D)],
                [pltpu.VMEM((D, QKV), BF16), sem((4,))],
                mm * 2600, n_tok * D * 8,
            )(x, gain[l], c_tab, s_tab, *q_pieces[l])
            z, m, y = call(
                fwd_mlp_kernel, n_tok,
                [tok_spec(D), tok_spec(D), tok_spec(D)] + [ANY] * 8,
                [((n_tok, 2 * FF), BF16), ((n_tok, FF), BF16), ((n_tok, D), BF16)],
                [tok_spec(2 * FF), tok_spec(FF), tok_spec(D)],
                [pltpu.VMEM((D, 2 * FF), BF16), pltpu.VMEM((D + FF, D), BF16), sem((8,))],
                mm * 6700, n_tok * D * 32,
            )(x, h, o, *g_pieces[l], *o_pieces[l])
            saved.append((x, h, qkv, o, z, m))
            x = y

        dy = grad_y.reshape(n_tok, D)
        d_gain = [None] * n_layers
        d_win = [None] * n_layers
        d_wout = [None] * n_layers
        q4 = (D + FF) // 4

        def grad_outs(shape):
            return [(shape, F32), (shape, F32), ((2,) + shape, F32)]

        for l in reversed(range(n_layers)):
            xl, h, qkv, o, z, m = saved[l]
            g = call(
                dwo_kernel, n_tok, [tok_spec(D), tok_spec(D), tok_spec(FF)],
                grad_outs((D, q4)), [ANY] * 3,
                [pltpu.VMEM((D, D + FF), F32), sem((4,))],
                mm * 2560, n_tok * D * 12,
            )(dy, o, m)
            d_wout[l] = reduce4(*g).T
            hw = FF // 2
            dzs, win_parts = [], []
            for hf in range(2):
                dg, du, *g = call(
                    functools.partial(bmlp_kernel, hf), n_tok,
                    [tok_spec(D), tok_spec(D), tok_spec(hw, hf), tok_spec(hw, 2 + hf)] + [ANY] * 4,
                    [((n_tok, hw), BF16), ((n_tok, hw), BF16)] + grad_outs((D // 4, 2 * hw)),
                    [tok_spec(hw), tok_spec(hw)] + [ANY] * 3,
                    [pltpu.VMEM((D + FF, D), BF16), pltpu.VMEM((D, 2 * hw), F32), sem((4,))],
                    mm * 3072, n_tok * D * 20,
                )(dy, h, z, z, *o_pieces[l])
                dzs += [dg, du]
                win_parts.append(reduce4(*g))
            n_part = 2 if l == 0 else 1
            n_sub = n_tok // n_part
            dzq, g = None, ()
            for part in range(n_part):
                f0 = part * n_sub // TOK
                prev = (dzq, *g) if part else ()
                dzq, *g = call(
                    functools.partial(battn_kernel, part > 0), n_sub,
                    [tok_spec(D, 0, f0), tok_spec(D, 0, f0), tok_spec(QKV, 0, f0), full_spec((SEQ, 256)),
                     full_spec((SEQ, 256))] + [ANY] * (4 + len(prev)),
                    [((n_tok, QKV), BF16)] + grad_outs((D // 4, QKV)),
                    [tok_spec(QKV, 0, f0)] + [ANY] * 3,
                    [pltpu.VMEM((D + FF, D), BF16), pltpu.VMEM((D, QKV), F32), sem((4,))],
                    mm * 6200 / n_part, n_tok * D * 10 / n_part,
                    {9: 0} if part else None,
                )(dy, h, qkv, c_tab, s_tab, *o_pieces[l], *prev)
            wq = reduce4(*g)
            p0, p1 = win_parts
            d_win[l] = jnp.concatenate([wq, p0[:, :hw], p1[:, :hw], p0[:, hw:], p1[:, hw:]], axis=1)
            dx, gains = None, []
            for part in range(n_part):
                f0 = part * n_sub // TOK
                prev = (dx,) if part else ()
                dx, d_g = call(
                    dx_kernel, n_sub,
                    [tok_spec(D, 0, f0), full_spec((1, D)), tok_spec(D, 0, f0), tok_spec(QKV, 0, f0)]
                    + [tok_spec(hw, 0, f0)] * 4 + [ANY] * (8 + len(prev)),
                    [((n_tok, D), BF16), ((1, D), F32)],
                    [tok_spec(D, 0, f0), full_spec((1, D))],
                    [pltpu.VMEM((D, QKV), BF16), pltpu.VMEM((D, 2 * FF), BF16), sem((8,))],
                    mm * 4736 / n_part, n_tok * D * 20 / n_part,
                    {16: 0} if part else None,
                )(xl, gain[l], dy, dzq, *dzs, *q_pieces[l], *g_pieces[l], *prev)
                gains.append(d_g)
            dy = dx
            d_gain[l] = sum(gains)

        gg = jnp.concatenate(d_gain, axis=0)
        gg = gg + pp_core(gg)
        gg = gg + pp_x(gg)
        gg = gg + pp_y(gg)
        gg = lax.dynamic_slice(gg, (0, lax.axis_index("fsdp") * (D // 4)), (n_layers, D // 4))
        return (x.reshape(x_in.shape), dy.reshape(x_in.shape), gg, jnp.stack(d_win), jnp.stack(d_wout))

    return jax.shard_map(
        inner_step,
        mesh=mesh,
        in_specs=(batch_spec, batch_spec, scale_spec, weight_spec, weight_spec),
        out_specs=(batch_spec, batch_spec, scale_spec, weight_spec, weight_spec),
        check_vma=False,
    )
```

time: 1010 us -> 776 us (0.77)
  matrix products: 493 us -> 0 us
  Pallas kernels: 0 us -> 462 us
  other arithmetic: 214 us -> 20.4 us
  starting transfers between devices: 0.37 us -> 32.2 us
  blocking collectives: 25.9 us -> 0 us
  between operations: 15.8 us -> 1.57 us
    dot_general x24 -> x0, matrix products: 493 us -> none  [the longest x6 110 us: mix_block(): jnp.einsum('crie,cle->cirl', q_rot, k_rot, preferred_element_type=jnp.flo...]
    pallas_call x0 -> x16, Pallas kernels: none -> 462 us  [the longest x4 110 us: inner_step(): call(functools.partial(bmlp_kernel, hf), n_tok, [tok_spec(D), tok_spec(D)...]
    ppermute x0 -> x45, waiting for transfers between devices: none -> 234 us  [the longest x15 166 us: pp_x(): return lax.ppermute(a, 'fsdp', x_perm)]
    convert_element_type x14 -> x4, other arithmetic: 133 us -> 2.3 us  [inner_step(): gp[r][:, None, :].astype(F32)]
    reduce_scatter x4 -> x0, waiting for transfers between devices: 110 us -> none  [reduce_grad(): lax.psum_scatter(part_sum, 'fsdp', scatter_dimension=0, tiled=True)]
    psum x1 -> x0, waiting for transfers between devices: 106 us -> none  [reduce_grad(): return lax.psum(shard_sum, 'dp')]
    reduce_sum x7 -> x0, other arithmetic: 47.6 us -> none  [the longest x2 28.2 us: mix_block(): attn_probs = jax.nn.softmax(scores, axis=-1).astype(jnp.bfloat16)]
    ppermute x0 -> x45, starting transfers between devices: none -> 32.2 us  [the longest x15 16.5 us: pp_x(): return lax.ppermute(a, 'fsdp', x_perm)]
  transfers between devices with their start and end apart: 9 -> 45, of which waited for: 4 -> 15; matrix products, arithmetic and copies ran while one was open for 37% -> 4% of each run, Pallas kernels for 0% -> 60%
where the time goes in v1:
time: 776 us; the launch traced here: 766 us
  Pallas kernels  462 us (60%)
  waiting for transfers between devices  234 us (30%)
  starting transfers between devices  32.2 us (4%)
  other arithmetic  20.4 us (3%)
  local copies, waits for them, and re-layouts  16.1 us (2%)
    ppermute x15, waiting for transfers between devices, pp_x(): return lax.ppermute(a, 'fsdp', x_perm)  166 us
    pallas_call x4, Pallas kernels, inner_step(): call(functools.partial(bmlp_kernel, hf), n_tok, [tok_spec(D), tok_spec(D)...  110 us
    pallas_call x3, Pallas kernels, inner_step(): call(functools.partial(battn_kernel, part > 0), n_sub, [tok_spec(D, 0, f0...  96.1 us
    pallas_call x2, Pallas kernels, inner_step(): call(fwd_mlp_kernel, n_tok, [tok_spec(D), tok_spec(D), tok_spec(D)] + [AN...  76.9 us
    pallas_call x3, Pallas kernels, inner_step(): call(dx_kernel, n_sub, [tok_spec(D, 0, f0), full_spec((1, D)), tok_spec(D...  74.1 us
    pallas_call x2, Pallas kernels, inner_step(): call(fwd_attn_kernel, n_tok, [tok_spec(D), full_spec((1, D)), full_spec((...  67.7 us
    ppermute x9, waiting for transfers between devices, pp_y(): return lax.ppermute(a, 'dp', y_perm)  63.6 us
    pallas_call x2, Pallas kernels, inner_step(): call(dwo_kernel, n_tok, [tok_spec(D), tok_spec(D), tok_spec(FF)], grad_ou...  37.1 us
  transfers between devices with their start and end apart: 45, of which 15 were waited for; matrix products, arithmetic and copies ran while one was open for 4% of the time, Pallas kernels for 60%

profile of v1, /device:TPU:0, one launch (start us, length us, event | category | flops | bytes accessed | tf_op | source)
XLA Modules:
  0.0 766.4 jit_solution(820974949510214640)
XLA Ops:
  3.9 3.3 collective-permute-start.1
  16.4 2.0 concatenate.30.s_ref.refs_4_
  25.4 24.1 %collective-permute-done.4.g2.w2 = bf16[128,4096]{1,0:T(8,128)(2,1)S(1)} collective-permute-done((bf16[128,4096]{1,0:T(8,128)(2,1)S(1)}, bf16[128,4096]{1,0:T(8,128)(2,1)S(1)}, u32[]{:S(2)}, u32[]{:S(2)}) %collective-permute-start.4) | collective-permute-done | bytes 1048608 | tf_op jit(solution)/shard_map/ppermute | solution.py:384
  50.6 33.8 %shard_map.92 = (bf16[4096,512]{1,0:T(8,128)(2,1)}, bf16[4096,640]{1,0:T(8,128)(2,1)}, bf16[4096,512]{1,0:T(8,128)(2,1)}) custom-call(bf16[4096,512]{1,0:T(8,128)(2,1)} %bitcast.120, f32[1,512]{1,0:T(1,128)} %bitcast.128, f32[256,256]{1,0:T(8,128)} %concatenate.28.c_ref.refs_3_, f32[256,256]{1,0:T(8,128)} %concatenate.30.s_ref.refs_4_, ...), custom_call_target="tpu_custom_call" | custom-call | flops 10905190400 | bytes 16777216 | tf_op jit(solution)/shard_map/pallas_call | solution.py:435
  84.5 2.3 collective-permute-start.16
  87.4 38.5 %shard_map.93 = (bf16[4096,4096]{1,0:T(8,128)(2,1)}, bf16[4096,2048]{1,0:T(8,128)(2,1)}, bf16[4096,512]{1,0:T(8,128)(2,1)}) custom-call(bf16[4096,512]{1,0:T(8,128)(2,1)} %bitcast.121, bf16[4096,512]{1,0:T(8,128)(2,1)} %get-tuple-element.61.h_ref.refs_1_, bf16[4096,512]{1,0:T(8,128)(2,1)} %get-tuple-element.62.o_ref, bf16[128,4096]{1,0:T(8,128)(2,1)} %copy-done, ...), custom_call_target="tpu_custom_call" | custom-call | flops 28101836800 | bytes 67108864 | tf_op jit(solution)/shard_map/pallas_call | solution.py:443
  127.6 33.9 %shard_map.94 = (bf16[4096,512]{1,0:T(8,128)(2,1)}, bf16[4096,640]{1,0:T(8,128)(2,1)}, bf16[4096,512]{1,0:T(8,128)(2,1)}) custom-call(bf16[4096,512]{1,0:T(8,128)(2,1)} %get-tuple-element.63.x_ref, f32[1,512]{1,0:T(1,128)} %bitcast.131, f32[256,256]{1,0:T(8,128)} %concatenate.28.c_ref.refs_3_, f32[256,256]{1,0:T(8,128)} %concatenate.30.s_ref.refs_4_, ...), custom_call_target="tpu_custom_call" | custom-call | flops 10905190400 | bytes 16777216 | tf_op jit(solution)/shard_map/pallas_call | solution.py:435
  162.5 44.5 %shard_map.96 = (bf16[4096,640]{1,0:T(8,128)(2,1)}, f32[128,640]{1,0:T(8,128)}, f32[128,640]{1,0:T(8,128)}, f32[2,128,640]{2,1,0:T(8,128)}) custom-call(bf16[4096,512]{1,0:T(8,128)(2,1)} %bitcast.115, bf16[4096,512]{1,0:T(8,128)(2,1)} %get-tuple-element.64.h_ref.refs_1_, bf16[4096,640]{1,0:T(8,128)(2,1)} %get-tuple-element.67.refs_2_, ...), custom_call_target="tpu_custom_call" | custom-call | flops 26004684800 | bytes 20971520 | tf_op jit(solution)/shard_map/pallas_call | solution.py:491
  207.1 38.4 %shard_map.95 = (bf16[4096,4096]{1,0:T(8,128)(2,1)}, bf16[4096,2048]{1,0:T(8,128)(2,1)}, bf16[4096,512]{1,0:T(8,128)(2,1)}) custom-call(bf16[4096,512]{1,0:T(8,128)(2,1)} %get-tuple-element.63.x_ref, bf16[4096,512]{1,0:T(8,128)(2,1)} %get-tuple-element.64.h_ref.refs_1_, bf16[4096,512]{1,0:T(8,128)(2,1)} %get-tuple-element.65.o_ref, ...), custom_call_target="tpu_custom_call" | custom-call | flops 28101836800 | bytes 67108864 | tf_op jit(solution)/shard_map/pallas_call | solution.py:443
  245.5 27.5 %shard_map.98 = (bf16[4096,1024]{1,0:T(8,128)(2,1)}, bf16[4096,1024]{1,0:T(8,128)(2,1)}, f32[128,2048]{1,0:T(8,128)}, f32[128,2048]{1,0:T(8,128)}, f32[2,128,2048]{2,1,0:T(8,128)}) custom-call(bf16[4096,512]{1,0:T(8,128)(2,1)} %bitcast.116, bf16[4096,512]{1,0:T(8,128)(2,1)} %get-tuple-element.64.h_ref.refs_1_, ...), custom_call_target="tpu_custom_call" | custom-call | flops 12884901888 | bytes 41943040 | tf_op jit(solution)/shard_map/pallas_call | solution.py:475
  273.0 27.6 %shard_map.97 = (bf16[4096,1024]{1,0:T(8,128)(2,1)}, bf16[4096,1024]{1,0:T(8,128)(2,1)}, f32[128,2048]{1,0:T(8,128)}, f32[128,2048]{1,0:T(8,128)}, f32[2,128,2048]{2,1,0:T(8,128)}) custom-call(bf16[4096,512]{1,0:T(8,128)(2,1)} %bitcast.117, bf16[4096,512]{1,0:T(8,128)(2,1)} %get-tuple-element.64.h_ref.refs_1_, ...), custom_call_target="tpu_custom_call" | custom-call | flops 12884901888 | bytes 41943040 | tf_op jit(solution)/shard_map/pallas_call | solution.py:475
  300.7 33.5 %shard_map.99 = (bf16[4096,512]{1,0:T(8,128)(2,1)}, f32[1,512]{1,0:T(1,128)}) custom-call(bf16[4096,512]{1,0:T(8,128)(2,1)} %get-tuple-element.63.x_ref, f32[1,512]{1,0:T(1,128)} %bitcast.132, bf16[4096,512]{1,0:T(8,128)(2,1)} %bitcast.118, bf16[4096,640]{1,0:T(8,128)(2,1)} %get-tuple-element.68.dzq_ref, bf16[4096,1024]{1,0:T(8,128)(2,1)} %get-tuple-element.70.dg0_ref, ...), custom_call_target="tpu_custom_call" | custom-call | flops 19864223744 | bytes 41943040 | tf_op jit(solution)/shard_map/pallas_call | solution.py:508
  334.2 25.0 %shard_map.100 = (bf16[4096,640]{1,0:T(8,128)(2,1)}, f32[128,640]{1,0:T(8,128)}, f32[128,640]{1,0:T(8,128)}, f32[2,128,640]{2,1,0:T(8,128)}) custom-call(bf16[4096,512]{1,0:T(8,128)(2,1)} %get-tuple-element.74.refs_0_.dy_ref, bf16[4096,512]{1,0:T(8,128)(2,1)} %get-tuple-element.61.h_ref.refs_1_, bf16[4096,640]{1,0:T(8,128)(2,1)} %get-tuple-element.75.refs_2_, ...), custom_call_target="tpu_custom_call" | custom-call | flops 13002342400 | bytes 10485760 | tf_op jit(solution)/shard_map/pallas_call | solution.py:491
  359.1 26.7 %shard_map.101 = (bf16[4096,640]{1,0:T(8,128)(2,1)}, f32[128,640]{1,0:T(8,128)}, f32[128,640]{1,0:T(8,128)}, f32[2,128,640]{2,1,0:T(8,128)}) custom-call(bf16[4096,512]{1,0:T(8,128)(2,1)} %get-tuple-element.74.refs_0_.dy_ref, bf16[4096,512]{1,0:T(8,128)(2,1)} %get-tuple-element.61.h_ref.refs_1_, ...), custom_call_target="tpu_custom_call", output_to_operand_aliasing={{0}: (9, {})} | custom-call | flops 13002342400 | bytes 10485760 | tf_op jit(solution)/shard_map/pallas_call | solution.py:491
  386.3 27.4 %shard_map.103 = (bf16[4096,1024]{1,0:T(8,128)(2,1)}, bf16[4096,1024]{1,0:T(8,128)(2,1)}, f32[128,2048]{1,0:T(8,128)}, f32[128,2048]{1,0:T(8,128)}, f32[2,128,2048]{2,1,0:T(8,128)}) custom-call(bf16[4096,512]{1,0:T(8,128)(2,1)} %get-tuple-element.74.refs_0_.dy_ref, bf16[4096,512]{1,0:T(8,128)(2,1)} %get-tuple-element.61.h_ref.refs_1_, ...), custom_call_target="tpu_custom_call" | custom-call | flops 12884901888 | bytes 41943040 | tf_op jit(solution)/shard_map/pallas_call | solution.py:475
  413.8 27.5 %shard_map.102 = (bf16[4096,1024]{1,0:T(8,128)(2,1)}, bf16[4096,1024]{1,0:T(8,128)(2,1)}, f32[128,2048]{1,0:T(8,128)}, f32[128,2048]{1,0:T(8,128)}, f32[2,128,2048]{2,1,0:T(8,128)}) custom-call(bf16[4096,512]{1,0:T(8,128)(2,1)} %get-tuple-element.74.refs_0_.dy_ref, bf16[4096,512]{1,0:T(8,128)(2,1)} %get-tuple-element.61.h_ref.refs_1_, ...), custom_call_target="tpu_custom_call" | custom-call | flops 12884901888 | bytes 41943040 | tf_op jit(solution)/shard_map/pallas_call | solution.py:475
  441.3 20.4 %shard_map.104 = (bf16[4096,512]{1,0:T(8,128)(2,1)}, f32[1,512]{1,0:T(1,128)}) custom-call(bf16[4096,512]{1,0:T(8,128)(2,1)} %bitcast.122, f32[1,512]{1,0:T(1,128)} %bitcast.129, bf16[4096,512]{1,0:T(8,128)(2,1)} %get-tuple-element.74.refs_0_.dy_ref, bf16[4096,640]{1,0:T(8,128)(2,1)} %get-tuple-element.80.dzq_ref, ...), custom_call_target="tpu_custom_call" | custom-call | flops 9932111872 | bytes 20971520 | tf_op jit(solution)/shard_map/pallas_call | solution.py:508
  461.7 20.2 %shard_map.105 = (bf16[4096,512]{1,0:T(8,128)(2,1)}, f32[1,512]{1,0:T(1,128)}) custom-call(bf16[4096,512]{1,0:T(8,128)(2,1)} %bitcast.123, f32[1,512]{1,0:T(1,128)} %bitcast.130, bf16[4096,512]{1,0:T(8,128)(2,1)} %get-tuple-element.74.refs_0_.dy_ref, bf16[4096,640]{1,0:T(8,128)(2,1)} %get-tuple-element.80.dzq_ref, ...), custom_call_target="tpu_custom_call", output_to_operand_aliasing={{0}: (16, {})} | custom-call | flops 9932111872 | bytes 20971520 | tf_op jit(solution)/shard_map/pallas_call | solution.py:508
  482.8 18.5 %shard_map.107 = (f32[512,640]{1,0:T(8,128)}, f32[512,640]{1,0:T(8,128)}, f32[2,512,640]{2,1,0:T(8,128)}) custom-call(bf16[4096,512]{1,0:T(8,128)(2,1)} %bitcast.119, bf16[4096,512]{1,0:T(8,128)(2,1)} %get-tuple-element.65.o_ref, bf16[4096,2048]{1,0:T(8,128)(2,1)} %get-tuple-element.113.m_ref), custom_call_target="tpu_custom_call" | custom-call | flops 10737418240 | bytes 25165824 | tf_op jit(solution)/shard_map/pallas_call | solution.py:465
  507.7 8.0 %collective-permute-done.31 = f32[128,640]{1,0:T(8,128)S(1)} collective-permute-done((f32[128,640]{1,0:T(8,128)S(1)}, f32[128,640]{1,0:T(8,128)S(1)}, u32[]{:S(2)}, u32[]{:S(2)}) %collective-permute-start.31) | collective-permute-done | bytes 327712 | tf_op jit(solution)/shard_map/ppermute | solution.py:384
  518.3 3.3 collective-permute-done.22
  523.7 18.6 %shard_map.106 = (f32[512,640]{1,0:T(8,128)}, f32[512,640]{1,0:T(8,128)}, f32[2,512,640]{2,1,0:T(8,128)}) custom-call(bf16[4096,512]{1,0:T(8,128)(2,1)} %get-tuple-element.74.refs_0_.dy_ref, bf16[4096,512]{1,0:T(8,128)(2,1)} %get-tuple-element.62.o_ref, bf16[4096,2048]{1,0:T(8,128)(2,1)} %get-tuple-element.109.m_ref), custom_call_target="tpu_custom_call" | custom-call | flops 10737418240 | bytes 25165824 | tf_op jit(solution)/shard_map/pallas_call | solution.py:465
  554.7 16.4 %collective-permute-done.37 = f32[128,2048]{1,0:T(8,128)S(1)} collective-permute-done((f32[128,2048]{1,0:T(8,128)S(1)}, f32[128,2048]{1,0:T(8,128)S(1)}, u32[]{:S(2)}, u32[]{:S(2)}) %collective-permute-start.37) | collective-permute-done | bytes 1048608 | tf_op jit(solution)/shard_map/ppermute | solution.py:384
  572.9 20.7 %collective-permute-done.34 = f32[128,2048]{1,0:T(8,128)S(1)} collective-permute-done((f32[128,2048]{1,0:T(8,128)S(1)}, f32[128,2048]{1,0:T(8,128)S(1)}, u32[]{:S(2)}, u32[]{:S(2)}) %collective-permute-start.34) | collective-permute-done | bytes 1048608 | tf_op jit(solution)/shard_map/ppermute | solution.py:384
  596.6 42.0 %collective-permute-done.25 = f32[128,2048]{1,0:T(8,128)S(1)} collective-permute-done((f32[128,2048]{1,0:T(8,128)S(1)}, f32[128,2048]{1,0:T(8,128)S(1)}, u32[]{:S(2)}, u32[]{:S(2)}) %collective-permute-start.25) | collective-permute-done | bytes 1048608 | tf_op jit(solution)/shard_map/ppermute | solution.py:384
  641.0 25.6 %collective-permute-done.43 = f32[512,640]{1,0:T(8,128)S(1)} collective-permute-done((f32[512,640]{1,0:T(8,128)S(1)}, f32[512,640]{1,0:T(8,128)S(1)}, u32[]{:S(2)}, u32[]{:S(2)}) %collective-permute-start.43) | collective-permute-done | bytes 1310752 | tf_op jit(solution)/shard_map/ppermute | solution.py:384
  668.4 25.8 %collective-permute-done.40 = f32[512,640]{1,0:T(8,128)S(1)} collective-permute-done((f32[512,640]{1,0:T(8,128)S(1)}, f32[512,640]{1,0:T(8,128)S(1)}, u32[]{:S(2)}, u32[]{:S(2)}) %collective-permute-start.40) | collective-permute-done | bytes 1310752 | tf_op jit(solution)/shard_map/ppermute | solution.py:384
  697.2 12.3 %collective-permute-done.29 = f32[128,2048]{1,0:T(8,128)S(1)} collective-permute-done((f32[128,2048]{1,0:T(8,128)S(1)}, f32[128,2048]{1,0:T(8,128)S(1)}, u32[]{:S(2)}, u32[]{:S(2)}) %collective-permute-start.29) | collective-permute-done | bytes 1048608 | tf_op jit(solution)/shard_map/ppermute | solution.py:387
  709.8 2.5 pad_maximum_fusion
  712.3 25.3 %collective-permute-done.44 = f32[512,640]{1,0:T(8,128)S(1)} collective-permute-done((f32[512,640]{1,0:T(8,128)S(1)}, f32[512,640]{1,0:T(8,128)S(1)}, u32[]{:S(2)}, u32[]{:S(2)}) %collective-permute-start.44) | collective-permute-done | bytes 1310752 | tf_op jit(solution)/shard_map/ppermute | solution.py:387
  737.7 26.0 %collective-permute-done.41 = f32[512,640]{1,0:T(8,128)S(1)} collective-permute-done((f32[512,640]{1,0:T(8,128)S(1)}, f32[512,640]{1,0:T(8,128)S(1)}, u32[]{:S(2)}, u32[]{:S(2)}) %collective-permute-start.41) | collective-permute-done | bytes 1310752 | tf_op jit(solution)/shard_map/ppermute | solution.py:387
  764.1 2.1 copy.16
  (197 shorter events, 61.0 us)
Async XLA Ops:
  8.7 41.4 %collective-permute-start.7 = (bf16[640,512]{1,0:T(8,128)(2,1)S(1)}, bf16[640,512]{1,0:T(8,128)(2,1)}, u32[]{:S(2)}, u32[]{:S(2)}) collective-permute-start(bf16[640,512]{1,0:T(8,128)(2,1)S(1)} %get-tuple-element.127.u0.refs_5_.w0), channel_id=1, source_target_pairs={{0,2},{2,0},{1,3},{3,1},{4,6},{6,4},{5,7},{7,5}} | collective-permute-start | bytes 1966088 | tf_op jit(solution)/shard_map/ppermute | solution.py:384
  8.7 75.8 %collective-permute-start.6 = (bf16[640,512]{1,0:T(8,128)(2,1)S(1)}, bf16[640,512]{1,0:T(8,128)(2,1)}, u32[]{:S(2)}, u32[]{:S(2)}) collective-permute-start(bf16[640,512]{1,0:T(8,128)(2,1)S(1)} %get-tuple-element.127.u0.refs_5_.w0), channel_id=1, source_target_pairs={{0,1},{1,0},{2,3},{3,2},{4,5},{5,4},{6,7},{7,6}} | collective-permute-start | bytes 1966088 | tf_op jit(solution)/shard_map/ppermute | solution.py:381
  10.4 39.0 %collective-permute-start.4 = (bf16[128,4096]{1,0:T(8,128)(2,1)S(1)}, bf16[128,4096]{1,0:T(8,128)(2,1)S(1)}, u32[]{:S(2)}, u32[]{:S(2)}) collective-permute-start(bf16[128,4096]{1,0:T(8,128)(2,1)S(1)} %get-tuple-element.123.g0.w0), channel_id=1, source_target_pairs={{0,2},{2,0},{1,3},{3,1},{4,6},{6,4},{5,7},{7,5}} | collective-permute-start | bytes 3145736 | tf_op jit(solution)/shard_map/ppermute | solution.py:384
  21.1 65.8 %collective-permute-start.3 = (bf16[128,4096]{1,0:T(8,128)(2,1)S(1)}, bf16[128,4096]{1,0:T(8,128)(2,1)}, u32[]{:S(2)}, u32[]{:S(2)}) collective-permute-start(bf16[128,4096]{1,0:T(8,128)(2,1)S(1)} %get-tuple-element.123.g0.w0), channel_id=1, source_target_pairs={{0,1},{1,0},{2,3},{3,2},{4,5},{5,4},{6,7},{7,6}} | collective-permute-start | bytes 3145736 | tf_op jit(solution)/shard_map/ppermute | solution.py:381
  24.2 60.3 %collective-permute-start.10 = (bf16[128,640]{1,0:T(8,128)(2,1)}, bf16[128,640]{1,0:T(8,128)(2,1)}, u32[]{:S(2)}, u32[]{:S(2)}) collective-permute-start(bf16[128,640]{1,0:T(8,128)(2,1)} %get-tuple-element.124.w0.q0), channel_id=1, source_target_pairs={{0,2},{2,0},{1,3},{3,1},{4,6},{6,4},{5,7},{7,5}} | collective-permute-start | bytes 491528 | tf_op jit(solution)/shard_map/ppermute | solution.py:384
  49.5 37.9 %collective-permute-start.5 = (bf16[128,4096]{1,0:T(8,128)(2,1)S(1)}, bf16[128,4096]{1,0:T(8,128)(2,1)}, u32[]{:S(2)}, u32[]{:S(2)}) collective-permute-start(bf16[128,4096]{1,0:T(8,128)(2,1)S(1)} %collective-permute-done.4.g2.w2), channel_id=1, source_target_pairs={{0,1},{1,0},{2,3},{3,2},{4,5},{5,4},{6,7},{7,6}} | collective-permute-start | bytes 3145736 | tf_op jit(solution)/shard_map/ppermute | solution.py:381
  50.1 36.9 %collective-permute-start.8 = (bf16[640,512]{1,0:T(8,128)(2,1)}, bf16[640,512]{1,0:T(8,128)(2,1)}, u32[]{:S(2)}, u32[]{:S(2)}) collective-permute-start(bf16[640,512]{1,0:T(8,128)(2,1)} %collective-permute-done.7.u2.refs_7_.w2), channel_id=1, source_target_pairs={{0,1},{1,0},{2,3},{3,2},{4,5},{5,4},{6,7},{7,6}} | collective-permute-start | bytes 1966088 | tf_op jit(solution)/shard_map/ppermute | solution.py:381
  84.5 41.4 %collective-permute-start.9 = (bf16[128,640]{1,0:T(8,128)(2,1)}, bf16[128,640]{1,0:T(8,128)(2,1)}, u32[]{:S(2)}, u32[]{:S(2)}) collective-permute-start(bf16[128,640]{1,0:T(8,128)(2,1)} %get-tuple-element.124.w0.q0), channel_id=1, source_target_pairs={{0,1},{1,0},{2,3},{3,2},{4,5},{5,4},{6,7},{7,6}} | collective-permute-start | bytes 491528 | tf_op jit(solution)/shard_map/ppermute | solution.py:381
  84.5 41.9 %collective-permute-start.16 = (bf16[640,512]{1,0:T(8,128)(2,1)S(1)}, bf16[640,512]{1,0:T(8,128)(2,1)S(1)}, u32[]{:S(2)}, u32[]{:S(2)}) collective-permute-start(bf16[640,512]{1,0:T(8,128)(2,1)S(1)} %get-tuple-element.126.u0.refs_5_.w0), channel_id=1, source_target_pairs={{0,2},{2,0},{1,3},{3,1},{4,6},{6,4},{5,7},{7,5}} | collective-permute-start | bytes 1966088 | tf_op jit(solution)/shard_map/ppermute | solution.py:384
  86.8 74.6 %collective-permute-start.15 = (bf16[640,512]{1,0:T(8,128)(2,1)S(1)}, bf16[640,512]{1,0:T(8,128)(2,1)S(1)}, u32[]{:S(2)}, u32[]{:S(2)}) collective-permute-start(bf16[640,512]{1,0:T(8,128)(2,1)S(1)} %get-tuple-element.126.u0.refs_5_.w0), channel_id=1, source_target_pairs={{0,1},{1,0},{2,3},{3,2},{4,5},{5,4},{6,7},{7,6}} | collective-permute-start | bytes 1966088 | tf_op jit(solution)/shard_map/ppermute | solution.py:381
  87.0 39.4 %collective-permute-start.13 = (bf16[128,4096]{1,0:T(8,128)(2,1)}, bf16[128,4096]{1,0:T(8,128)(2,1)}, u32[]{:S(2)}, u32[]{:S(2)}) collective-permute-start(bf16[128,4096]{1,0:T(8,128)(2,1)} %get-tuple-element.122.g0.w0), channel_id=1, source_target_pairs={{0,2},{2,0},{1,3},{3,1},{4,6},{6,4},{5,7},{7,5}} | collective-permute-start | bytes 3145736 | tf_op jit(solution)/shard_map/ppermute | solution.py:384
  87.3 39.6 %collective-permute-start.11 = (bf16[128,640]{1,0:T(8,128)(2,1)}, bf16[128,640]{1,0:T(8,128)(2,1)S(1)}, u32[]{:S(2)}, u32[]{:S(2)}) collective-permute-start(bf16[128,640]{1,0:T(8,128)(2,1)} %collective-permute-done.10.w2.q2), channel_id=1, source_target_pairs={{0,1},{1,0},{2,3},{3,2},{4,5},{5,4},{6,7},{7,6}} | collective-permute-start | bytes 491528 | tf_op jit(solution)/shard_map/ppermute | solution.py:381
  125.9 81.2 %collective-permute-start.12 = (bf16[128,4096]{1,0:T(8,128)(2,1)S(1)}, bf16[128,4096]{1,0:T(8,128)(2,1)}, u32[]{:S(2)}, u32[]{:S(2)}) collective-permute-start(bf16[128,4096]{1,0:T(8,128)(2,1)S(1)} %copy-done.19), channel_id=1, source_target_pairs={{0,1},{1,0},{2,3},{3,2},{4,5},{5,4},{6,7},{7,6}} | collective-permute-start | bytes 3145736 | tf_op jit(solution)/shard_map/ppermute | solution.py:381
  126.4 35.1 %collective-permute-start.17 = (bf16[640,512]{1,0:T(8,128)(2,1)S(1)}, bf16[640,512]{1,0:T(8,128)(2,1)S(1)}, u32[]{:S(2)}, u32[]{:S(2)}) collective-permute-start(bf16[640,512]{1,0:T(8,128)(2,1)S(1)} %collective-permute-done.16.u2.refs_7_.w2), channel_id=1, source_target_pairs={{0,1},{1,0},{2,3},{3,2},{4,5},{5,4},{6,7},{7,6}} | collective-permute-start | bytes 1966088 | tf_op jit(solution)/shard_map/ppermute | solution.py:381
  126.4 80.7 %collective-permute-start.14 = (bf16[128,4096]{1,0:T(8,128)(2,1)}, bf16[128,4096]{1,0:T(8,128)(2,1)}, u32[]{:S(2)}, u32[]{:S(2)}) collective-permute-start(bf16[128,4096]{1,0:T(8,128)(2,1)} %collective-permute-done.13.g2.w2), channel_id=1, source_target_pairs={{0,1},{1,0},{2,3},{3,2},{4,5},{5,4},{6,7},{7,6}} | collective-permute-start | bytes 3145736 | tf_op jit(solution)/shard_map/ppermute | solution.py:381
  207.0 295.3 %collective-permute-start.30 = (f32[2,128,640]{2,1,0:T(8,128)}, f32[2,128,640]{2,1,0:T(8,128)}, u32[]{:S(2)}, u32[]{:S(2)}) collective-permute-start(f32[2,128,640]{2,1,0:T(8,128)} %get-tuple-element.101), channel_id=1, source_target_pairs={{0,1},{1,0},{2,3},{3,2},{4,5},{5,4},{6,7},{7,6}} | collective-permute-start | bytes 1966088 | tf_op jit(solution)/shard_map/ppermute | solution.py:381
  385.8 119.3 %collective-permute-start.21 = (f32[2,128,640]{2,1,0:T(8,128)}, f32[2,128,640]{2,1,0:T(8,128)S(1)}, u32[]{:S(2)}, u32[]{:S(2)}) collective-permute-start(f32[2,128,640]{2,1,0:T(8,128)} %get-tuple-element.92), channel_id=1, source_target_pairs={{0,1},{1,0},{2,3},{3,2},{4,5},{5,4},{6,7},{7,6}} | collective-permute-start | bytes 1966088 | tf_op jit(solution)/shard_map/ppermute | solution.py:381
  501.3 42.1 %collective-permute-start.36 = (f32[2,128,2048]{2,1,0:T(8,128)}, f32[2,128,2048]{2,1,0:T(8,128)}, u32[]{:S(2)}, u32[]{:S(2)}) collective-permute-start(f32[2,128,2048]{2,1,0:T(8,128)} %get-tuple-element.107), channel_id=1, source_target_pairs={{0,1},{1,0},{2,3},{3,2},{4,5},{5,4},{6,7},{7,6}} | collective-permute-start | bytes 6291464 | tf_op jit(solution)/shard_map/ppermute | solution.py:381
  501.8 43.2 %collective-permute-start.33 = (f32[2,128,2048]{2,1,0:T(8,128)}, f32[2,128,2048]{2,1,0:T(8,128)}, u32[]{:S(2)}, u32[]{:S(2)}) collective-permute-start(f32[2,128,2048]{2,1,0:T(8,128)} %get-tuple-element.104), channel_id=1, source_target_pairs={{0,1},{1,0},{2,3},{3,2},{4,5},{5,4},{6,7},{7,6}} | collective-permute-start | bytes 6291464 | tf_op jit(solution)/shard_map/ppermute | solution.py:381
  501.9 45.0 %collective-permute-start.27 = (f32[2,128,2048]{2,1,0:T(8,128)}, f32[2,128,2048]{2,1,0:T(8,128)S(1)}, u32[]{:S(2)}, u32[]{:S(2)}) collective-permute-start(f32[2,128,2048]{2,1,0:T(8,128)} %get-tuple-element.98), channel_id=1, source_target_pairs={{0,1},{1,0},{2,3},{3,2},{4,5},{5,4},{6,7},{7,6}} | collective-permute-start | bytes 6291464 | tf_op jit(solution)/shard_map/ppermute | solution.py:381
  545.1 26.1 %collective-permute-start.37 = (f32[128,2048]{1,0:T(8,128)S(1)}, f32[128,2048]{1,0:T(8,128)S(1)}, u32[]{:S(2)}, u32[]{:S(2)}) collective-permute-start(f32[128,2048]{1,0:T(8,128)S(1)} %fusion.6), channel_id=1, source_target_pairs={{0,2},{2,0},{1,3},{3,1},{4,6},{6,4},{5,7},{7,5}} | collective-permute-start | bytes 3145736 | tf_op jit(solution)/shard_map/ppermute | solution.py:384
  546.8 46.8 %collective-permute-start.34 = (f32[128,2048]{1,0:T(8,128)S(1)}, f32[128,2048]{1,0:T(8,128)S(1)}, u32[]{:S(2)}, u32[]{:S(2)}) collective-permute-start(f32[128,2048]{1,0:T(8,128)S(1)} %fusion.9), channel_id=1, source_target_pairs={{0,2},{2,0},{1,3},{3,1},{4,6},{6,4},{5,7},{7,5}} | collective-permute-start | bytes 3145736 | tf_op jit(solution)/shard_map/ppermute | solution.py:384
  550.5 89.8 %collective-permute-start.28 = (f32[128,2048]{1,0:T(8,128)S(1)}, f32[128,2048]{1,0:T(8,128)S(1)}, u32[]{:S(2)}, u32[]{:S(2)}) collective-permute-start(f32[128,2048]{1,0:T(8,128)S(1)} %fusion.12), channel_id=1, source_target_pairs={{0,2},{2,0},{1,3},{3,1},{4,6},{6,4},{5,7},{7,5}} | collective-permute-start | bytes 3145736 | tf_op jit(solution)/shard_map/ppermute | solution.py:384
  550.9 87.6 %collective-permute-start.25 = (f32[128,2048]{1,0:T(8,128)S(1)}, f32[128,2048]{1,0:T(8,128)S(1)}, u32[]{:S(2)}, u32[]{:S(2)}) collective-permute-start(f32[128,2048]{1,0:T(8,128)S(1)} %fusion.15), channel_id=1, source_target_pairs={{0,2},{2,0},{1,3},{3,1},{4,6},{6,4},{5,7},{7,5}} | collective-permute-start | bytes 3145736 | tf_op jit(solution)/shard_map/ppermute | solution.py:384
  554.2 112.4 %collective-permute-start.43 = (f32[512,640]{1,0:T(8,128)S(1)}, f32[512,640]{1,0:T(8,128)S(1)}, u32[]{:S(2)}, u32[]{:S(2)}) collective-permute-start(f32[512,640]{1,0:T(8,128)S(1)} %fusion), channel_id=1, source_target_pairs={{0,2},{2,0},{1,3},{3,1},{4,6},{6,4},{5,7},{7,5}} | collective-permute-start | bytes 3932168 | tf_op jit(solution)/shard_map/ppermute | solution.py:384
  571.1 123.1 %collective-permute-start.40 = (f32[512,640]{1,0:T(8,128)S(1)}, f32[512,640]{1,0:T(8,128)S(1)}, u32[]{:S(2)}, u32[]{:S(2)}) collective-permute-start(f32[512,640]{1,0:T(8,128)S(1)} %fusion.3), channel_id=1, source_target_pairs={{0,2},{2,0},{1,3},{3,1},{4,6},{6,4},{5,7},{7,5}} | collective-permute-start | bytes 3932168 | tf_op jit(solution)/shard_map/ppermute | solution.py:384
  593.6 103.1 %collective-permute-start.38 = (f32[128,2048]{1,0:T(8,128)S(1)}, f32[128,2048]{1,0:T(8,128)S(1)}, u32[]{:S(2)}, u32[]{:S(2)}) collective-permute-start(f32[128,2048]{1,0:T(8,128)S(1)} %fusion.8), channel_id=1, source_target_pairs={{0,4},{4,0},{1,5},{5,1},{2,6},{6,2},{3,7},{7,3}} | collective-permute-start | bytes 3145736 | tf_op jit(solution)/shard_map/ppermute | solution.py:387
  638.5 57.4 %collective-permute-start.35 = (f32[128,2048]{1,0:T(8,128)S(1)}, f32[128,2048]{1,0:T(8,128)S(1)}, u32[]{:S(2)}, u32[]{:S(2)}) collective-permute-start(f32[128,2048]{1,0:T(8,128)S(1)} %fusion.11), channel_id=1, source_target_pairs={{0,4},{4,0},{1,5},{5,1},{2,6},{6,2},{3,7},{7,3}} | collective-permute-start | bytes 3145736 | tf_op jit(solution)/shard_map/ppermute | solution.py:387
  640.3 56.6 %collective-permute-start.26 = (f32[128,2048]{1,0:T(8,128)S(1)}, f32[128,2048]{1,0:T(8,128)S(1)}, u32[]{:S(2)}, u32[]{:S(2)}) collective-permute-start(f32[128,2048]{1,0:T(8,128)S(1)} %fusion.17), channel_id=1, source_target_pairs={{0,4},{4,0},{1,5},{5,1},{2,6},{6,2},{3,7},{7,3}} | collective-permute-start | bytes 3145736 | tf_op jit(solution)/shard_map/ppermute | solution.py:387
  666.6 42.9 %collective-permute-start.29 = (f32[128,2048]{1,0:T(8,128)S(1)}, f32[128,2048]{1,0:T(8,128)S(1)}, u32[]{:S(2)}, u32[]{:S(2)}) collective-permute-start(f32[128,2048]{1,0:T(8,128)S(1)} %fusion.14), channel_id=1, source_target_pairs={{0,4},{4,0},{1,5},{5,1},{2,6},{6,2},{3,7},{7,3}} | collective-permute-start | bytes 3145736 | tf_op jit(solution)/shard_map/ppermute | solution.py:387
  694.2 43.4 %collective-permute-start.44 = (f32[512,640]{1,0:T(8,128)S(1)}, f32[512,640]{1,0:T(8,128)S(1)}, u32[]{:S(2)}, u32[]{:S(2)}) collective-permute-start(f32[512,640]{1,0:T(8,128)S(1)} %fusion.2), channel_id=1, source_target_pairs={{0,4},{4,0},{1,5},{5,1},{2,6},{6,2},{3,7},{7,3}} | collective-permute-start | bytes 3932168 | tf_op jit(solution)/shard_map/ppermute | solution.py:387
  696.0 67.8 %collective-permute-start.41 = (f32[512,640]{1,0:T(8,128)S(1)}, f32[512,640]{1,0:T(8,128)S(1)}, u32[]{:S(2)}, u32[]{:S(2)}) collective-permute-start(f32[512,640]{1,0:T(8,128)S(1)} %fusion.5), channel_id=1, source_target_pairs={{0,4},{4,0},{1,5},{5,1},{2,6},{6,2},{3,7},{7,3}} | collective-permute-start | bytes 3932168 | tf_op jit(solution)/shard_map/ppermute | solution.py:387
  (43 other events, 832.4 us)

commit v2 on v1

--- a/solution.py
+++ b/solution.py
@@ -1,5 +1,6 @@
 import functools
 import jax
+import numpy as np
 import jax.numpy as jnp
 from jax import lax
 from jax.experimental import pallas as pl
@@ -98,9 +99,30 @@
     return out
 
 
-def fwd_attn_kernel(x_ref, gain_ref, c_ref, s_ref, w0, w1, w2, w3, h_ref, qkv_ref, o_ref, w_ref, sem):
+def expand_tables(cs_ref, c_ref, s_ref):
+    cs = cs_ref[...]
+    lo = lane_iota(cs.shape) < HD
+    rolled = pltpu.roll(cs, HD, 1)
+    cos = jnp.where(lo, cs, rolled)
+    sin = jnp.where(lo, rolled, cs)
+    c_ref[:, 0:128] = cos * HD ** -0.5
+    s_ref[:, 0:128] = sin * HD ** -0.5
+    c_ref[:, 128:256] = jnp.where(lo, cos, 1.0)
+    s_ref[:, 128:256] = jnp.where(lo, sin, 0.0)
+
+
+def rotary_table():
+    half = HD // 2
+    inv_freq = np.float32(10000.0) ** (-(np.arange(half, dtype=np.float32) * np.float32(2.0 / HD)))
+    angles = np.arange(SEQ, dtype=np.float32)[:, None] * inv_freq[None, :]
+    cos, sin = np.cos(angles), np.sin(angles)
+    return np.concatenate([cos, cos, -sin, sin], axis=1).astype(np.float32)
+
+
+def fwd_attn_kernel(x_ref, gain_ref, cs_ref, w0, w1, w2, w3, h_ref, qkv_ref, o_ref, w_ref, c_ref, s_ref, sem):
     @pl.when(pl.program_id(0) == 0)
     def _():
+        expand_tables(cs_ref, c_ref, s_ref)
         load_rows([((w0, w1, w2, w3), w_ref)], sem)
 
     x = x_ref[...].astype(F32)
@@ -162,17 +184,11 @@
 
 
 def store_grad_rows(acc, width, own_ref, xp_ref, send_ref, sem, by_cols):
-    move_grad_rows(acc, width, own_ref, xp_ref, send_ref, sem, by_cols, False)
-
-
-def move_grad_rows(acc, width, own_ref, xp_ref, send_ref, sem, by_cols, inward):
     own = owners()
     copies = []
     for r, dst in enumerate((own_ref, send_ref.at[0], xp_ref, send_ref.at[1])):
         start = pl.multiple_of(own[r] * width, 128)
         src = acc.at[:, pl.ds(start, width)] if by_cols else acc.at[pl.ds(start, width), :]
-        if inward:
-            src, dst = dst, src
         cp = pltpu.make_async_copy(src, dst, sem.at[r])
         cp.start()
         copies.append(cp)
@@ -198,6 +214,36 @@
         store_grad_rows(acc, (D + FF) // 4, own_ref, xp_ref, send_ref, sem, True)
 
 
+def mlp_grads(dy, h_t, wo_ref, row_base, zg_ref, zu_ref, dzg_ref, dzu_ref, acc, width, cw, side=None):
+    def dz_of(c):
+        cols = slice(c * cw, (c + 1) * cw)
+        rows = slice(row_base + c * cw, row_base + (c + 1) * cw)
+        dm = dot_nt(dy, wo_ref[rows, :]).astype(BF16).astype(F32)
+        g = zg_ref[:, cols].astype(F32)
+        u = zu_ref[:, cols].astype(F32)
+        sig = jax.nn.sigmoid(g)
+        sl = g * sig
+        du = (dm * sl).astype(BF16)
+        dg = (dm * u * (sig + sl * (1.0 - sig))).astype(BF16)
+        dzu_ref[:, cols] = du
+        dzg_ref[:, cols] = dg
+        return dg, du
+
+    def add_dw(c, parts):
+        dg, du = parts
+        acc[:, c * cw:(c + 1) * cw] += dot(h_t, dg)
+        acc[:, width + c * cw:width + (c + 1) * cw] += dot(h_t, du)
+
+    n = width // cw
+    prev = dz_of(0)
+    for c in range(n):
+        nxt = dz_of(c + 1) if c + 1 < n else None
+        if side is not None:
+            side(c)
+        add_dw(c, prev)
+        prev = nxt
+
+
 def bmlp_kernel(half, dy_ref, h_ref, zg_ref, zu_ref, w0, w1, w2, w3, dzg_ref, dzu_ref, own_ref, xp_ref, send_ref,
                 wo_ref, acc, sem):
     step = pl.program_id(0)
@@ -208,48 +254,48 @@
         load_rows([((w0, w1, w2, w3), wo_ref)], sem)
         acc[...] = jnp.zeros_like(acc)
 
+    mlp_grads(dy_ref[...], h_ref[...].T, wo_ref, D + half * hw, zg_ref, zu_ref, dzg_ref, dzu_ref, acc, hw, 256)
+
+    @pl.when(step == pl.num_programs(0) - 1)
+    def _():
+        store_grad_rows(acc, D // 4, own_ref, xp_ref, send_ref, sem, False)
+
+
+def bmlp_dwo_kernel(dy_ref, h_ref, o_ref, m_ref, zg_ref, zu_ref, w0, w1, w2, w3, dzg_ref, dzu_ref,
+                    oo_ref, ox_ref, os_ref, own_ref, xp_ref, send_ref, wo_ref, acc_o, acc, sem):
+    step = pl.program_id(0)
+
+    @pl.when(step == 0)
+    def _():
+        load_rows([((w0, w1, w2, w3), wo_ref)], sem)
+        acc[...] = jnp.zeros_like(acc)
+        acc_o[...] = jnp.zeros_like(acc_o)
+
     dy = dy_ref[...]
+    dy_t = dy.T
     cw = 256
-    h_t = h_ref[...].T
-    n = hw // cw
-
-    def dm_of(c):
-        row0 = D + half * hw + c * cw
-        return dot_nt(dy, wo_ref[row0:row0 + cw, :]).astype(BF16)
-
-    for c in range(n):
-        cols = slice(c * cw, (c + 1) * cw)
-        dm = dm_of(c).astype(F32)
-        g = zg_ref[:, cols].astype(F32)
-        u = zu_ref[:, cols].astype(F32)
-        sig = jax.nn.sigmoid(g)
-        sl = g * sig
-        dzu_ref[:, cols] = (dm * sl).astype(BF16)
-        dzg_ref[:, cols] = (dm * u * (sig + sl * (1.0 - sig))).astype(BF16)
-    acc[:, 0:hw] += dot(h_t, dzg_ref[...])
-    acc[:, hw:2 * hw] += dot(h_t, dzu_ref[...])
+
+    def side(c):
+        acc_o[:, D + c * cw:D + (c + 1) * cw] += dot(dy_t, m_ref[:, c * cw:(c + 1) * cw])
+
+    acc_o[:, 0:D] += dot(dy_t, o_ref[...])
+    mlp_grads(dy, h_ref[...].T, wo_ref, D, zg_ref, zu_ref, dzg_ref, dzu_ref, acc, FF, cw, side)
 
     @pl.when(step == pl.num_programs(0) - 1)
     def _():
+        store_grad_rows(acc_o, (D + FF) // 4, oo_ref, ox_ref, os_ref, sem, True)
         store_grad_rows(acc, D // 4, own_ref, xp_ref, send_ref, sem, False)
 
 
-def battn_kernel(chained, *refs):
-    if chained:
-        (dy_ref, h_ref, qkv_ref, c_ref, s_ref, w0, w1, w2, w3, _, in_own, in_xp, in_send,
-         dz_ref, own_ref, xp_ref, send_ref, wo_ref, acc, sem) = refs
-    else:
-        (dy_ref, h_ref, qkv_ref, c_ref, s_ref, w0, w1, w2, w3,
-         dz_ref, own_ref, xp_ref, send_ref, wo_ref, acc, sem) = refs
+def battn_kernel(dy_ref, h_ref, qkv_ref, cs_ref, w0, w1, w2, w3, dz_ref, own_ref, xp_ref, send_ref,
+                 wo_ref, acc, c_ref, s_ref, sem):
     step = pl.program_id(0)
 
     @pl.when(step == 0)
     def _():
         load_rows([((w0, w1, w2, w3), wo_ref)], sem)
-        if chained:
-            move_grad_rows(acc, D // 4, in_own, in_xp, in_send, sem, False, True)
-        else:
-            acc[...] = jnp.zeros_like(acc)
+        expand_tables(cs_ref, c_ref, s_ref)
+        acc[...] = jnp.zeros_like(acc)
 
     do_all = dot_nt(dy_ref[...], wo_ref[0:D, :]).astype(BF16)
     lo = lane_iota((SEQ, 2 * HD)) < HD
@@ -313,11 +359,10 @@
         store_grad_rows(acc, D // 4, own_ref, xp_ref, send_ref, sem, False)
 
 
-def dx_kernel(x_ref, gain_ref, dy_ref, dzq_ref, dg0_ref, du0_ref, dg1_ref, du1_ref,
-              q0, q1, q2, q3, w0, w1, w2, w3, *rest):
-    dx_ref, dgain_ref, wq_ref, w_ref, sem = rest[-5:]
+def dx_kernel(spans, x_ref, gain_ref, dy_ref, dzq_ref, *refs):
+    dz_refs = refs[:len(spans)]
+    q0, q1, q2, q3, w0, w1, w2, w3, dx_ref, dgain_ref, wq_ref, w_ref, sem = refs[len(spans):]
     step = pl.program_id(0)
-    hw = FF // 2
 
     @pl.when(step == 0)
     def _():
@@ -325,10 +370,8 @@
         dgain_ref[...] = jnp.zeros_like(dgain_ref)
 
     dh = dot_nt(dzq_ref[...], wq_ref[...])
-    dh += dot_nt(dg0_ref[...], w_ref[:, 0:hw])
-    dh += dot_nt(dg1_ref[...], w_ref[:, hw:2 * hw])
-    dh += dot_nt(du0_ref[...], w_ref[:, 2 * hw:3 * hw])
-    dh += dot_nt(du1_ref[...], w_ref[:, 3 * hw:4 * hw])
+    for (start, width), dz_ref in zip(spans, dz_refs):
+        dh += dot_nt(dz_ref[...], w_ref[:, start:start + width])
     dh = dh.astype(BF16).astype(F32)
     x = x_ref[...].astype(F32)
     cen = x - jnp.mean(x, axis=-1, keepdims=True)
@@ -401,16 +444,7 @@
         n_batch = x_in.shape[0]
         n_tok = n_batch * SEQ
 
-        half = HD // 2
-        inv_freq = 10000.0 ** (-(jnp.arange(half, dtype=F32) * 2.0 / HD))
-        angles = jnp.arange(SEQ, dtype=F32)[:, None] * inv_freq[None, :]
-        cos, sin = jnp.cos(angles), jnp.sin(angles)
-        cos2 = jnp.concatenate([cos, cos], axis=1)
-        sin2 = jnp.concatenate([-sin, sin], axis=1)
-        qs = HD ** -0.5
-        ones, zeros = jnp.ones_like(cos2), jnp.zeros_like(cos2)
-        c_tab = jnp.concatenate([cos2 * qs, cos2 * qs, cos2, ones], axis=1)
-        s_tab = jnp.concatenate([sin2 * qs, sin2 * qs, sin2, zeros], axis=1)
+        cs_tab = jnp.asarray(rotary_table())
 
         q_pieces, g_pieces, o_pieces = [], [], []
         for l in range(n_layers):
@@ -434,12 +468,12 @@
         for l in range(n_layers):
             h, qkv, o = call(
                 fwd_attn_kernel, n_tok,
-                [tok_spec(D), full_spec((1, D)), full_spec((SEQ, 256)), full_spec((SEQ, 256))] + [ANY] * 4,
+                [tok_spec(D), full_spec((1, D)), full_spec((SEQ, 128))] + [ANY] * 4,
                 [((n_tok, D), BF16), ((n_tok, QKV), BF16), ((n_tok, D), BF16)],
                 [tok_spec(D), tok_spec(QKV), tok_spec(D)],
-                [pltpu.VMEM((D, QKV), BF16), sem((4,))],
+                [pltpu.VMEM((D, QKV), BF16), pltpu.VMEM((SEQ, 256), F32), pltpu.VMEM((SEQ, 256), F32), sem((4,))],
                 mm * 2600, n_tok * D * 8,
-            )(x, gain[l], c_tab, s_tab, *q_pieces[l])
+            )(x, gain[l], cs_tab, *q_pieces[l])
             z, m, y = call(
                 fwd_mlp_kernel, n_tok,
                 [tok_spec(D), tok_spec(D), tok_spec(D)] + [ANY] * 8,
@@ -462,62 +496,63 @@
 
         for l in reversed(range(n_layers)):
             xl, h, qkv, o, z, m = saved[l]
-            g = call(
-                dwo_kernel, n_tok, [tok_spec(D), tok_spec(D), tok_spec(FF)],
-                grad_outs((D, q4)), [ANY] * 3,
-                [pltpu.VMEM((D, D + FF), F32), sem((4,))],
-                mm * 2560, n_tok * D * 12,
-            )(dy, o, m)
-            d_wout[l] = reduce4(*g).T
             hw = FF // 2
-            dzs, win_parts = [], []
-            for hf in range(2):
+            n_half = 2 if l == 0 else 1
+            fw = FF // n_half
+            dzs, spans, win_parts = [], [], []
+            if n_half == 1:
                 dg, du, *g = call(
-                    functools.partial(bmlp_kernel, hf), n_tok,
-                    [tok_spec(D), tok_spec(D), tok_spec(hw, hf), tok_spec(hw, 2 + hf)] + [ANY] * 4,
-                    [((n_tok, hw), BF16), ((n_tok, hw), BF16)] + grad_outs((D // 4, 2 * hw)),
-                    [tok_spec(hw), tok_spec(hw)] + [ANY] * 3,
-                    [pltpu.VMEM((D + FF, D), BF16), pltpu.VMEM((D, 2 * hw), F32), sem((4,))],
-                    mm * 3072, n_tok * D * 20,
-                )(dy, h, z, z, *o_pieces[l])
-                dzs += [dg, du]
-                win_parts.append(reduce4(*g))
-            n_part = 2 if l == 0 else 1
-            n_sub = n_tok // n_part
-            dzq, g = None, ()
-            for part in range(n_part):
-                f0 = part * n_sub // TOK
-                prev = (dzq, *g) if part else ()
-                dzq, *g = call(
-                    functools.partial(battn_kernel, part > 0), n_sub,
-                    [tok_spec(D, 0, f0), tok_spec(D, 0, f0), tok_spec(QKV, 0, f0), full_spec((SEQ, 256)),
-                     full_spec((SEQ, 256))] + [ANY] * (4 + len(prev)),
-                    [((n_tok, QKV), BF16)] + grad_outs((D // 4, QKV)),
-                    [tok_spec(QKV, 0, f0)] + [ANY] * 3,
-                    [pltpu.VMEM((D + FF, D), BF16), pltpu.VMEM((D, QKV), F32), sem((4,))],
-                    mm * 6200 / n_part, n_tok * D * 10 / n_part,
-                    {9: 0} if part else None,
-                )(dy, h, qkv, c_tab, s_tab, *o_pieces[l], *prev)
+                    bmlp_dwo_kernel, n_tok,
+                    [tok_spec(D)] * 3 + [tok_spec(FF), tok_spec(FF, 0), tok_spec(FF, 1)] + [ANY] * 4,
+                    [((n_tok, FF), BF16), ((n_tok, FF), BF16)] + grad_outs((D, q4)) + grad_outs((D // 4, 2 * FF)),
+                    [tok_spec(FF), tok_spec(FF)] + [ANY] * 6,
+                    [pltpu.VMEM((D + FF, D), BF16), pltpu.VMEM((D, D + FF), F32), pltpu.VMEM((D, 2 * FF), F32),
+                     sem((4,))],
+                    mm * 8704, n_tok * D * 50,
+                )(dy, h, o, m, z, z, *o_pieces[l])
+                dzs, spans = [dg, du], [(0, FF), (FF, FF)]
+                d_wout[l] = reduce4(*g[:3]).T
+                win_parts.append(reduce4(*g[3:]))
+            else:
+                g = call(
+                    dwo_kernel, n_tok, [tok_spec(D), tok_spec(D), tok_spec(FF)],
+                    grad_outs((D, q4)), [ANY] * 3,
+                    [pltpu.VMEM((D, D + FF), F32), sem((4,))],
+                    mm * 2560, n_tok * D * 12,
+                )(dy, o, m)
+                d_wout[l] = reduce4(*g).T
+                for hf in range(2):
+                    dg, du, *g = call(
+                        functools.partial(bmlp_kernel, hf), n_tok,
+                        [tok_spec(D), tok_spec(D), tok_spec(hw, hf), tok_spec(hw, 2 + hf)] + [ANY] * 4,
+                        [((n_tok, hw), BF16), ((n_tok, hw), BF16)] + grad_outs((D // 4, 2 * hw)),
+                        [tok_spec(hw), tok_spec(hw)] + [ANY] * 3,
+                        [pltpu.VMEM((D + FF, D), BF16), pltpu.VMEM((D, 2 * hw), F32), sem((4,))],
+                        mm * 3072, n_tok * D * 20,
+                    )(dy, h, z, z, *o_pieces[l])
+                    dzs += [dg, du]
+                    spans += [(hf * hw, hw), (FF + hf * hw, hw)]
+                    win_parts.append(reduce4(*g))
+            dzq, *g = call(
+                battn_kernel, n_tok,
+                [tok_spec(D), tok_spec(D), tok_spec(QKV), full_spec((SEQ, 128))] + [ANY] * 4,
+                [((n_tok, QKV), BF16)] + grad_outs((D // 4, QKV)),
+                [tok_spec(QKV)] + [ANY] * 3,
+                [pltpu.VMEM((D + FF, D), BF16), pltpu.VMEM((D, QKV), F32), pltpu.VMEM((SEQ, 256), F32),
+                 pltpu.VMEM((SEQ, 256), F32), sem((4,))],
+                mm * 6200, n_tok * D * 10,
+            )(dy, h, qkv, cs_tab, *o_pieces[l])
             wq = reduce4(*g)
-            p0, p1 = win_parts
-            d_win[l] = jnp.concatenate([wq, p0[:, :hw], p1[:, :hw], p0[:, hw:], p1[:, hw:]], axis=1)
-            dx, gains = None, []
-            for part in range(n_part):
-                f0 = part * n_sub // TOK
-                prev = (dx,) if part else ()
-                dx, d_g = call(
-                    dx_kernel, n_sub,
-                    [tok_spec(D, 0, f0), full_spec((1, D)), tok_spec(D, 0, f0), tok_spec(QKV, 0, f0)]
-                    + [tok_spec(hw, 0, f0)] * 4 + [ANY] * (8 + len(prev)),
-                    [((n_tok, D), BF16), ((1, D), F32)],
-                    [tok_spec(D, 0, f0), full_spec((1, D))],
-                    [pltpu.VMEM((D, QKV), BF16), pltpu.VMEM((D, 2 * FF), BF16), sem((8,))],
-                    mm * 4736 / n_part, n_tok * D * 20 / n_part,
-                    {16: 0} if part else None,
-                )(xl, gain[l], dy, dzq, *dzs, *q_pieces[l], *g_pieces[l], *prev)
-                gains.append(d_g)
-            dy = dx
-            d_gain[l] = sum(gains)
+            d_win[l] = jnp.concatenate(
+                [wq] + [p[:, :fw] for p in win_parts] + [p[:, fw:] for p in win_parts], axis=1)
+            dy, d_gain[l] = call(
+                functools.partial(dx_kernel, tuple(spans)), n_tok,
+                [tok_spec(D), full_spec((1, D)), tok_spec(D), tok_spec(QKV)] + [tok_spec(fw)] * len(dzs) + [ANY] * 8,
+                [((n_tok, D), BF16), ((1, D), F32)],
+                [tok_spec(D), full_spec((1, D))],
+                [pltpu.VMEM((D, QKV), BF16), pltpu.VMEM((D, 2 * FF), BF16), sem((8,))],
+                mm * 4736, n_tok * D * 20,
+            )(xl, gain[l], dy, dzq, *dzs, *q_pieces[l], *g_pieces[l])
 
         gg = jnp.concatenate(d_gain, axis=0)
         gg = gg + pp_core(gg)

time: 776 us -> 761 us (0.981)
  Pallas kernels: 462 us -> 434 us
  waiting for transfers between devices: 234 us -> 247 us
    pallas_call x4 -> x2, Pallas kernels: 110 us -> 54.2 us  [inner_step(): call(functools.partial(bmlp_kernel, hf), n_tok, [tok_spec(D), tok_spec(D)...]
    pallas_call x6 -> x5, Pallas kernels: 170 us -> 217 us  [the longest x2 88.9 us: inner_step(): call(battn_kernel, n_tok, [tok_spec(D), tok_spec(D), tok_spec(QKV), full_...]
    pallas_call x2 -> x1, Pallas kernels: 37.1 us -> 18.4 us  [inner_step(): call(dwo_kernel, n_tok, [tok_spec(D), tok_spec(D), tok_spec(FF)], grad_ou...]
    ppermute x9 -> x8, waiting for transfers between devices: 63.6 us -> 72.7 us  [pp_y(): return lax.ppermute(a, 'dp', y_perm)]
    ppermute x15 -> x14, waiting for transfers between devices: 166 us -> 171 us  [pp_x(): return lax.ppermute(a, 'fsdp', x_perm)]
    ppermute x15 -> x14, starting transfers between devices: 16.5 us -> 18.8 us  [pp_x(): return lax.ppermute(a, 'fsdp', x_perm)]
  transfers between devices with their start and end apart: 45 -> 42, of which waited for: 15 -> 12; matrix products, arithmetic and copies ran while one was open for 4% -> 3% of each run, Pallas kernels for 60% -> 34%
where the time goes in v2:
time: 761 us; the launch traced here: 753 us
  Pallas kernels  434 us (57%)
  waiting for transfers between devices  247 us (32%)
  starting transfers between devices  34.8 us (5%)
  other arithmetic  22.5 us (3%)
  local copies, waits for them, and re-layouts  13.6 us (2%)
    ppermute x14, waiting for transfers between devices, pp_x(): return lax.ppermute(a, 'fsdp', x_perm)  171 us
    pallas_call x2, Pallas kernels, inner_step(): call(battn_kernel, n_tok, [tok_spec(D), tok_spec(D), tok_spec(QKV), full_...  88.9 us
    pallas_call x2, Pallas kernels, inner_step(): call(fwd_mlp_kernel, n_tok, [tok_spec(D), tok_spec(D), tok_spec(D)] + [AN...  76.9 us
    ppermute x8, waiting for transfers between devices, pp_y(): return lax.ppermute(a, 'dp', y_perm)  72.7 us
    pallas_call x2, Pallas kernels, inner_step(): call(functools.partial(dx_kernel, tuple(spans)), n_tok, [tok_spec(D), ful...  67.3 us
    pallas_call x2, Pallas kernels, inner_step(): call(fwd_attn_kernel, n_tok, [tok_spec(D), full_spec((1, D)), full_spec((...  67.1 us
    pallas_call x1, Pallas kernels, inner_step(): call(bmlp_dwo_kernel, n_tok, [tok_spec(D)] * 3 + [tok_spec(FF), tok_spec(...  60.9 us
    pallas_call x2, Pallas kernels, inner_step(): call(functools.partial(bmlp_kernel, hf), n_tok, [tok_spec(D), tok_spec(D)...  54.2 us
  transfers between devices with their start and end apart: 42, of which 12 were waited for; matrix products, arithmetic and copies ran while one was open for 3% of the time, Pallas kernels for 34%

profile of v2, /device:TPU:0, one launch (start us, length us, event | category | flops | bytes accessed | tf_op | source)
XLA Modules:
  0.0 752.9 jit_solution(5368762024264240629)
XLA Ops:
  0.6 1.7 slice_bitcast_fusion.18
  3.1 3.3 collective-permute-start.1
  10.0 1.7 collective-permute-start.4
  12.5 2.5 collective-permute-done.2.w3.refs_7_
  14.9 2.5 collective-permute-start.10
  17.5 30.8 %collective-permute-done.4.g2.refs_10_ = bf16[128,4096]{1,0:T(8,128)(2,1)} collective-permute-done((bf16[128,4096]{1,0:T(8,128)(2,1)}, bf16[128,4096]{1,0:T(8,128)(2,1)}, u32[]{:S(2)}, u32[]{:S(2)}) %collective-permute-start.4) | collective-permute-done | bytes 1048608 | tf_op jit(solution)/shard_map/ppermute | solution.py:427
  49.5 33.6 %shard_map.101 = (bf16[4096,512]{1,0:T(8,128)(2,1)}, bf16[4096,640]{1,0:T(8,128)(2,1)}, bf16[4096,512]{1,0:T(8,128)(2,1)}) custom-call(bf16[4096,512]{1,0:T(8,128)(2,1)} %bitcast.115, f32[1,512]{1,0:T(1,128)} %bitcast.108, f32[256,128]{1,0:T(8,128)} %constant.31.clone.cs_ref, bf16[128,768]{1,0:T(8,128)(2,1)} %copy-done.25, bf16[128,768]{1,0:T(8,128)(2,1)} %copy-done.28, ...), custom_call_target="tpu_custom_call" | custom-call | flops 10905190400 | bytes 16777216 | tf_op jit(solution)/shard_map/pallas_call | solution.py:469
  83.4 2.5 collective-permute-start.16
  86.7 38.5 %shard_map.102 = (bf16[4096,4096]{1,0:T(8,128)(2,1)}, bf16[4096,2048]{1,0:T(8,128)(2,1)}, bf16[4096,512]{1,0:T(8,128)(2,1)}) custom-call(bf16[4096,512]{1,0:T(8,128)(2,1)} %bitcast.116, bf16[4096,512]{1,0:T(8,128)(2,1)} %get-tuple-element.50.h_ref, bf16[4096,512]{1,0:T(8,128)(2,1)} %get-tuple-element.51.o_ref, ...), custom_call_target="tpu_custom_call" | custom-call | flops 28101836800 | bytes 67108864 | tf_op jit(solution)/shard_map/pallas_call | solution.py:477
  126.9 33.6 %shard_map.103 = (bf16[4096,512]{1,0:T(8,128)(2,1)}, bf16[4096,640]{1,0:T(8,128)(2,1)}, bf16[4096,512]{1,0:T(8,128)(2,1)}) custom-call(bf16[4096,512]{1,0:T(8,128)(2,1)} %get-tuple-element.52.x_ref, f32[1,512]{1,0:T(1,128)} %bitcast.110, f32[256,128]{1,0:T(8,128)} %constant.31.clone.cs_ref, bf16[128,640]{1,0:T(8,128)(2,1)} %get-tuple-element.102.w0.refs_2_, ...), custom_call_target="tpu_custom_call" | custom-call | flops 10905190400 | bytes 16777216 | tf_op jit(solution)/shard_map/pallas_call | solution.py:469
  161.4 44.3 %shard_map.105 = (bf16[4096,640]{1,0:T(8,128)(2,1)}, f32[128,640]{1,0:T(8,128)}, f32[128,640]{1,0:T(8,128)}, f32[2,128,640]{2,1,0:T(8,128)}) custom-call(bf16[4096,512]{1,0:T(8,128)(2,1)} %bitcast.112, bf16[4096,512]{1,0:T(8,128)(2,1)} %get-tuple-element.53.h_ref, bf16[4096,640]{1,0:T(8,128)(2,1)} %get-tuple-element.56.qkv_ref, ...), custom_call_target="tpu_custom_call" | custom-call | flops 26004684800 | bytes 20971520 | tf_op jit(solution)/shard_map/pallas_call | solution.py:536
  206.7 38.4 %shard_map.104 = (bf16[4096,4096]{1,0:T(8,128)(2,1)}, bf16[4096,2048]{1,0:T(8,128)(2,1)}, bf16[4096,512]{1,0:T(8,128)(2,1)}) custom-call(bf16[4096,512]{1,0:T(8,128)(2,1)} %get-tuple-element.52.x_ref, bf16[4096,512]{1,0:T(8,128)(2,1)} %get-tuple-element.53.h_ref, bf16[4096,512]{1,0:T(8,128)(2,1)} %get-tuple-element.54.o_ref, ...), custom_call_target="tpu_custom_call" | custom-call | flops 28101836800 | bytes 67108864 | tf_op jit(solution)/shard_map/pallas_call | solution.py:477
  245.1 60.9 %shard_map.106 = (bf16[4096,2048]{1,0:T(8,128)(2,1)}, bf16[4096,2048]{1,0:T(8,128)(2,1)}, f32[512,640]{1,0:T(8,128)}, f32[512,640]{1,0:T(8,128)}, f32[2,512,640]...) custom-call(bf16[4096,512]{1,0:T(8,128)(2,1)} %bitcast.113, ...), custom_call_target="tpu_custom_call" | custom-call | flops 36507222016 | bytes 104857600 | tf_op jit(solution)/shard_map/pallas_call | solution.py:504
  306.0 33.5 %shard_map.107 = (bf16[4096,512]{1,0:T(8,128)(2,1)}, f32[1,512]{1,0:T(1,128)}) custom-call(bf16[4096,512]{1,0:T(8,128)(2,1)} %get-tuple-element.52.x_ref, f32[1,512]{1,0:T(1,128)} %bitcast.111, bf16[4096,512]{1,0:T(8,128)(2,1)} %bitcast.114, bf16[4096,640]{1,0:T(8,128)(2,1)} %get-tuple-element.57.dzq_ref, bf16[4096,2048]{1,0:T(8,128)(2,1)} %get-tuple-element.60.refs_0_, ...), custom_call_target="tpu_custom_call" | custom-call | flops 19864223744 | bytes 41943040 | tf_op jit(solution)/shard_map/pallas_call | solution.py:548
  339.5 44.6 %shard_map.108 = (bf16[4096,640]{1,0:T(8,128)(2,1)}, f32[128,640]{1,0:T(8,128)}, f32[128,640]{1,0:T(8,128)}, f32[2,128,640]{2,1,0:T(8,128)}) custom-call(bf16[4096,512]{1,0:T(8,128)(2,1)} %get-tuple-element.62.dy_ref, bf16[4096,512]{1,0:T(8,128)(2,1)} %get-tuple-element.50.h_ref, bf16[4096,640]{1,0:T(8,128)(2,1)} %get-tuple-element.63.qkv_ref, ...), custom_call_target="tpu_custom_call" | custom-call | flops 26004684800 | bytes 20971520 | tf_op jit(solution)/shard_map/pallas_call | solution.py:536
  384.7 27.1 %shard_map.110 = (bf16[4096,1024]{1,0:T(8,128)(2,1)}, bf16[4096,1024]{1,0:T(8,128)(2,1)}, f32[128,2048]{1,0:T(8,128)}, f32[128,2048]{1,0:T(8,128)}, f32[2,128,2048]{2,1,0:T(8,128)}) custom-call(bf16[4096,512]{1,0:T(8,128)(2,1)} %get-tuple-element.62.dy_ref, bf16[4096,512]{1,0:T(8,128)(2,1)} %get-tuple-element.50.h_ref, ...), custom_call_target="tpu_custom_call" | custom-call | flops 12884901888 | bytes 41943040 | tf_op jit(solution)/shard_map/pallas_call | solution.py:525
  411.8 27.1 %shard_map.109 = (bf16[4096,1024]{1,0:T(8,128)(2,1)}, bf16[4096,1024]{1,0:T(8,128)(2,1)}, f32[128,2048]{1,0:T(8,128)}, f32[128,2048]{1,0:T(8,128)}, f32[2,128,2048]{2,1,0:T(8,128)}) custom-call(bf16[4096,512]{1,0:T(8,128)(2,1)} %get-tuple-element.62.dy_ref, bf16[4096,512]{1,0:T(8,128)(2,1)} %get-tuple-element.50.h_ref, ...), custom_call_target="tpu_custom_call" | custom-call | flops 12884901888 | bytes 41943040 | tf_op jit(solution)/shard_map/pallas_call | solution.py:525
  439.0 33.9 %shard_map.111 = (bf16[4096,512]{1,0:T(8,128)(2,1)}, f32[1,512]{1,0:T(1,128)}) custom-call(bf16[4096,512]{1,0:T(8,128)(2,1)} %bitcast.117, f32[1,512]{1,0:T(1,128)} %bitcast.109, bf16[4096,512]{1,0:T(8,128)(2,1)} %get-tuple-element.62.dy_ref, bf16[4096,640]{1,0:T(8,128)(2,1)} %get-tuple-element.64.dzq_ref, bf16[4096,1024]{1,0:T(8,128)(2,1)} %get-tuple-element.66.refs_0_, ...), custom_call_target="tpu_custom_call" | custom-call | flops 19864223744 | bytes 41943040 | tf_op jit(solution)/shard_map/pallas_call | solution.py:548
  481.3 6.4 collective-permute-done.22
  489.3 4.4 collective-permute-done.31
  495.8 18.4 %shard_map.112 = (f32[512,640]{1,0:T(8,128)}, f32[512,640]{1,0:T(8,128)}, f32[2,512,640]{2,1,0:T(8,128)}) custom-call(bf16[4096,512]{1,0:T(8,128)(2,1)} %get-tuple-element.62.dy_ref, bf16[4096,512]{1,0:T(8,128)(2,1)} %get-tuple-element.51.o_ref, bf16[4096,2048]{1,0:T(8,128)(2,1)} %get-tuple-element.88.m_ref), custom_call_target="tpu_custom_call" | custom-call | flops 10737418240 | bytes 25165824 | tf_op jit(solution)/shard_map/pallas_call | solution.py:517
  523.3 1.9 fusion
  528.4 17.5 %collective-permute-done.28 = f32[128,2048]{1,0:T(8,128)S(1)} collective-permute-done((f32[128,2048]{1,0:T(8,128)S(1)}, f32[128,2048]{1,0:T(8,128)S(1)}, u32[]{:S(2)}, u32[]{:S(2)}) %collective-permute-start.28) | collective-permute-done | bytes 1048608 | tf_op jit(solution)/shard_map/ppermute | solution.py:427
  548.9 19.5 %collective-permute-done.25 = f32[128,2048]{1,0:T(8,128)S(1)} collective-permute-done((f32[128,2048]{1,0:T(8,128)S(1)}, f32[128,2048]{1,0:T(8,128)S(1)}, u32[]{:S(2)}, u32[]{:S(2)}) %collective-permute-start.25) | collective-permute-done | bytes 1048608 | tf_op jit(solution)/shard_map/ppermute | solution.py:427
  571.4 70.0 %collective-permute-done.37 = f32[512,640]{1,0:T(8,128)S(1)} collective-permute-done((f32[512,640]{1,0:T(8,128)S(1)}, f32[512,640]{1,0:T(8,128)S(1)}, u32[]{:S(2)}, u32[]{:S(2)}) %collective-permute-start.37) | collective-permute-done | bytes 1310752 | tf_op jit(solution)/shard_map/ppermute | solution.py:427
  643.2 3.3 fusion.2
  647.8 20.7 %collective-permute-done.40 = f32[512,640]{1,0:T(8,128)S(1)} collective-permute-done((f32[512,640]{1,0:T(8,128)S(1)}, f32[512,640]{1,0:T(8,128)S(1)}, u32[]{:S(2)}, u32[]{:S(2)}) %collective-permute-start.40) | collective-permute-done | bytes 1310752 | tf_op jit(solution)/shard_map/ppermute | solution.py:427
  670.7 2.6 collective-permute-done.38
  673.4 70.1 %collective-permute-done.41 = f32[512,640]{1,0:T(8,128)S(1)} collective-permute-done((f32[512,640]{1,0:T(8,128)S(1)}, f32[512,640]{1,0:T(8,128)S(1)}, u32[]{:S(2)}, u32[]{:S(2)}) %collective-permute-start.41) | collective-permute-done | bytes 1310752 | tf_op jit(solution)/shard_map/ppermute | solution.py:430
  743.9 2.1 copy.15
  746.0 2.5 add.147
  750.1 2.5 pad_maximum_fusion
  (185 shorter events, 49.2 us)
Async XLA Ops:
  7.9 41.1 %collective-permute-start.7 = (bf16[640,512]{1,0:T(8,128)(2,1)S(1)}, bf16[640,512]{1,0:T(8,128)(2,1)S(1)}, u32[]{:S(2)}, u32[]{:S(2)}) collective-permute-start(bf16[640,512]{1,0:T(8,128)(2,1)S(1)} %get-tuple-element.105.u0.w0), channel_id=1, source_target_pairs={{0,2},{2,0},{1,3},{3,1},{4,6},{6,4},{5,7},{7,5}} | collective-permute-start | bytes 1966088 | tf_op jit(solution)/shard_map/ppermute | solution.py:427
  8.1 75.3 %collective-permute-start.6 = (bf16[640,512]{1,0:T(8,128)(2,1)S(1)}, bf16[640,512]{1,0:T(8,128)(2,1)S(1)}, u32[]{:S(2)}, u32[]{:S(2)}) collective-permute-start(bf16[640,512]{1,0:T(8,128)(2,1)S(1)} %get-tuple-element.105.u0.w0), channel_id=1, source_target_pairs={{0,1},{1,0},{2,3},{3,2},{4,5},{5,4},{6,7},{7,6}} | collective-permute-start | bytes 1966088 | tf_op jit(solution)/shard_map/ppermute | solution.py:424
  10.0 38.4 %collective-permute-start.4 = (bf16[128,4096]{1,0:T(8,128)(2,1)}, bf16[128,4096]{1,0:T(8,128)(2,1)}, u32[]{:S(2)}, u32[]{:S(2)}) collective-permute-start(bf16[128,4096]{1,0:T(8,128)(2,1)} %get-tuple-element.101.g0.refs_8_), channel_id=1, source_target_pairs={{0,2},{2,0},{1,3},{3,1},{4,6},{6,4},{5,7},{7,5}} | collective-permute-start | bytes 3145736 | tf_op jit(solution)/shard_map/ppermute | solution.py:427
  11.8 74.1 %collective-permute-start.3 = (bf16[128,4096]{1,0:T(8,128)(2,1)}, bf16[128,4096]{1,0:T(8,128)(2,1)}, u32[]{:S(2)}, u32[]{:S(2)}) collective-permute-start(bf16[128,4096]{1,0:T(8,128)(2,1)} %get-tuple-element.101.g0.refs_8_), channel_id=1, source_target_pairs={{0,1},{1,0},{2,3},{3,2},{4,5},{5,4},{6,7},{7,6}} | collective-permute-start | bytes 3145736 | tf_op jit(solution)/shard_map/ppermute | solution.py:424
  14.9 68.2 %collective-permute-start.10 = (bf16[128,640]{1,0:T(8,128)(2,1)}, bf16[128,640]{1,0:T(8,128)(2,1)}, u32[]{:S(2)}, u32[]{:S(2)}) collective-permute-start(bf16[128,640]{1,0:T(8,128)(2,1)} %get-tuple-element.102.w0.refs_2_), channel_id=1, source_target_pairs={{0,2},{2,0},{1,3},{3,1},{4,6},{6,4},{5,7},{7,5}} | collective-permute-start | bytes 491528 | tf_op jit(solution)/shard_map/ppermute | solution.py:427
  48.4 37.8 %collective-permute-start.5 = (bf16[128,4096]{1,0:T(8,128)(2,1)}, bf16[128,4096]{1,0:T(8,128)(2,1)}, u32[]{:S(2)}, u32[]{:S(2)}) collective-permute-start(bf16[128,4096]{1,0:T(8,128)(2,1)} %collective-permute-done.4.g2.refs_10_), channel_id=1, source_target_pairs={{0,1},{1,0},{2,3},{3,2},{4,5},{5,4},{6,7},{7,6}} | collective-permute-start | bytes 3145736 | tf_op jit(solution)/shard_map/ppermute | solution.py:424
  49.0 36.9 %collective-permute-start.8 = (bf16[640,512]{1,0:T(8,128)(2,1)S(1)}, bf16[640,512]{1,0:T(8,128)(2,1)S(1)}, u32[]{:S(2)}, u32[]{:S(2)}) collective-permute-start(bf16[640,512]{1,0:T(8,128)(2,1)S(1)} %collective-permute-done.7.u2.w2), channel_id=1, source_target_pairs={{0,1},{1,0},{2,3},{3,2},{4,5},{5,4},{6,7},{7,6}} | collective-permute-start | bytes 1966088 | tf_op jit(solution)/shard_map/ppermute | solution.py:424
  83.1 42.1 %collective-permute-start.9 = (bf16[128,640]{1,0:T(8,128)(2,1)}, bf16[128,640]{1,0:T(8,128)(2,1)S(1)}, u32[]{:S(2)}, u32[]{:S(2)}) collective-permute-start(bf16[128,640]{1,0:T(8,128)(2,1)} %get-tuple-element.102.w0.refs_2_), channel_id=1, source_target_pairs={{0,1},{1,0},{2,3},{3,2},{4,5},{5,4},{6,7},{7,6}} | collective-permute-start | bytes 491528 | tf_op jit(solution)/shard_map/ppermute | solution.py:424
  83.4 42.4 %collective-permute-start.16 = (bf16[640,512]{1,0:T(8,128)(2,1)S(1)}, bf16[640,512]{1,0:T(8,128)(2,1)}, u32[]{:S(2)}, u32[]{:S(2)}) collective-permute-start(bf16[640,512]{1,0:T(8,128)(2,1)S(1)} %get-tuple-element.104.u0.w0), channel_id=1, source_target_pairs={{0,2},{2,0},{1,3},{3,1},{4,6},{6,4},{5,7},{7,5}} | collective-permute-start | bytes 1966088 | tf_op jit(solution)/shard_map/ppermute | solution.py:427
  85.9 74.6 %collective-permute-start.15 = (bf16[640,512]{1,0:T(8,128)(2,1)S(1)}, bf16[640,512]{1,0:T(8,128)(2,1)}, u32[]{:S(2)}, u32[]{:S(2)}) collective-permute-start(bf16[640,512]{1,0:T(8,128)(2,1)S(1)} %get-tuple-element.104.u0.w0), channel_id=1, source_target_pairs={{0,1},{1,0},{2,3},{3,2},{4,5},{5,4},{6,7},{7,6}} | collective-permute-start | bytes 1966088 | tf_op jit(solution)/shard_map/ppermute | solution.py:424
  85.9 39.9 %collective-permute-start.13 = (bf16[128,4096]{1,0:T(8,128)(2,1)}, bf16[128,4096]{1,0:T(8,128)(2,1)}, u32[]{:S(2)}, u32[]{:S(2)}) collective-permute-start(bf16[128,4096]{1,0:T(8,128)(2,1)} %get-tuple-element.100.g0.refs_6_), channel_id=1, source_target_pairs={{0,2},{2,0},{1,3},{3,1},{4,6},{6,4},{5,7},{7,5}} | collective-permute-start | bytes 3145736 | tf_op jit(solution)/shard_map/ppermute | solution.py:427
  86.2 40.1 %collective-permute-start.11 = (bf16[128,640]{1,0:T(8,128)(2,1)}, bf16[128,640]{1,0:T(8,128)(2,1)S(1)}, u32[]{:S(2)}, u32[]{:S(2)}) collective-permute-start(bf16[128,640]{1,0:T(8,128)(2,1)} %collective-permute-done.10.w2.refs_4_), channel_id=1, source_target_pairs={{0,1},{1,0},{2,3},{3,2},{4,5},{5,4},{6,7},{7,6}} | collective-permute-start | bytes 491528 | tf_op jit(solution)/shard_map/ppermute | solution.py:424
  125.2 80.5 %collective-permute-start.12 = (bf16[128,4096]{1,0:T(8,128)(2,1)S(1)}, bf16[128,4096]{1,0:T(8,128)(2,1)S(1)}, u32[]{:S(2)}, u32[]{:S(2)}) collective-permute-start(bf16[128,4096]{1,0:T(8,128)(2,1)S(1)} %copy-done.16), channel_id=1, source_target_pairs={{0,1},{1,0},{2,3},{3,2},{4,5},{5,4},{6,7},{7,6}} | collective-permute-start | bytes 3145736 | tf_op jit(solution)/shard_map/ppermute | solution.py:424
  125.8 34.7 %collective-permute-start.17 = (bf16[640,512]{1,0:T(8,128)(2,1)}, bf16[640,512]{1,0:T(8,128)(2,1)S(1)}, u32[]{:S(2)}, u32[]{:S(2)}) collective-permute-start(bf16[640,512]{1,0:T(8,128)(2,1)} %collective-permute-done.16.u2.w2), channel_id=1, source_target_pairs={{0,1},{1,0},{2,3},{3,2},{4,5},{5,4},{6,7},{7,6}} | collective-permute-start | bytes 1966088 | tf_op jit(solution)/shard_map/ppermute | solution.py:424
  125.8 79.9 %collective-permute-start.14 = (bf16[128,4096]{1,0:T(8,128)(2,1)}, bf16[128,4096]{1,0:T(8,128)(2,1)}, u32[]{:S(2)}, u32[]{:S(2)}) collective-permute-start(bf16[128,4096]{1,0:T(8,128)(2,1)} %collective-permute-done.13.g2.refs_8_), channel_id=1, source_target_pairs={{0,1},{1,0},{2,3},{3,2},{4,5},{5,4},{6,7},{7,6}} | collective-permute-start | bytes 3145736 | tf_op jit(solution)/shard_map/ppermute | solution.py:424
  384.1 91.7 %collective-permute-start.21 = (f32[2,128,640]{2,1,0:T(8,128)}, f32[2,128,640]{2,1,0:T(8,128)S(1)}, u32[]{:S(2)}, u32[]{:S(2)}) collective-permute-start(f32[2,128,640]{2,1,0:T(8,128)} %get-tuple-element.74), channel_id=1, source_target_pairs={{0,1},{1,0},{2,3},{3,2},{4,5},{5,4},{6,7},{7,6}} | collective-permute-start | bytes 1966088 | tf_op jit(solution)/shard_map/ppermute | solution.py:424
  384.2 92.9 %collective-permute-start.30 = (f32[2,128,640]{2,1,0:T(8,128)S(1)}, f32[2,128,640]{2,1,0:T(8,128)S(1)}, u32[]{:S(2)}, u32[]{:S(2)}) collective-permute-start(f32[2,128,640]{2,1,0:T(8,128)S(1)} %copy-done.32), channel_id=1, source_target_pairs={{0,1},{1,0},{2,3},{3,2},{4,5},{5,4},{6,7},{7,6}} | collective-permute-start | bytes 1966088 | tf_op jit(solution)/shard_map/ppermute | solution.py:424
  384.6 138.6 %collective-permute-start.33 = (f32[2,128,4096]{2,1,0:T(8,128)}, f32[2,128,4096]{2,1,0:T(8,128)}, u32[]{:S(2)}, u32[]{:S(2)}) collective-permute-start(f32[2,128,4096]{2,1,0:T(8,128)} %get-tuple-element.86), channel_id=1, source_target_pairs={{0,1},{1,0},{2,3},{3,2},{4,5},{5,4},{6,7},{7,6}} | collective-permute-start | bytes 12582920 | tf_op jit(solution)/shard_map/ppermute | solution.py:424
  474.0 44.4 %collective-permute-start.27 = (f32[2,128,2048]{2,1,0:T(8,128)}, f32[2,128,2048]{2,1,0:T(8,128)}, u32[]{:S(2)}, u32[]{:S(2)}) collective-permute-start(f32[2,128,2048]{2,1,0:T(8,128)} %get-tuple-element.80), channel_id=1, source_target_pairs={{0,1},{1,0},{2,3},{3,2},{4,5},{5,4},{6,7},{7,6}} | collective-permute-start | bytes 6291464 | tf_op jit(solution)/shard_map/ppermute | solution.py:424
  474.8 45.9 %collective-permute-start.24 = (f32[2,128,2048]{2,1,0:T(8,128)}, f32[2,128,2048]{2,1,0:T(8,128)}, u32[]{:S(2)}, u32[]{:S(2)}) collective-permute-start(f32[2,128,2048]{2,1,0:T(8,128)} %get-tuple-element.77), channel_id=1, source_target_pairs={{0,1},{1,0},{2,3},{3,2},{4,5},{5,4},{6,7},{7,6}} | collective-permute-start | bytes 6291464 | tf_op jit(solution)/shard_map/ppermute | solution.py:424
  493.7 23.1 %collective-permute-start.23 = (f32[128,640]{1,0:T(8,128)S(1)}, f32[128,640]{1,0:T(8,128)}, u32[]{:S(2)}, u32[]{:S(2)}) collective-permute-start(f32[128,640]{1,0:T(8,128)S(1)} %fusion.21), channel_id=1, source_target_pairs={{0,4},{4,0},{1,5},{5,1},{2,6},{6,2},{3,7},{7,3}} | collective-permute-start | bytes 983048 | tf_op jit(solution)/shard_map/ppermute | solution.py:430
  495.3 19.0 %collective-permute-start.32 = (f32[128,640]{1,0:T(8,128)S(1)}, f32[128,640]{1,0:T(8,128)S(1)}, u32[]{:S(2)}, u32[]{:S(2)}) collective-permute-start(f32[128,640]{1,0:T(8,128)S(1)} %fusion.18), channel_id=1, source_target_pairs={{0,4},{4,0},{1,5},{5,1},{2,6},{6,2},{3,7},{7,3}} | collective-permute-start | bytes 983048 | tf_op jit(solution)/shard_map/ppermute | solution.py:430
  519.8 26.1 %collective-permute-start.28 = (f32[128,2048]{1,0:T(8,128)S(1)}, f32[128,2048]{1,0:T(8,128)S(1)}, u32[]{:S(2)}, u32[]{:S(2)}) collective-permute-start(f32[128,2048]{1,0:T(8,128)S(1)} %fusion.9), channel_id=1, source_target_pairs={{0,2},{2,0},{1,3},{3,1},{4,6},{6,4},{5,7},{7,5}} | collective-permute-start | bytes 3145736 | tf_op jit(solution)/shard_map/ppermute | solution.py:427
  522.0 46.3 %collective-permute-start.25 = (f32[128,2048]{1,0:T(8,128)S(1)}, f32[128,2048]{1,0:T(8,128)S(1)}, u32[]{:S(2)}, u32[]{:S(2)}) collective-permute-start(f32[128,2048]{1,0:T(8,128)S(1)} %fusion.12), channel_id=1, source_target_pairs={{0,2},{2,0},{1,3},{3,1},{4,6},{6,4},{5,7},{7,5}} | collective-permute-start | bytes 3145736 | tf_op jit(solution)/shard_map/ppermute | solution.py:427
  525.2 118.0 %collective-permute-start.34 = (f32[128,4096]{1,0:T(8,128)S(1)}, f32[128,4096]{1,0:T(8,128)S(1)}, u32[]{:S(2)}, u32[]{:S(2)}) collective-permute-start(f32[128,4096]{1,0:T(8,128)S(1)} %fusion), channel_id=1, source_target_pairs={{0,2},{2,0},{1,3},{3,1},{4,6},{6,4},{5,7},{7,5}} | collective-permute-start | bytes 6291464 | tf_op jit(solution)/shard_map/ppermute | solution.py:427
  526.2 115.2 %collective-permute-start.37 = (f32[512,640]{1,0:T(8,128)S(1)}, f32[512,640]{1,0:T(8,128)S(1)}, u32[]{:S(2)}, u32[]{:S(2)}) collective-permute-start(f32[512,640]{1,0:T(8,128)S(1)} %fusion.6), channel_id=1, source_target_pairs={{0,2},{2,0},{1,3},{3,1},{4,6},{6,4},{5,7},{7,5}} | collective-permute-start | bytes 3932168 | tf_op jit(solution)/shard_map/ppermute | solution.py:427
  527.6 141.0 %collective-permute-start.40 = (f32[512,640]{1,0:T(8,128)S(1)}, f32[512,640]{1,0:T(8,128)S(1)}, u32[]{:S(2)}, u32[]{:S(2)}) collective-permute-start(f32[512,640]{1,0:T(8,128)S(1)} %fusion.3), channel_id=1, source_target_pairs={{0,2},{2,0},{1,3},{3,1},{4,6},{6,4},{5,7},{7,5}} | collective-permute-start | bytes 3932168 | tf_op jit(solution)/shard_map/ppermute | solution.py:427
  547.4 122.9 %collective-permute-start.29 = (f32[128,2048]{1,0:T(8,128)S(1)}, f32[128,2048]{1,0:T(8,128)S(1)}, u32[]{:S(2)}, u32[]{:S(2)}) collective-permute-start(f32[128,2048]{1,0:T(8,128)S(1)} %fusion.11), channel_id=1, source_target_pairs={{0,4},{4,0},{1,5},{5,1},{2,6},{6,2},{3,7},{7,3}} | collective-permute-start | bytes 3145736 | tf_op jit(solution)/shard_map/ppermute | solution.py:430
  569.8 100.6 %collective-permute-start.26 = (f32[128,2048]{1,0:T(8,128)S(1)}, f32[128,2048]{1,0:T(8,128)S(1)}, u32[]{:S(2)}, u32[]{:S(2)}) collective-permute-start(f32[128,2048]{1,0:T(8,128)S(1)} %fusion.14), channel_id=1, source_target_pairs={{0,4},{4,0},{1,5},{5,1},{2,6},{6,2},{3,7},{7,3}} | collective-permute-start | bytes 3145736 | tf_op jit(solution)/shard_map/ppermute | solution.py:430
  641.6 31.7 %collective-permute-start.38 = (f32[512,640]{1,0:T(8,128)S(1)}, f32[512,640]{1,0:T(8,128)S(1)}, u32[]{:S(2)}, u32[]{:S(2)}) collective-permute-start(f32[512,640]{1,0:T(8,128)S(1)} %fusion.8), channel_id=1, source_target_pairs={{0,4},{4,0},{1,5},{5,1},{2,6},{6,2},{3,7},{7,3}} | collective-permute-start | bytes 3932168 | tf_op jit(solution)/shard_map/ppermute | solution.py:430
  646.5 99.5 %collective-permute-start.35 = (f32[128,4096]{1,0:T(8,128)}, f32[128,4096]{1,0:T(8,128)}, u32[]{:S(2)}, u32[]{:S(2)}) collective-permute-start(f32[128,4096]{1,0:T(8,128)} %fusion.2), channel_id=1, source_target_pairs={{0,4},{4,0},{1,5},{5,1},{2,6},{6,2},{3,7},{7,3}} | collective-permute-start | bytes 6291464 | tf_op jit(solution)/shard_map/ppermute | solution.py:430
  668.7 74.8 %collective-permute-start.41 = (f32[512,640]{1,0:T(8,128)S(1)}, f32[512,640]{1,0:T(8,128)S(1)}, u32[]{:S(2)}, u32[]{:S(2)}) collective-permute-start(f32[512,640]{1,0:T(8,128)S(1)} %fusion.5), channel_id=1, source_target_pairs={{0,4},{4,0},{1,5},{5,1},{2,6},{6,2},{3,7},{7,3}} | collective-permute-start | bytes 3932168 | tf_op jit(solution)/shard_map/ppermute | solution.py:430
  (46 other events, 957.3 us)

commit v3 on v2

--- a/solution.py
+++ b/solution.py
@@ -39,7 +39,7 @@
     return [2 * x + c, 2 * x + (1 - c), 2 * (1 - x) + c, 2 * (1 - x) + (1 - c)]
 
 
-def load_rows(groups, sem):
+def start_rows(groups, sem):
     own = owners()
     copies = []
     for pieces, dst in groups:
@@ -50,6 +50,10 @@
             cp = pltpu.make_async_copy(src, dst.at[pl.ds(start, rows), :], sem.at[len(copies)])
             cp.start()
             copies.append(cp)
+    return copies
+
+
+def wait_all(copies):
     for cp in copies:
         cp.wait()
 
@@ -122,8 +126,9 @@
 def fwd_attn_kernel(x_ref, gain_ref, cs_ref, w0, w1, w2, w3, h_ref, qkv_ref, o_ref, w_ref, c_ref, s_ref, sem):
     @pl.when(pl.program_id(0) == 0)
     def _():
+        copies = start_rows([((w0, w1, w2, w3), w_ref)], sem)
         expand_tables(cs_ref, c_ref, s_ref)
-        load_rows([((w0, w1, w2, w3), w_ref)], sem)
+        wait_all(copies)
 
     x = x_ref[...].astype(F32)
     cen = x - jnp.mean(x, axis=-1, keepdims=True)
@@ -164,7 +169,8 @@
 def fwd_mlp_kernel(x_ref, h_ref, o_ref, g0, g1, g2, g3, u0, u1, u2, u3, z_ref, m_ref, y_ref, w_ref, wo_ref, sem):
     @pl.when(pl.program_id(0) == 0)
     def _():
-        load_rows([((g0, g1, g2, g3), w_ref), ((u0, u1, u2, u3), wo_ref)], sem)
+        copies = start_rows([((g0, g1, g2, g3), w_ref), ((u0, u1, u2, u3), wo_ref)], sem)
+        wait_all(copies)
 
     h = h_ref[...]
     cw = 512
@@ -183,17 +189,20 @@
     y_ref[...] = (x_ref[...].astype(F32) + acc).astype(BF16)
 
 
-def store_grad_rows(acc, width, own_ref, xp_ref, send_ref, sem, by_cols):
+def start_grad_rows(acc, width, own_ref, xp_ref, send_ref, sem, by_cols, first=0):
     own = owners()
     copies = []
-    for r, dst in enumerate((own_ref, send_ref.at[0], xp_ref, send_ref.at[1])):
+    for r, dst in ((1, send_ref.at[0]), (3, send_ref.at[1]), (0, own_ref), (2, xp_ref)):
         start = pl.multiple_of(own[r] * width, 128)
         src = acc.at[:, pl.ds(start, width)] if by_cols else acc.at[pl.ds(start, width), :]
-        cp = pltpu.make_async_copy(src, dst, sem.at[r])
+        cp = pltpu.make_async_copy(src, dst, sem.at[first + r])
         cp.start()
         copies.append(cp)
-    for cp in copies:
-        cp.wait()
+    return copies
+
+
+def store_grad_rows(*args):
+    wait_all(start_grad_rows(*args))
 
 
 def dwo_kernel(dy_ref, o_ref, m_ref, own_ref, xp_ref, send_ref, acc, sem):
@@ -251,8 +260,9 @@
 
     @pl.when(step == 0)
     def _():
-        load_rows([((w0, w1, w2, w3), wo_ref)], sem)
+        copies = start_rows([((w0, w1, w2, w3), wo_ref)], sem)
         acc[...] = jnp.zeros_like(acc)
+        wait_all(copies)
 
     mlp_grads(dy_ref[...], h_ref[...].T, wo_ref, D + half * hw, zg_ref, zu_ref, dzg_ref, dzu_ref, acc, hw, 256)
 
@@ -267,9 +277,10 @@
 
     @pl.when(step == 0)
     def _():
-        load_rows([((w0, w1, w2, w3), wo_ref)], sem)
+        copies = start_rows([((w0, w1, w2, w3), wo_ref)], sem)
         acc[...] = jnp.zeros_like(acc)
         acc_o[...] = jnp.zeros_like(acc_o)
+        wait_all(copies)
 
     dy = dy_ref[...]
     dy_t = dy.T
@@ -283,8 +294,9 @@
 
     @pl.when(step == pl.num_programs(0) - 1)
     def _():
-        store_grad_rows(acc_o, (D + FF) // 4, oo_ref, ox_ref, os_ref, sem, True)
-        store_grad_rows(acc, D // 4, own_ref, xp_ref, send_ref, sem, False)
+        copies = start_grad_rows(acc_o, (D + FF) // 4, oo_ref, ox_ref, os_ref, sem, True)
+        copies += start_grad_rows(acc, D // 4, own_ref, xp_ref, send_ref, sem, False, 4)
+        wait_all(copies)
 
 
 def battn_kernel(dy_ref, h_ref, qkv_ref, cs_ref, w0, w1, w2, w3, dz_ref, own_ref, xp_ref, send_ref,
@@ -293,9 +305,10 @@
 
     @pl.when(step == 0)
     def _():
-        load_rows([((w0, w1, w2, w3), wo_ref)], sem)
+        copies = start_rows([((w0, w1, w2, w3), wo_ref)], sem)
         expand_tables(cs_ref, c_ref, s_ref)
         acc[...] = jnp.zeros_like(acc)
+        wait_all(copies)
 
     do_all = dot_nt(dy_ref[...], wo_ref[0:D, :]).astype(BF16)
     lo = lane_iota((SEQ, 2 * HD)) < HD
@@ -366,8 +379,9 @@
 
     @pl.when(step == 0)
     def _():
-        load_rows([((q0, q1, q2, q3), wq_ref), ((w0, w1, w2, w3), w_ref)], sem)
+        copies = start_rows([((q0, q1, q2, q3), wq_ref), ((w0, w1, w2, w3), w_ref)], sem)
         dgain_ref[...] = jnp.zeros_like(dgain_ref)
+        wait_all(copies)
 
     dh = dot_nt(dzq_ref[...], wq_ref[...])
     for (start, width), dz_ref in zip(spans, dz_refs):
@@ -507,7 +521,7 @@
                     [((n_tok, FF), BF16), ((n_tok, FF), BF16)] + grad_outs((D, q4)) + grad_outs((D // 4, 2 * FF)),
                     [tok_spec(FF), tok_spec(FF)] + [ANY] * 6,
                     [pltpu.VMEM((D + FF, D), BF16), pltpu.VMEM((D, D + FF), F32), pltpu.VMEM((D, 2 * FF), F32),
-                     sem((4,))],
+                     sem((8,))],
                     mm * 8704, n_tok * D * 50,
                 )(dy, h, o, m, z, z, *o_pieces[l])
                 dzs, spans = [dg, du], [(0, FF), (FF, FF)]
@@ -557,9 +571,10 @@
         gg = jnp.concatenate(d_gain, axis=0)
         gg = gg + pp_core(gg)
         gg = gg + pp_x(gg)
+        gg, g_wout = lax.optimization_barrier((gg, jnp.stack(d_wout)))
         gg = gg + pp_y(gg)
         gg = lax.dynamic_slice(gg, (0, lax.axis_index("fsdp") * (D // 4)), (n_layers, D // 4))
-        return (x.reshape(x_in.shape), dy.reshape(x_in.shape), gg, jnp.stack(d_win), jnp.stack(d_wout))
+        return (x.reshape(x_in.shape), dy.reshape(x_in.shape), gg, jnp.stack(d_win), g_wout)
 
     return jax.shard_map(
         inner_step,

time: 761 us -> 799 us (1.050)
  waiting for transfers between devices: 247 us -> 281 us
    ppermute x8, waiting for transfers between devices: 72.7 us -> 94.5 us  [pp_y(): return lax.ppermute(a, 'dp', y_perm)]
    ppermute x14, waiting for transfers between devices: 171 us -> 185 us  [pp_x(): return lax.ppermute(a, 'fsdp', x_perm)]
  transfers between devices with their start and end apart: 42 -> 42, of which waited for: 12 -> 15; matrix products, arithmetic and copies ran while one was open for 3% -> 4% of each run, Pallas kernels for 34% -> 42%
where the time goes in v3:
time: 799 us; the launch traced here: 790 us
  Pallas kernels  431 us (54%)
  waiting for transfers between devices  281 us (35%)
  starting transfers between devices  30.9 us (4%)
  other arithmetic  28.9 us (4%)
  local copies, waits for them, and re-layouts  16.7 us (2%)
    ppermute x14, waiting for transfers between devices, pp_x(): return lax.ppermute(a, 'fsdp', x_perm)  185 us
    ppermute x8, waiting for transfers between devices, pp_y(): return lax.ppermute(a, 'dp', y_perm)  94.5 us
    pallas_call x2, Pallas kernels, inner_step(): call(battn_kernel, n_tok, [tok_spec(D), tok_spec(D), tok_spec(QKV), full_...  88.2 us
    pallas_call x2, Pallas kernels, inner_step(): call(fwd_mlp_kernel, n_tok, [tok_spec(D), tok_spec(D), tok_spec(D)] + [AN...  77 us
    pallas_call x2, Pallas kernels, inner_step(): call(fwd_attn_kernel, n_tok, [tok_spec(D), full_spec((1, D)), full_spec((...  67.2 us
    pallas_call x2, Pallas kernels, inner_step(): call(functools.partial(dx_kernel, tuple(spans)), n_tok, [tok_spec(D), ful...  67.2 us
    pallas_call x1, Pallas kernels, inner_step(): call(bmlp_dwo_kernel, n_tok, [tok_spec(D)] * 3 + [tok_spec(FF), tok_spec(...  59 us
    pallas_call x2, Pallas kernels, inner_step(): call(functools.partial(bmlp_kernel, hf), n_tok, [tok_spec(D), tok_spec(D)...  54.1 us
  transfers between devices with their start and end apart: 42, of which 15 were waited for; matrix products, arithmetic and copies ran while one was open for 4% of the time, Pallas kernels for 42%

profile of v3, /device:TPU:0, one launch (start us, length us, event | category | flops | bytes accessed | tf_op | source)
XLA Modules:
  0.0 790.4 jit_solution(3407401352291383174)
XLA Ops:
  3.3 3.3 collective-permute-start.1
  6.6 3.1 slice_bitcast_fusion.10
  16.8 19.2 %collective-permute-done.4.g2.refs_10_ = bf16[128,4096]{1,0:T(8,128)(2,1)} collective-permute-done((bf16[128,4096]{1,0:T(8,128)(2,1)}, bf16[128,4096]{1,0:T(8,128)(2,1)}, u32[]{:S(2)}, u32[]{:S(2)}) %collective-permute-start.4) | collective-permute-done | bytes 1048608 | tf_op jit(solution)/shard_map/ppermute | solution.py:441
  36.5 17.0 %collective-permute-done.10.w2.refs_4_ = bf16[128,640]{1,0:T(8,128)(2,1)} collective-permute-done((bf16[128,640]{1,0:T(8,128)(2,1)}, bf16[128,640]{1,0:T(8,128)(2,1)}, u32[]{:S(2)}, u32[]{:S(2)}) %collective-permute-start.10) | collective-permute-done | bytes 163872 | tf_op jit(solution)/shard_map/ppermute | solution.py:441
  54.1 33.6 %shard_map.101 = (bf16[4096,512]{1,0:T(8,128)(2,1)}, bf16[4096,640]{1,0:T(8,128)(2,1)}, bf16[4096,512]{1,0:T(8,128)(2,1)}) custom-call(bf16[4096,512]{1,0:T(8,128)(2,1)} %bitcast.114, f32[1,512]{1,0:T(1,128)} %bitcast.107, f32[256,128]{1,0:T(8,128)} %constant.31.clone.cs_ref, bf16[128,768]{1,0:T(8,128)(2,1)} %copy-done.21, ...), custom_call_target="tpu_custom_call" | custom-call | flops 10905190400 | bytes 16777216 | tf_op jit(solution)/shard_map/pallas_call | solution.py:483
  89.2 38.4 %shard_map.102 = (bf16[4096,4096]{1,0:T(8,128)(2,1)}, bf16[4096,2048]{1,0:T(8,128)(2,1)}, bf16[4096,512]{1,0:T(8,128)(2,1)}) custom-call(bf16[4096,512]{1,0:T(8,128)(2,1)} %bitcast.115, bf16[4096,512]{1,0:T(8,128)(2,1)} %get-tuple-element.52.h_ref, bf16[4096,512]{1,0:T(8,128)(2,1)} %get-tuple-element.53.o_ref, ...), custom_call_target="tpu_custom_call" | custom-call | flops 28101836800 | bytes 67108864 | tf_op jit(solution)/shard_map/pallas_call | solution.py:491
  128.8 33.6 %shard_map.103 = (bf16[4096,512]{1,0:T(8,128)(2,1)}, bf16[4096,640]{1,0:T(8,128)(2,1)}, bf16[4096,512]{1,0:T(8,128)(2,1)}) custom-call(bf16[4096,512]{1,0:T(8,128)(2,1)} %get-tuple-element.54.x_ref, f32[1,512]{1,0:T(1,128)} %bitcast.109, f32[256,128]{1,0:T(8,128)} %constant.31.clone.cs_ref, bf16[128,640]{1,0:T(8,128)(2,1)} %get-tuple-element.106.w0.refs_2_, ...), custom_call_target="tpu_custom_call" | custom-call | flops 10905190400 | bytes 16777216 | tf_op jit(solution)/shard_map/pallas_call | solution.py:483
  163.9 38.6 %shard_map.104 = (bf16[4096,4096]{1,0:T(8,128)(2,1)}, bf16[4096,2048]{1,0:T(8,128)(2,1)}, bf16[4096,512]{1,0:T(8,128)(2,1)}) custom-call(bf16[4096,512]{1,0:T(8,128)(2,1)} %get-tuple-element.54.x_ref, bf16[4096,512]{1,0:T(8,128)(2,1)} %get-tuple-element.55.h_ref, bf16[4096,512]{1,0:T(8,128)(2,1)} %get-tuple-element.56.o_ref, ...), custom_call_target="tpu_custom_call" | custom-call | flops 28101836800 | bytes 67108864 | tf_op jit(solution)/shard_map/pallas_call | solution.py:491
  202.4 59.0 %shard_map.106 = (bf16[4096,2048]{1,0:T(8,128)(2,1)}, bf16[4096,2048]{1,0:T(8,128)(2,1)}, f32[512,640]{1,0:T(8,128)}, f32[512,640]{1,0:T(8,128)}, f32[2,512,640]...) custom-call(bf16[4096,512]{1,0:T(8,128)(2,1)} %bitcast.111, ...), custom_call_target="tpu_custom_call" | custom-call | flops 36507222016 | bytes 104857600 | tf_op jit(solution)/shard_map/pallas_call | solution.py:518
  261.7 44.2 %shard_map.105 = (bf16[4096,640]{1,0:T(8,128)(2,1)}, f32[128,640]{1,0:T(8,128)}, f32[128,640]{1,0:T(8,128)}, f32[2,128,640]{2,1,0:T(8,128)}) custom-call(bf16[4096,512]{1,0:T(8,128)(2,1)} %bitcast.112, bf16[4096,512]{1,0:T(8,128)(2,1)} %get-tuple-element.55.h_ref, bf16[4096,640]{1,0:T(8,128)(2,1)} %get-tuple-element.58.qkv_ref, ...), custom_call_target="tpu_custom_call" | custom-call | flops 26004684800 | bytes 20971520 | tf_op jit(solution)/shard_map/pallas_call | solution.py:550
  305.9 33.5 %shard_map.107 = (bf16[4096,512]{1,0:T(8,128)(2,1)}, f32[1,512]{1,0:T(1,128)}) custom-call(bf16[4096,512]{1,0:T(8,128)(2,1)} %get-tuple-element.54.x_ref, f32[1,512]{1,0:T(1,128)} %bitcast.110, bf16[4096,512]{1,0:T(8,128)(2,1)} %bitcast.113, bf16[4096,640]{1,0:T(8,128)(2,1)} %get-tuple-element.59.dzq_ref, bf16[4096,2048]{1,0:T(8,128)(2,1)} %get-tuple-element.62.refs_0_, ...), custom_call_target="tpu_custom_call" | custom-call | flops 19864223744 | bytes 41943040 | tf_op jit(solution)/shard_map/pallas_call | solution.py:562
  339.4 26.9 %shard_map.110 = (bf16[4096,1024]{1,0:T(8,128)(2,1)}, bf16[4096,1024]{1,0:T(8,128)(2,1)}, f32[128,2048]{1,0:T(8,128)}, f32[128,2048]{1,0:T(8,128)}, f32[2,128,2048]{2,1,0:T(8,128)}) custom-call(bf16[4096,512]{1,0:T(8,128)(2,1)} %get-tuple-element.64.dy_ref, bf16[4096,512]{1,0:T(8,128)(2,1)} %get-tuple-element.52.h_ref, ...), custom_call_target="tpu_custom_call" | custom-call | flops 12884901888 | bytes 41943040 | tf_op jit(solution)/shard_map/pallas_call | solution.py:539
  366.3 27.2 %shard_map.109 = (bf16[4096,1024]{1,0:T(8,128)(2,1)}, bf16[4096,1024]{1,0:T(8,128)(2,1)}, f32[128,2048]{1,0:T(8,128)}, f32[128,2048]{1,0:T(8,128)}, f32[2,128,2048]{2,1,0:T(8,128)}) custom-call(bf16[4096,512]{1,0:T(8,128)(2,1)} %get-tuple-element.64.dy_ref, bf16[4096,512]{1,0:T(8,128)(2,1)} %get-tuple-element.52.h_ref, ...), custom_call_target="tpu_custom_call" | custom-call | flops 12884901888 | bytes 41943040 | tf_op jit(solution)/shard_map/pallas_call | solution.py:539
  393.5 44.0 %shard_map.108 = (bf16[4096,640]{1,0:T(8,128)(2,1)}, f32[128,640]{1,0:T(8,128)}, f32[128,640]{1,0:T(8,128)}, f32[2,128,640]{2,1,0:T(8,128)}) custom-call(bf16[4096,512]{1,0:T(8,128)(2,1)} %get-tuple-element.64.dy_ref, bf16[4096,512]{1,0:T(8,128)(2,1)} %get-tuple-element.52.h_ref, bf16[4096,640]{1,0:T(8,128)(2,1)} %get-tuple-element.65.qkv_ref, ...), custom_call_target="tpu_custom_call" | custom-call | flops 26004684800 | bytes 20971520 | tf_op jit(solution)/shard_map/pallas_call | solution.py:550
  437.5 33.7 %shard_map.111 = (bf16[4096,512]{1,0:T(8,128)(2,1)}, f32[1,512]{1,0:T(1,128)}) custom-call(bf16[4096,512]{1,0:T(8,128)(2,1)} %bitcast.116, f32[1,512]{1,0:T(1,128)} %bitcast.108, bf16[4096,512]{1,0:T(8,128)(2,1)} %get-tuple-element.64.dy_ref, bf16[4096,640]{1,0:T(8,128)(2,1)} %get-tuple-element.66.dzq_ref, bf16[4096,1024]{1,0:T(8,128)(2,1)} %get-tuple-element.68.refs_0_, ...), custom_call_target="tpu_custom_call" | custom-call | flops 19864223744 | bytes 41943040 | tf_op jit(solution)/shard_map/pallas_call | solution.py:562
  473.8 1.9 collective-permute-start.19
  477.4 18.7 %shard_map.112 = (f32[512,640]{1,0:T(8,128)}, f32[512,640]{1,0:T(8,128)}, f32[2,512,640]{2,1,0:T(8,128)}) custom-call(bf16[4096,512]{1,0:T(8,128)(2,1)} %get-tuple-element.64.dy_ref, bf16[4096,512]{1,0:T(8,128)(2,1)} %get-tuple-element.53.o_ref, bf16[4096,2048]{1,0:T(8,128)(2,1)} %get-tuple-element.75.m_ref), custom_call_target="tpu_custom_call" | custom-call | flops 10737418240 | bytes 25165824 | tf_op jit(solution)/shard_map/pallas_call | solution.py:531
  498.5 1.9 collective-permute-start.37
  501.4 6.9 collective-permute-done.37
  511.2 6.1 collective-permute-done.28
  519.7 6.5 collective-permute-done.38
  539.9 18.3 %collective-permute-done.34 = f32[128,2048]{1,0:T(8,128)S(1)} collective-permute-done((f32[128,2048]{1,0:T(8,128)S(1)}, f32[128,2048]{1,0:T(8,128)S(1)}, u32[]{:S(2)}, u32[]{:S(2)}) %collective-permute-start.34) | collective-permute-done | bytes 1048608 | tf_op jit(solution)/shard_map/ppermute | solution.py:441
  561.1 19.6 %collective-permute-done.31 = f32[128,2048]{1,0:T(8,128)S(1)} collective-permute-done((f32[128,2048]{1,0:T(8,128)S(1)}, f32[128,2048]{1,0:T(8,128)S(1)}, u32[]{:S(2)}, u32[]{:S(2)}) %collective-permute-start.31) | collective-permute-done | bytes 1048608 | tf_op jit(solution)/shard_map/ppermute | solution.py:441
  582.6 26.1 %collective-permute-done.21 = f32[512,640]{1,0:T(8,128)S(1)} collective-permute-done((f32[512,640]{1,0:T(8,128)S(1)}, f32[512,640]{1,0:T(8,128)S(1)}, u32[]{:S(2)}, u32[]{:S(2)}) %collective-permute-start.21) | collective-permute-done | bytes 1310752 | tf_op jit(solution)/shard_map/ppermute | solution.py:441
  609.5 70.8 %collective-permute-done.24 = f32[512,640]{1,0:T(8,128)S(1)} collective-permute-done((f32[512,640]{1,0:T(8,128)S(1)}, f32[512,640]{1,0:T(8,128)S(1)}, u32[]{:S(2)}, u32[]{:S(2)}) %collective-permute-start.24) | collective-permute-done | bytes 1310752 | tf_op jit(solution)/shard_map/ppermute | solution.py:441
  682.6 3.2 fusion.2
  690.8 21.1 %collective-permute-done.22 = f32[512,640]{1,0:T(8,128)S(1)} collective-permute-done((f32[512,640]{1,0:T(8,128)S(1)}, f32[512,640]{1,0:T(8,128)S(1)}, u32[]{:S(2)}, u32[]{:S(2)}) %collective-permute-start.22) | collective-permute-done | bytes 1310752 | tf_op jit(solution)/shard_map/ppermute | solution.py:444
  712.1 28.0 %collective-permute-done.25 = f32[512,640]{1,0:T(8,128)S(1)} collective-permute-done((f32[512,640]{1,0:T(8,128)S(1)}, f32[512,640]{1,0:T(8,128)S(1)}, u32[]{:S(2)}, u32[]{:S(2)}) %collective-permute-start.25) | collective-permute-done | bytes 1310752 | tf_op jit(solution)/shard_map/ppermute | solution.py:444
  741.8 2.1 copy.15
  743.9 38.9 %collective-permute-done.26 = f32[2,512]{1,0:T(2,128)S(1)} collective-permute-done((f32[2,512]{1,0:T(2,128)S(1)}, f32[2,512]{1,0:T(2,128)S(1)}, u32[]{:S(2)}, u32[]{:S(2)}) %collective-permute-start.26) | collective-permute-done | bytes 4128 | tf_op jit(solution)/shard_map/ppermute | solution.py:444
  783.4 2.5 add.155
  786.0 4.2 pad_maximum_fusion
  (179 shorter events, 57.1 us)
Async XLA Ops:
  9.6 26.3 %collective-permute-start.4 = (bf16[128,4096]{1,0:T(8,128)(2,1)}, bf16[128,4096]{1,0:T(8,128)(2,1)}, u32[]{:S(2)}, u32[]{:S(2)}) collective-permute-start(bf16[128,4096]{1,0:T(8,128)(2,1)} %get-tuple-element.105.g0.refs_8_), channel_id=1, source_target_pairs={{0,2},{2,0},{1,3},{3,1},{4,6},{6,4},{5,7},{7,5}} | collective-permute-start | bytes 3145736 | tf_op jit(solution)/shard_map/ppermute | solution.py:441
  9.7 78.3 %collective-permute-start.3 = (bf16[128,4096]{1,0:T(8,128)(2,1)}, bf16[128,4096]{1,0:T(8,128)(2,1)}, u32[]{:S(2)}, u32[]{:S(2)}) collective-permute-start(bf16[128,4096]{1,0:T(8,128)(2,1)} %get-tuple-element.105.g0.refs_8_), channel_id=1, source_target_pairs={{0,1},{1,0},{2,3},{3,2},{4,5},{5,4},{6,7},{7,6}} | collective-permute-start | bytes 3145736 | tf_op jit(solution)/shard_map/ppermute | solution.py:438
  10.3 43.3 %collective-permute-start.7 = (bf16[640,512]{1,0:T(8,128)(2,1)S(1)}, bf16[640,512]{1,0:T(8,128)(2,1)S(1)}, u32[]{:S(2)}, u32[]{:S(2)}) collective-permute-start(bf16[640,512]{1,0:T(8,128)(2,1)S(1)} %get-tuple-element.109.u0.w0), channel_id=1, source_target_pairs={{0,2},{2,0},{1,3},{3,1},{4,6},{6,4},{5,7},{7,5}} | collective-permute-start | bytes 1966088 | tf_op jit(solution)/shard_map/ppermute | solution.py:441
  12.1 41.5 %collective-permute-start.10 = (bf16[128,640]{1,0:T(8,128)(2,1)}, bf16[128,640]{1,0:T(8,128)(2,1)}, u32[]{:S(2)}, u32[]{:S(2)}) collective-permute-start(bf16[128,640]{1,0:T(8,128)(2,1)} %get-tuple-element.106.w0.refs_2_), channel_id=1, source_target_pairs={{0,2},{2,0},{1,3},{3,1},{4,6},{6,4},{5,7},{7,5}} | collective-permute-start | bytes 491528 | tf_op jit(solution)/shard_map/ppermute | solution.py:441
  15.8 72.4 %collective-permute-start.13 = (bf16[128,4096]{1,0:T(8,128)(2,1)}, bf16[128,4096]{1,0:T(8,128)(2,1)}, u32[]{:S(2)}, u32[]{:S(2)}) collective-permute-start(bf16[128,4096]{1,0:T(8,128)(2,1)} %get-tuple-element.104.g0.refs_6_), channel_id=1, source_target_pairs={{0,2},{2,0},{1,3},{3,1},{4,6},{6,4},{5,7},{7,5}} | collective-permute-start | bytes 3145736 | tf_op jit(solution)/shard_map/ppermute | solution.py:441
  36.0 52.6 %collective-permute-start.5 = (bf16[128,4096]{1,0:T(8,128)(2,1)}, bf16[128,4096]{1,0:T(8,128)(2,1)}, u32[]{:S(2)}, u32[]{:S(2)}) collective-permute-start(bf16[128,4096]{1,0:T(8,128)(2,1)} %collective-permute-done.4.g2.refs_10_), channel_id=1, source_target_pairs={{0,1},{1,0},{2,3},{3,2},{4,5},{5,4},{6,7},{7,6}} | collective-permute-start | bytes 3145736 | tf_op jit(solution)/shard_map/ppermute | solution.py:438
  53.5 34.2 %collective-permute-start.6 = (bf16[640,512]{1,0:T(8,128)(2,1)S(1)}, bf16[640,512]{1,0:T(8,128)(2,1)S(1)}, u32[]{:S(2)}, u32[]{:S(2)}) collective-permute-start(bf16[640,512]{1,0:T(8,128)(2,1)S(1)} %get-tuple-element.109.u0.w0), channel_id=1, source_target_pairs={{0,1},{1,0},{2,3},{3,2},{4,5},{5,4},{6,7},{7,6}} | collective-permute-start | bytes 1966088 | tf_op jit(solution)/shard_map/ppermute | solution.py:438
  53.6 34.8 %collective-permute-start.8 = (bf16[640,512]{1,0:T(8,128)(2,1)S(1)}, bf16[640,512]{1,0:T(8,128)(2,1)S(1)}, u32[]{:S(2)}, u32[]{:S(2)}) collective-permute-start(bf16[640,512]{1,0:T(8,128)(2,1)S(1)} %collective-permute-done.7.u2.w2), channel_id=1, source_target_pairs={{0,1},{1,0},{2,3},{3,2},{4,5},{5,4},{6,7},{7,6}} | collective-permute-start | bytes 1966088 | tf_op jit(solution)/shard_map/ppermute | solution.py:438
  87.7 39.9 %collective-permute-start.9 = (bf16[128,640]{1,0:T(8,128)(2,1)S(1)}, bf16[128,640]{1,0:T(8,128)(2,1)S(1)}, u32[]{:S(2)}, u32[]{:S(2)}) collective-permute-start(bf16[128,640]{1,0:T(8,128)(2,1)S(1)} %copy-done.22), channel_id=1, source_target_pairs={{0,1},{1,0},{2,3},{3,2},{4,5},{5,4},{6,7},{7,6}} | collective-permute-start | bytes 491528 | tf_op jit(solution)/shard_map/ppermute | solution.py:438
  88.0 74.4 %collective-permute-start.12 = (bf16[128,4096]{1,0:T(8,128)(2,1)}, bf16[128,4096]{1,0:T(8,128)(2,1)}, u32[]{:S(2)}, u32[]{:S(2)}) collective-permute-start(bf16[128,4096]{1,0:T(8,128)(2,1)} %get-tuple-element.104.g0.refs_6_), channel_id=1, source_target_pairs={{0,1},{1,0},{2,3},{3,2},{4,5},{5,4},{6,7},{7,6}} | collective-permute-start | bytes 3145736 | tf_op jit(solution)/shard_map/ppermute | solution.py:438
  88.3 39.6 %collective-permute-start.16 = (bf16[640,512]{1,0:T(8,128)(2,1)S(1)}, bf16[640,512]{1,0:T(8,128)(2,1)}, u32[]{:S(2)}, u32[]{:S(2)}) collective-permute-start(bf16[640,512]{1,0:T(8,128)(2,1)S(1)} %get-tuple-element.108.u0.w0), channel_id=1, source_target_pairs={{0,2},{2,0},{1,3},{3,1},{4,6},{6,4},{5,7},{7,5}} | collective-permute-start | bytes 1966088 | tf_op jit(solution)/shard_map/ppermute | solution.py:441
  88.4 39.8 %collective-permute-start.11 = (bf16[128,640]{1,0:T(8,128)(2,1)}, bf16[128,640]{1,0:T(8,128)(2,1)S(1)}, u32[]{:S(2)}, u32[]{:S(2)}) collective-permute-start(bf16[128,640]{1,0:T(8,128)(2,1)} %collective-permute-done.10.w2.refs_4_), channel_id=1, source_target_pairs={{0,1},{1,0},{2,3},{3,2},{4,5},{5,4},{6,7},{7,6}} | collective-permute-start | bytes 491528 | tf_op jit(solution)/shard_map/ppermute | solution.py:438
  88.6 73.9 %collective-permute-start.14 = (bf16[128,4096]{1,0:T(8,128)(2,1)}, bf16[128,4096]{1,0:T(8,128)(2,1)S(1)}, u32[]{:S(2)}, u32[]{:S(2)}) collective-permute-start(bf16[128,4096]{1,0:T(8,128)(2,1)} %collective-permute-done.13.g2.refs_8_), channel_id=1, source_target_pairs={{0,1},{1,0},{2,3},{3,2},{4,5},{5,4},{6,7},{7,6}} | collective-permute-start | bytes 3145736 | tf_op jit(solution)/shard_map/ppermute | solution.py:438
  127.6 34.8 %collective-permute-start.15 = (bf16[640,512]{1,0:T(8,128)(2,1)S(1)}, bf16[640,512]{1,0:T(8,128)(2,1)S(1)}, u32[]{:S(2)}, u32[]{:S(2)}) collective-permute-start(bf16[640,512]{1,0:T(8,128)(2,1)S(1)} %get-tuple-element.108.u0.w0), channel_id=1, source_target_pairs={{0,1},{1,0},{2,3},{3,2},{4,5},{5,4},{6,7},{7,6}} | collective-permute-start | bytes 1966088 | tf_op jit(solution)/shard_map/ppermute | solution.py:438
  127.9 34.6 %collective-permute-start.17 = (bf16[640,512]{1,0:T(8,128)(2,1)}, bf16[640,512]{1,0:T(8,128)(2,1)S(1)}, u32[]{:S(2)}, u32[]{:S(2)}) collective-permute-start(bf16[640,512]{1,0:T(8,128)(2,1)} %collective-permute-done.16.u2.w2), channel_id=1, source_target_pairs={{0,1},{1,0},{2,3},{3,2},{4,5},{5,4},{6,7},{7,6}} | collective-permute-start | bytes 1966088 | tf_op jit(solution)/shard_map/ppermute | solution.py:438
  261.5 274.2 %collective-permute-start.39 = (f32[2,128,4096]{2,1,0:T(8,128)}, f32[2,128,4096]{2,1,0:T(8,128)}, u32[]{:S(2)}, u32[]{:S(2)}) collective-permute-start(f32[2,128,4096]{2,1,0:T(8,128)} %get-tuple-element.96), channel_id=1, source_target_pairs={{0,1},{1,0},{2,3},{3,2},{4,5},{5,4},{6,7},{7,6}} | collective-permute-start | bytes 12582920 | tf_op jit(solution)/shard_map/ppermute | solution.py:438
  475.7 53.5 %collective-permute-start.33 = (f32[2,128,2048]{2,1,0:T(8,128)}, f32[2,128,2048]{2,1,0:T(8,128)}, u32[]{:S(2)}, u32[]{:S(2)}) collective-permute-start(f32[2,128,2048]{2,1,0:T(8,128)} %get-tuple-element.90), channel_id=1, source_target_pairs={{0,1},{1,0},{2,3},{3,2},{4,5},{5,4},{6,7},{7,6}} | collective-permute-start | bytes 6291464 | tf_op jit(solution)/shard_map/ppermute | solution.py:438
  475.8 56.3 %collective-permute-start.30 = (f32[2,128,2048]{2,1,0:T(8,128)}, f32[2,128,2048]{2,1,0:T(8,128)}, u32[]{:S(2)}, u32[]{:S(2)}) collective-permute-start(f32[2,128,2048]{2,1,0:T(8,128)} %get-tuple-element.87), channel_id=1, source_target_pairs={{0,1},{1,0},{2,3},{3,2},{4,5},{5,4},{6,7},{7,6}} | collective-permute-start | bytes 6291464 | tf_op jit(solution)/shard_map/ppermute | solution.py:438
  476.2 22.3 %collective-permute-start.27 = (f32[2,128,640]{2,1,0:T(8,128)}, f32[2,128,640]{2,1,0:T(8,128)S(1)}, u32[]{:S(2)}, u32[]{:S(2)}) collective-permute-start(f32[2,128,640]{2,1,0:T(8,128)} %get-tuple-element.84), channel_id=1, source_target_pairs={{0,1},{1,0},{2,3},{3,2},{4,5},{5,4},{6,7},{7,6}} | collective-permute-start | bytes 1966088 | tf_op jit(solution)/shard_map/ppermute | solution.py:438
  496.9 38.0 %collective-permute-start.20 = (f32[2,512,640]{2,1,0:T(8,128)}, f32[2,512,640]{2,1,0:T(8,128)S(1)}, u32[]{:S(2)}, u32[]{:S(2)}) collective-permute-start(f32[2,512,640]{2,1,0:T(8,128)} %get-tuple-element.77), channel_id=1, source_target_pairs={{0,1},{1,0},{2,3},{3,2},{4,5},{5,4},{6,7},{7,6}} | collective-permute-start | bytes 7864328 | tf_op jit(solution)/shard_map/ppermute | solution.py:438
  529.2 156.6 %collective-permute-start.29 = (f32[128,640]{1,0:T(8,128)S(1)}, f32[128,640]{1,0:T(8,128)S(1)}, u32[]{:S(2)}, u32[]{:S(2)}) collective-permute-start(f32[128,640]{1,0:T(8,128)S(1)} %fusion.21), channel_id=1, source_target_pairs={{0,4},{4,0},{1,5},{5,1},{2,6},{6,2},{3,7},{7,3}} | collective-permute-start | bytes 983048 | tf_op jit(solution)/shard_map/ppermute | solution.py:444
  532.1 26.1 %collective-permute-start.34 = (f32[128,2048]{1,0:T(8,128)S(1)}, f32[128,2048]{1,0:T(8,128)S(1)}, u32[]{:S(2)}, u32[]{:S(2)}) collective-permute-start(f32[128,2048]{1,0:T(8,128)S(1)} %fusion.9), channel_id=1, source_target_pairs={{0,2},{2,0},{1,3},{3,1},{4,6},{6,4},{5,7},{7,5}} | collective-permute-start | bytes 3145736 | tf_op jit(solution)/shard_map/ppermute | solution.py:441
  535.0 45.7 %collective-permute-start.31 = (f32[128,2048]{1,0:T(8,128)S(1)}, f32[128,2048]{1,0:T(8,128)S(1)}, u32[]{:S(2)}, u32[]{:S(2)}) collective-permute-start(f32[128,2048]{1,0:T(8,128)S(1)} %fusion.12), channel_id=1, source_target_pairs={{0,2},{2,0},{1,3},{3,1},{4,6},{6,4},{5,7},{7,5}} | collective-permute-start | bytes 3145736 | tf_op jit(solution)/shard_map/ppermute | solution.py:441
  535.7 73.0 %collective-permute-start.21 = (f32[512,640]{1,0:T(8,128)S(1)}, f32[512,640]{1,0:T(8,128)S(1)}, u32[]{:S(2)}, u32[]{:S(2)}) collective-permute-start(f32[512,640]{1,0:T(8,128)S(1)} %fusion.6), channel_id=1, source_target_pairs={{0,2},{2,0},{1,3},{3,1},{4,6},{6,4},{5,7},{7,5}} | collective-permute-start | bytes 3932168 | tf_op jit(solution)/shard_map/ppermute | solution.py:441
  539.1 142.0 %collective-permute-start.40 = (f32[128,4096]{1,0:T(8,128)S(1)}, f32[128,4096]{1,0:T(8,128)S(1)}, u32[]{:S(2)}, u32[]{:S(2)}) collective-permute-start(f32[128,4096]{1,0:T(8,128)S(1)} %fusion), channel_id=1, source_target_pairs={{0,2},{2,0},{1,3},{3,1},{4,6},{6,4},{5,7},{7,5}} | collective-permute-start | bytes 6291464 | tf_op jit(solution)/shard_map/ppermute | solution.py:441
  558.2 122.1 %collective-permute-start.24 = (f32[512,640]{1,0:T(8,128)S(1)}, f32[512,640]{1,0:T(8,128)S(1)}, u32[]{:S(2)}, u32[]{:S(2)}) collective-permute-start(f32[512,640]{1,0:T(8,128)S(1)} %fusion.3), channel_id=1, source_target_pairs={{0,2},{2,0},{1,3},{3,1},{4,6},{6,4},{5,7},{7,5}} | collective-permute-start | bytes 3932168 | tf_op jit(solution)/shard_map/ppermute | solution.py:441
  580.6 107.3 %collective-permute-start.35 = (f32[128,2048]{1,0:T(8,128)S(1)}, f32[128,2048]{1,0:T(8,128)S(1)}, u32[]{:S(2)}, u32[]{:S(2)}) collective-permute-start(f32[128,2048]{1,0:T(8,128)S(1)} %fusion.11), channel_id=1, source_target_pairs={{0,4},{4,0},{1,5},{5,1},{2,6},{6,2},{3,7},{7,3}} | collective-permute-start | bytes 3145736 | tf_op jit(solution)/shard_map/ppermute | solution.py:444
  608.7 79.4 %collective-permute-start.32 = (f32[128,2048]{1,0:T(8,128)S(1)}, f32[128,2048]{1,0:T(8,128)S(1)}, u32[]{:S(2)}, u32[]{:S(2)}) collective-permute-start(f32[128,2048]{1,0:T(8,128)S(1)} %fusion.14), channel_id=1, source_target_pairs={{0,4},{4,0},{1,5},{5,1},{2,6},{6,2},{3,7},{7,3}} | collective-permute-start | bytes 3145736 | tf_op jit(solution)/shard_map/ppermute | solution.py:444
  680.3 31.6 %collective-permute-start.22 = (f32[512,640]{1,0:T(8,128)S(1)}, f32[512,640]{1,0:T(8,128)S(1)}, u32[]{:S(2)}, u32[]{:S(2)}) collective-permute-start(f32[512,640]{1,0:T(8,128)S(1)} %fusion.8), channel_id=1, source_target_pairs={{0,4},{4,0},{1,5},{5,1},{2,6},{6,2},{3,7},{7,3}} | collective-permute-start | bytes 3932168 | tf_op jit(solution)/shard_map/ppermute | solution.py:444
  681.2 58.8 %collective-permute-start.25 = (f32[512,640]{1,0:T(8,128)S(1)}, f32[512,640]{1,0:T(8,128)S(1)}, u32[]{:S(2)}, u32[]{:S(2)}) collective-permute-start(f32[512,640]{1,0:T(8,128)S(1)} %fusion.5), channel_id=1, source_target_pairs={{0,4},{4,0},{1,5},{5,1},{2,6},{6,2},{3,7},{7,3}} | collective-permute-start | bytes 3932168 | tf_op jit(solution)/shard_map/ppermute | solution.py:444
  685.8 97.5 %collective-permute-start.41 = (f32[128,4096]{1,0:T(8,128)}, f32[128,4096]{1,0:T(8,128)}, u32[]{:S(2)}, u32[]{:S(2)}) collective-permute-start(f32[128,4096]{1,0:T(8,128)} %fusion.2), channel_id=1, source_target_pairs={{0,4},{4,0},{1,5},{5,1},{2,6},{6,2},{3,7},{7,3}} | collective-permute-start | bytes 6291464 | tf_op jit(solution)/shard_map/ppermute | solution.py:444
  740.3 42.5 %collective-permute-start.26 = (f32[2,512]{1,0:T(2,128)S(1)}, f32[2,512]{1,0:T(2,128)S(1)}, u32[]{:S(2)}, u32[]{:S(2)}) collective-permute-start(f32[2,512]{1,0:T(2,128)S(1)} %fusion.25), channel_id=1, source_target_pairs={{0,4},{4,0},{1,5},{5,1},{2,6},{6,2},{3,7},{7,3}} | collective-permute-start | bytes 12296 | tf_op jit(solution)/shard_map/ppermute | solution.py:444
  (43 other events, 755.6 us)

commit v4 on v3

--- a/solution.py
+++ b/solution.py
@@ -399,6 +399,19 @@
     dx_ref[...] = (dy_ref[...].astype(F32) + dx.astype(BF16).astype(F32)).astype(BF16)
 
 
+def place_win_kernel(moves, *refs):
+    out_ref = refs[-1]
+    for k, group in enumerate(moves):
+        a_ref, b_ref = refs[2 * k], refs[2 * k + 1]
+        for src, dst, width in group:
+            out_ref[0, :, dst:dst + width] = a_ref[:, src:src + width] + b_ref[:, src:src + width]
+
+
+def place_wout_kernel(a_ref, b_ref, *rest):
+    out_ref = rest[-1]
+    out_ref[0] = (a_ref[...] + b_ref[...]).T
+
+
 ANY = pl.BlockSpec(memory_space=pl.ANY)
 
 
@@ -451,7 +464,7 @@
         recv = pp_core(send)
         far = pp_x(xp + recv[1])
         mine = own + recv[0] + far
-        return mine + pp_y(mine)
+        return mine, pp_y(mine)
 
     def inner_step(x_in, grad_y, norm_scale, w_in, w_out):
         n_layers = w_in.shape[0]
@@ -525,7 +538,7 @@
                     mm * 8704, n_tok * D * 50,
                 )(dy, h, o, m, z, z, *o_pieces[l])
                 dzs, spans = [dg, du], [(0, FF), (FF, FF)]
-                d_wout[l] = reduce4(*g[:3]).T
+                d_wout[l] = reduce4(*g[:3])
                 win_parts.append(reduce4(*g[3:]))
             else:
                 g = call(
@@ -534,7 +547,7 @@
                     [pltpu.VMEM((D, D + FF), F32), sem((4,))],
                     mm * 2560, n_tok * D * 12,
                 )(dy, o, m)
-                d_wout[l] = reduce4(*g).T
+                d_wout[l] = reduce4(*g)
                 for hf in range(2):
                     dg, du, *g = call(
                         functools.partial(bmlp_kernel, hf), n_tok,
@@ -557,8 +570,8 @@
                 mm * 6200, n_tok * D * 10,
             )(dy, h, qkv, cs_tab, *o_pieces[l])
             wq = reduce4(*g)
-            d_win[l] = jnp.concatenate(
-                [wq] + [p[:, :fw] for p in win_parts] + [p[:, fw:] for p in win_parts], axis=1)
+            d_win[l] = [(wq, ((0, 0, QKV),))] + [
+                (p, ((0, QKV + i * fw, fw), (fw, QKV + FF + i * fw, fw))) for i, p in enumerate(win_parts)]
             dy, d_gain[l] = call(
                 functools.partial(dx_kernel, tuple(spans)), n_tok,
                 [tok_spec(D), full_spec((1, D)), tok_spec(D), tok_spec(QKV)] + [tok_spec(fw)] * len(dzs) + [ANY] * 8,
@@ -568,13 +581,39 @@
                 mm * 4736, n_tok * D * 20,
             )(xl, gain[l], dy, dzq, *dzs, *q_pieces[l], *g_pieces[l])
 
+        g_win, g_wout = None, None
+        rows = D // 4
+        for l in reversed(range(n_layers)):
+            layer_row = functools.partial(lambda layer, i: (layer, i, 0), l)
+            prev = () if g_win is None else (g_win,)
+            args = [a for pair, _ in d_win[l] for a in pair]
+            g_win = pl.pallas_call(
+                functools.partial(place_win_kernel, tuple(m for _, m in d_win[l])),
+                grid=(8,),
+                in_specs=[pl.BlockSpec((rows // 8, a.shape[1]), lambda i: (i, 0)) for a in args] + [ANY] * len(prev),
+                out_specs=pl.BlockSpec((1, rows // 8, QKV + 2 * FF), layer_row),
+                out_shape=jax.ShapeDtypeStruct((n_layers, rows, QKV + 2 * FF), F32),
+                input_output_aliases={len(args): 0} if prev else {},
+                cost_estimate=pl.CostEstimate(flops=10 ** 6, bytes_accessed=10 ** 7, transcendentals=0),
+            )(*args, *prev)
+            prev = () if g_wout is None else (g_wout,)
+            g_wout = pl.pallas_call(
+                place_wout_kernel,
+                grid=(q4 // 128,),
+                in_specs=[pl.BlockSpec((D, 128), lambda i: (0, i))] * 2 + [ANY] * len(prev),
+                out_specs=pl.BlockSpec((1, 128, D), layer_row),
+                out_shape=jax.ShapeDtypeStruct((n_layers, q4, D), F32),
+                input_output_aliases={2: 0} if prev else {},
+                cost_estimate=pl.CostEstimate(flops=10 ** 6, bytes_accessed=4 * 10 ** 6, transcendentals=0),
+            )(*d_wout[l], *prev)
+
         gg = jnp.concatenate(d_gain, axis=0)
         gg = gg + pp_core(gg)
         gg = gg + pp_x(gg)
-        gg, g_wout = lax.optimization_barrier((gg, jnp.stack(d_wout)))
+        gg, g_wout = lax.optimization_barrier((gg, g_wout))
         gg = gg + pp_y(gg)
         gg = lax.dynamic_slice(gg, (0, lax.axis_index("fsdp") * (D // 4)), (n_layers, D // 4))
-        return (x.reshape(x_in.shape), dy.reshape(x_in.shape), gg, jnp.stack(d_win), g_wout)
+        return (x.reshape(x_in.shape), dy.reshape(x_in.shape), gg, g_win, g_wout)
 
     return jax.shard_map(
         inner_step,

time: 799 us -> 784 us (0.981)
  Pallas kernels: 431 us -> 453 us
  waiting for transfers between devices: 281 us -> 265 us
  other arithmetic: 28.9 us -> 15.8 us
    pallas_call x0 -> x4, Pallas kernels: none -> 21.9 us  [the longest x2 12.7 us: inner_step(): pl.pallas_call(functools.partial(place_win_kernel, tuple((m for _, m in d...]
    ppermute x8, waiting for transfers between devices: 94.5 us -> 84.4 us  [pp_y(): return lax.ppermute(a, 'dp', y_perm)]
  transfers between devices with their start and end apart: 42 -> 42, of which waited for: 15 -> 11; matrix products, arithmetic and copies ran while one was open for 4% -> 3% of each run, Pallas kernels for 42% -> 45%
where the time goes in v4:
time: 784 us; the launch traced here: 775 us
  Pallas kernels  453 us (58%)
  waiting for transfers between devices  265 us (34%)
  starting transfers between devices  28.6 us (4%)
  other arithmetic  15.8 us (2%)
  local copies, waits for them, and re-layouts  10.2 us (1%)
    ppermute x14, waiting for transfers between devices, pp_x(): return lax.ppermute(a, 'fsdp', x_perm)  177 us
    pallas_call x2, Pallas kernels, inner_step(): call(battn_kernel, n_tok, [tok_spec(D), tok_spec(D), tok_spec(QKV), full_...  88.4 us
    ppermute x8, waiting for transfers between devices, pp_y(): return lax.ppermute(a, 'dp', y_perm)  84.4 us
    pallas_call x2, Pallas kernels, inner_step(): call(fwd_mlp_kernel, n_tok, [tok_spec(D), tok_spec(D), tok_spec(D)] + [AN...  77 us
    pallas_call x2, Pallas kernels, inner_step(): call(fwd_attn_kernel, n_tok, [tok_spec(D), full_spec((1, D)), full_spec((...  67.5 us
    pallas_call x2, Pallas kernels, inner_step(): call(functools.partial(dx_kernel, tuple(spans)), n_tok, [tok_spec(D), ful...  67.4 us
    pallas_call x1, Pallas kernels, inner_step(): call(bmlp_dwo_kernel, n_tok, [tok_spec(D)] * 3 + [tok_spec(FF), tok_spec(...  59 us
    pallas_call x2, Pallas kernels, inner_step(): call(functools.partial(bmlp_kernel, hf), n_tok, [tok_spec(D), tok_spec(D)...  53.7 us
  transfers between devices with their start and end apart: 42, of which 11 were waited for; matrix products, arithmetic and copies ran while one was open for 3% of the time, Pallas kernels for 45%

profile of v4, /device:TPU:0, one launch (start us, length us, event | category | flops | bytes accessed | tf_op | source)
XLA Modules:
  0.0 774.7 jit_solution(15898472593695996817)
XLA Ops:
  2.5 3.3 collective-permute-start.1
  5.9 3.1 slice_bitcast_fusion.10
  15.1 20.2 %collective-permute-done.4.g2.refs_10_ = bf16[128,4096]{1,0:T(8,128)(2,1)} collective-permute-done((bf16[128,4096]{1,0:T(8,128)(2,1)}, bf16[128,4096]{1,0:T(8,128)(2,1)}, u32[]{:S(2)}, u32[]{:S(2)}) %collective-permute-start.4) | collective-permute-done | bytes 1048608 | tf_op jit(solution)/shard_map/ppermute | solution.py:454
  35.9 16.8 %collective-permute-done.10.w2.refs_4_ = bf16[128,640]{1,0:T(8,128)(2,1)S(1)} collective-permute-done((bf16[128,640]{1,0:T(8,128)(2,1)S(1)}, bf16[128,640]{1,0:T(8,128)(2,1)S(1)}, u32[]{:S(2)}, u32[]{:S(2)}) %collective-permute-start.10) | collective-permute-done | bytes 163872 | tf_op jit(solution)/shard_map/ppermute | solution.py:454
  53.4 33.9 %shard_map.101 = (bf16[4096,512]{1,0:T(8,128)(2,1)}, bf16[4096,640]{1,0:T(8,128)(2,1)}, bf16[4096,512]{1,0:T(8,128)(2,1)}) custom-call(bf16[4096,512]{1,0:T(8,128)(2,1)} %bitcast.103, f32[1,512]{1,0:T(1,128)} %bitcast.96, f32[256,128]{1,0:T(8,128)} %constant.31.clone.cs_ref, bf16[128,768]{1,0:T(8,128)(2,1)} %copy-done.29, bf16[128,768]{1,0:T(8,128)(2,1)} %copy-done.35, ...), custom_call_target="tpu_custom_call" | custom-call | flops 10905190400 | bytes 16777216 | tf_op jit(solution)/shard_map/pallas_call | solution.py:496
  88.9 38.4 %shard_map.102 = (bf16[4096,4096]{1,0:T(8,128)(2,1)}, bf16[4096,2048]{1,0:T(8,128)(2,1)}, bf16[4096,512]{1,0:T(8,128)(2,1)}) custom-call(bf16[4096,512]{1,0:T(8,128)(2,1)} %bitcast.104, bf16[4096,512]{1,0:T(8,128)(2,1)} %get-tuple-element.52.h_ref, bf16[4096,512]{1,0:T(8,128)(2,1)} %get-tuple-element.53.o_ref, ...), custom_call_target="tpu_custom_call" | custom-call | flops 28101836800 | bytes 67108864 | tf_op jit(solution)/shard_map/pallas_call | solution.py:504
  128.6 33.6 %shard_map.103 = (bf16[4096,512]{1,0:T(8,128)(2,1)}, bf16[4096,640]{1,0:T(8,128)(2,1)}, bf16[4096,512]{1,0:T(8,128)(2,1)}) custom-call(bf16[4096,512]{1,0:T(8,128)(2,1)} %get-tuple-element.54.x_ref, f32[1,512]{1,0:T(1,128)} %bitcast.98, f32[256,128]{1,0:T(8,128)} %constant.31.clone.cs_ref, bf16[128,640]{1,0:T(8,128)(2,1)} %copy-done.30, ...), custom_call_target="tpu_custom_call" | custom-call | flops 10905190400 | bytes 16777216 | tf_op jit(solution)/shard_map/pallas_call | solution.py:496
  163.6 38.6 %shard_map.104 = (bf16[4096,4096]{1,0:T(8,128)(2,1)}, bf16[4096,2048]{1,0:T(8,128)(2,1)}, bf16[4096,512]{1,0:T(8,128)(2,1)}) custom-call(bf16[4096,512]{1,0:T(8,128)(2,1)} %get-tuple-element.54.x_ref, bf16[4096,512]{1,0:T(8,128)(2,1)} %get-tuple-element.55.h_ref, bf16[4096,512]{1,0:T(8,128)(2,1)} %get-tuple-element.56.o_ref, ...), custom_call_target="tpu_custom_call" | custom-call | flops 28101836800 | bytes 67108864 | tf_op jit(solution)/shard_map/pallas_call | solution.py:504
  202.2 59.0 %shard_map.106 = (bf16[4096,2048]{1,0:T(8,128)(2,1)}, bf16[4096,2048]{1,0:T(8,128)(2,1)}, f32[512,640]{1,0:T(8,128)}, f32[512,640]{1,0:T(8,128)}, f32[2,512,640]...) custom-call(bf16[4096,512]{1,0:T(8,128)(2,1)} %bitcast.100, ...), custom_call_target="tpu_custom_call" | custom-call | flops 36507222016 | bytes 104857600 | tf_op jit(solution)/shard_map/pallas_call | solution.py:531
  261.3 44.2 %shard_map.105 = (bf16[4096,640]{1,0:T(8,128)(2,1)}, f32[128,640]{1,0:T(8,128)}, f32[128,640]{1,0:T(8,128)}, f32[2,128,640]{2,1,0:T(8,128)}) custom-call(bf16[4096,512]{1,0:T(8,128)(2,1)} %bitcast.101, bf16[4096,512]{1,0:T(8,128)(2,1)} %get-tuple-element.55.h_ref, bf16[4096,640]{1,0:T(8,128)(2,1)} %get-tuple-element.58.qkv_ref, ...), custom_call_target="tpu_custom_call" | custom-call | flops 26004684800 | bytes 20971520 | tf_op jit(solution)/shard_map/pallas_call | solution.py:563
  306.0 33.5 %shard_map.107 = (bf16[4096,512]{1,0:T(8,128)(2,1)}, f32[1,512]{1,0:T(1,128)}) custom-call(bf16[4096,512]{1,0:T(8,128)(2,1)} %get-tuple-element.54.x_ref, f32[1,512]{1,0:T(1,128)} %bitcast.99, bf16[4096,512]{1,0:T(8,128)(2,1)} %bitcast.102, bf16[4096,640]{1,0:T(8,128)(2,1)} %get-tuple-element.59.dzq_ref, bf16[4096,2048]{1,0:T(8,128)(2,1)} %get-tuple-element.62.refs_0_, ...), custom_call_target="tpu_custom_call" | custom-call | flops 19864223744 | bytes 41943040 | tf_op jit(solution)/shard_map/pallas_call | solution.py:575
  339.5 18.4 %shard_map.112 = (f32[512,640]{1,0:T(8,128)}, f32[512,640]{1,0:T(8,128)}, f32[2,512,640]{2,1,0:T(8,128)}) custom-call(bf16[4096,512]{1,0:T(8,128)(2,1)} %get-tuple-element.64.dy_ref, bf16[4096,512]{1,0:T(8,128)(2,1)} %get-tuple-element.53.o_ref, bf16[4096,2048]{1,0:T(8,128)(2,1)} %get-tuple-element.75.m_ref), custom_call_target="tpu_custom_call" | custom-call | flops 10737418240 | bytes 25165824 | tf_op jit(solution)/shard_map/pallas_call | solution.py:544
  358.4 44.2 %shard_map.108 = (bf16[4096,640]{1,0:T(8,128)(2,1)}, f32[128,640]{1,0:T(8,128)}, f32[128,640]{1,0:T(8,128)}, f32[2,128,640]{2,1,0:T(8,128)}) custom-call(bf16[4096,512]{1,0:T(8,128)(2,1)} %get-tuple-element.64.dy_ref, bf16[4096,512]{1,0:T(8,128)(2,1)} %get-tuple-element.52.h_ref, bf16[4096,640]{1,0:T(8,128)(2,1)} %get-tuple-element.65.qkv_ref, ...), custom_call_target="tpu_custom_call" | custom-call | flops 26004684800 | bytes 20971520 | tf_op jit(solution)/shard_map/pallas_call | solution.py:563
  402.6 26.8 %shard_map.110 = (bf16[4096,1024]{1,0:T(8,128)(2,1)}, bf16[4096,1024]{1,0:T(8,128)(2,1)}, f32[128,2048]{1,0:T(8,128)}, f32[128,2048]{1,0:T(8,128)}, f32[2,128,2048]{2,1,0:T(8,128)}) custom-call(bf16[4096,512]{1,0:T(8,128)(2,1)} %get-tuple-element.64.dy_ref, bf16[4096,512]{1,0:T(8,128)(2,1)} %get-tuple-element.52.h_ref, ...), custom_call_target="tpu_custom_call" | custom-call | flops 12884901888 | bytes 41943040 | tf_op jit(solution)/shard_map/pallas_call | solution.py:552
  429.4 26.9 %shard_map.109 = (bf16[4096,1024]{1,0:T(8,128)(2,1)}, bf16[4096,1024]{1,0:T(8,128)(2,1)}, f32[128,2048]{1,0:T(8,128)}, f32[128,2048]{1,0:T(8,128)}, f32[2,128,2048]{2,1,0:T(8,128)}) custom-call(bf16[4096,512]{1,0:T(8,128)(2,1)} %get-tuple-element.64.dy_ref, bf16[4096,512]{1,0:T(8,128)(2,1)} %get-tuple-element.52.h_ref, ...), custom_call_target="tpu_custom_call" | custom-call | flops 12884901888 | bytes 41943040 | tf_op jit(solution)/shard_map/pallas_call | solution.py:552
  456.4 33.9 %shard_map.111 = (bf16[4096,512]{1,0:T(8,128)(2,1)}, f32[1,512]{1,0:T(1,128)}) custom-call(bf16[4096,512]{1,0:T(8,128)(2,1)} %bitcast.105, f32[1,512]{1,0:T(1,128)} %bitcast.97, bf16[4096,512]{1,0:T(8,128)(2,1)} %get-tuple-element.64.dy_ref, bf16[4096,640]{1,0:T(8,128)(2,1)} %get-tuple-element.66.dzq_ref, bf16[4096,1024]{1,0:T(8,128)(2,1)} %get-tuple-element.68.refs_0_, ...), custom_call_target="tpu_custom_call" | custom-call | flops 19864223744 | bytes 41943040 | tf_op jit(solution)/shard_map/pallas_call | solution.py:575
  495.5 1.8 collective-permute-start.19
  497.3 2.6 fusion
  500.3 1.9 collective-permute-start.24
  504.1 1.8 collective-permute-start.34
  506.0 70.5 %collective-permute-done.24 = f32[512,640]{1,0:T(8,128)S(1)} collective-permute-done((f32[512,640]{1,0:T(8,128)S(1)}, f32[512,640]{1,0:T(8,128)S(1)}, u32[]{:S(2)}, u32[]{:S(2)}) %collective-permute-start.24) | collective-permute-done | bytes 1310752 | tf_op jit(solution)/shard_map/ppermute | solution.py:454
  576.9 27.7 %collective-permute-done.21 = f32[512,640]{1,0:T(8,128)S(1)} collective-permute-done((f32[512,640]{1,0:T(8,128)S(1)}, f32[512,640]{1,0:T(8,128)S(1)}, u32[]{:S(2)}, u32[]{:S(2)}) %collective-permute-start.21) | collective-permute-done | bytes 1310752 | tf_op jit(solution)/shard_map/ppermute | solution.py:454
  606.1 2.7 fusion.8.a_ref
  609.4 2.0 fusion.2.refs_2_
  611.4 15.7 %collective-permute-done.34 = f32[128,2048]{1,0:T(8,128)S(1)} collective-permute-done((f32[128,2048]{1,0:T(8,128)S(1)}, f32[128,2048]{1,0:T(8,128)S(1)}, u32[]{:S(2)}, u32[]{:S(2)}) %collective-permute-start.34) | collective-permute-done | bytes 1048608 | tf_op jit(solution)/shard_map/ppermute | solution.py:454
  629.8 18.8 %collective-permute-done.31 = f32[128,2048]{1,0:T(8,128)S(1)} collective-permute-done((f32[128,2048]{1,0:T(8,128)S(1)}, f32[128,2048]{1,0:T(8,128)S(1)}, u32[]{:S(2)}, u32[]{:S(2)}) %collective-permute-start.31) | collective-permute-done | bytes 1048608 | tf_op jit(solution)/shard_map/ppermute | solution.py:454
  651.8 7.4 collective-permute-done.37
  661.9 4.7 shard_map.113.rest_0_
  667.6 4.6 shard_map.114
  674.3 84.3 %collective-permute-done.26 = f32[2,512]{1,0:T(2,128)S(1)} collective-permute-done((f32[2,512]{1,0:T(2,128)S(1)}, f32[2,512]{1,0:T(2,128)S(1)}, u32[]{:S(2)}, u32[]{:S(2)}) %collective-permute-start.26) | collective-permute-done | bytes 4128 | tf_op jit(solution)/shard_map/ppermute | solution.py:457
  760.8 6.3 shard_map.115.refs_6_
  767.8 6.4 shard_map.116
  (192 shorter events, 39.1 us)
Async XLA Ops:
  8.9 26.3 %collective-permute-start.4 = (bf16[128,4096]{1,0:T(8,128)(2,1)}, bf16[128,4096]{1,0:T(8,128)(2,1)}, u32[]{:S(2)}, u32[]{:S(2)}) collective-permute-start(bf16[128,4096]{1,0:T(8,128)(2,1)} %get-tuple-element.100.g0.refs_8_), channel_id=1, source_target_pairs={{0,2},{2,0},{1,3},{3,1},{4,6},{6,4},{5,7},{7,5}} | collective-permute-start | bytes 3145736 | tf_op jit(solution)/shard_map/ppermute | solution.py:454
  9.1 78.5 %collective-permute-start.3 = (bf16[128,4096]{1,0:T(8,128)(2,1)}, bf16[128,4096]{1,0:T(8,128)(2,1)}, u32[]{:S(2)}, u32[]{:S(2)}) collective-permute-start(bf16[128,4096]{1,0:T(8,128)(2,1)} %get-tuple-element.100.g0.refs_8_), channel_id=1, source_target_pairs={{0,1},{1,0},{2,3},{3,2},{4,5},{5,4},{6,7},{7,6}} | collective-permute-start | bytes 3145736 | tf_op jit(solution)/shard_map/ppermute | solution.py:451
  9.6 43.8 %collective-permute-start.7 = (bf16[640,512]{1,0:T(8,128)(2,1)S(1)}, bf16[640,512]{1,0:T(8,128)(2,1)S(1)}, u32[]{:S(2)}, u32[]{:S(2)}) collective-permute-start(bf16[640,512]{1,0:T(8,128)(2,1)S(1)} %get-tuple-element.104.u0.w0), channel_id=1, source_target_pairs={{0,2},{2,0},{1,3},{3,1},{4,6},{6,4},{5,7},{7,5}} | collective-permute-start | bytes 1966088 | tf_op jit(solution)/shard_map/ppermute | solution.py:454
  11.4 41.4 %collective-permute-start.10 = (bf16[128,640]{1,0:T(8,128)(2,1)S(1)}, bf16[128,640]{1,0:T(8,128)(2,1)S(1)}, u32[]{:S(2)}, u32[]{:S(2)}) collective-permute-start(bf16[128,640]{1,0:T(8,128)(2,1)S(1)} %get-tuple-element.101.w0.refs_2_), channel_id=1, source_target_pairs={{0,2},{2,0},{1,3},{3,1},{4,6},{6,4},{5,7},{7,5}} | collective-permute-start | bytes 491528 | tf_op jit(solution)/shard_map/ppermute | solution.py:454
  14.0 73.9 %collective-permute-start.13 = (bf16[128,4096]{1,0:T(8,128)(2,1)}, bf16[128,4096]{1,0:T(8,128)(2,1)}, u32[]{:S(2)}, u32[]{:S(2)}) collective-permute-start(bf16[128,4096]{1,0:T(8,128)(2,1)} %get-tuple-element.99.g0.refs_6_), channel_id=1, source_target_pairs={{0,2},{2,0},{1,3},{3,1},{4,6},{6,4},{5,7},{7,5}} | collective-permute-start | bytes 3145736 | tf_op jit(solution)/shard_map/ppermute | solution.py:454
  35.3 52.9 %collective-permute-start.5 = (bf16[128,4096]{1,0:T(8,128)(2,1)}, bf16[128,4096]{1,0:T(8,128)(2,1)}, u32[]{:S(2)}, u32[]{:S(2)}) collective-permute-start(bf16[128,4096]{1,0:T(8,128)(2,1)} %collective-permute-done.4.g2.refs_10_), channel_id=1, source_target_pairs={{0,1},{1,0},{2,3},{3,2},{4,5},{5,4},{6,7},{7,6}} | collective-permute-start | bytes 3145736 | tf_op jit(solution)/shard_map/ppermute | solution.py:451
  52.7 34.6 %collective-permute-start.6 = (bf16[640,512]{1,0:T(8,128)(2,1)S(1)}, bf16[640,512]{1,0:T(8,128)(2,1)S(1)}, u32[]{:S(2)}, u32[]{:S(2)}) collective-permute-start(bf16[640,512]{1,0:T(8,128)(2,1)S(1)} %get-tuple-element.104.u0.w0), channel_id=1, source_target_pairs={{0,1},{1,0},{2,3},{3,2},{4,5},{5,4},{6,7},{7,6}} | collective-permute-start | bytes 1966088 | tf_op jit(solution)/shard_map/ppermute | solution.py:451
  53.4 34.7 %collective-permute-start.8 = (bf16[640,512]{1,0:T(8,128)(2,1)S(1)}, bf16[640,512]{1,0:T(8,128)(2,1)S(1)}, u32[]{:S(2)}, u32[]{:S(2)}) collective-permute-start(bf16[640,512]{1,0:T(8,128)(2,1)S(1)} %collective-permute-done.7.u2.w2), channel_id=1, source_target_pairs={{0,1},{1,0},{2,3},{3,2},{4,5},{5,4},{6,7},{7,6}} | collective-permute-start | bytes 1966088 | tf_op jit(solution)/shard_map/ppermute | solution.py:451
  87.4 40.0 %collective-permute-start.9 = (bf16[128,640]{1,0:T(8,128)(2,1)S(1)}, bf16[128,640]{1,0:T(8,128)(2,1)S(1)}, u32[]{:S(2)}, u32[]{:S(2)}) collective-permute-start(bf16[128,640]{1,0:T(8,128)(2,1)S(1)} %copy-done.31), channel_id=1, source_target_pairs={{0,1},{1,0},{2,3},{3,2},{4,5},{5,4},{6,7},{7,6}} | collective-permute-start | bytes 491528 | tf_op jit(solution)/shard_map/ppermute | solution.py:451
  87.6 74.5 %collective-permute-start.12 = (bf16[128,4096]{1,0:T(8,128)(2,1)}, bf16[128,4096]{1,0:T(8,128)(2,1)}, u32[]{:S(2)}, u32[]{:S(2)}) collective-permute-start(bf16[128,4096]{1,0:T(8,128)(2,1)} %get-tuple-element.99.g0.refs_6_), channel_id=1, source_target_pairs={{0,1},{1,0},{2,3},{3,2},{4,5},{5,4},{6,7},{7,6}} | collective-permute-start | bytes 3145736 | tf_op jit(solution)/shard_map/ppermute | solution.py:451
  87.9 39.6 %collective-permute-start.16 = (bf16[640,512]{1,0:T(8,128)(2,1)S(1)}, bf16[640,512]{1,0:T(8,128)(2,1)}, u32[]{:S(2)}, u32[]{:S(2)}) collective-permute-start(bf16[640,512]{1,0:T(8,128)(2,1)S(1)} %get-tuple-element.103.u0.w0), channel_id=1, source_target_pairs={{0,2},{2,0},{1,3},{3,1},{4,6},{6,4},{5,7},{7,5}} | collective-permute-start | bytes 1966088 | tf_op jit(solution)/shard_map/ppermute | solution.py:454
  88.1 39.8 %collective-permute-start.11 = (bf16[128,640]{1,0:T(8,128)(2,1)S(1)}, bf16[128,640]{1,0:T(8,128)(2,1)S(1)}, u32[]{:S(2)}, u32[]{:S(2)}) collective-permute-start(bf16[128,640]{1,0:T(8,128)(2,1)S(1)} %copy-done.42), channel_id=1, source_target_pairs={{0,1},{1,0},{2,3},{3,2},{4,5},{5,4},{6,7},{7,6}} | collective-permute-start | bytes 491528 | tf_op jit(solution)/shard_map/ppermute | solution.py:451
  88.2 74.0 %collective-permute-start.14 = (bf16[128,4096]{1,0:T(8,128)(2,1)}, bf16[128,4096]{1,0:T(8,128)(2,1)S(1)}, u32[]{:S(2)}, u32[]{:S(2)}) collective-permute-start(bf16[128,4096]{1,0:T(8,128)(2,1)} %collective-permute-done.13.g2.refs_8_), channel_id=1, source_target_pairs={{0,1},{1,0},{2,3},{3,2},{4,5},{5,4},{6,7},{7,6}} | collective-permute-start | bytes 3145736 | tf_op jit(solution)/shard_map/ppermute | solution.py:451
  127.4 34.8 %collective-permute-start.15 = (bf16[640,512]{1,0:T(8,128)(2,1)S(1)}, bf16[640,512]{1,0:T(8,128)(2,1)S(1)}, u32[]{:S(2)}, u32[]{:S(2)}) collective-permute-start(bf16[640,512]{1,0:T(8,128)(2,1)S(1)} %get-tuple-element.103.u0.w0), channel_id=1, source_target_pairs={{0,1},{1,0},{2,3},{3,2},{4,5},{5,4},{6,7},{7,6}} | collective-permute-start | bytes 1966088 | tf_op jit(solution)/shard_map/ppermute | solution.py:451
  127.5 34.7 %collective-permute-start.17 = (bf16[640,512]{1,0:T(8,128)(2,1)}, bf16[640,512]{1,0:T(8,128)(2,1)S(1)}, u32[]{:S(2)}, u32[]{:S(2)}) collective-permute-start(bf16[640,512]{1,0:T(8,128)(2,1)} %collective-permute-done.16.u2.w2), channel_id=1, source_target_pairs={{0,1},{1,0},{2,3},{3,2},{4,5},{5,4},{6,7},{7,6}} | collective-permute-start | bytes 1966088 | tf_op jit(solution)/shard_map/ppermute | solution.py:451
  261.2 234.3 %collective-permute-start.39 = (f32[2,128,4096]{2,1,0:T(8,128)}, f32[2,128,4096]{2,1,0:T(8,128)}, u32[]{:S(2)}, u32[]{:S(2)}) collective-permute-start(f32[2,128,4096]{2,1,0:T(8,128)} %get-tuple-element.96), channel_id=1, source_target_pairs={{0,1},{1,0},{2,3},{3,2},{4,5},{5,4},{6,7},{7,6}} | collective-permute-start | bytes 12582920 | tf_op jit(solution)/shard_map/ppermute | solution.py:451
  305.5 187.5 %collective-permute-start.36 = (f32[2,128,640]{2,1,0:T(8,128)}, f32[2,128,640]{2,1,0:T(8,128)S(1)}, u32[]{:S(2)}, u32[]{:S(2)}) collective-permute-start(f32[2,128,640]{2,1,0:T(8,128)} %get-tuple-element.93), channel_id=1, source_target_pairs={{0,1},{1,0},{2,3},{3,2},{4,5},{5,4},{6,7},{7,6}} | collective-permute-start | bytes 1966088 | tf_op jit(solution)/shard_map/ppermute | solution.py:451
  306.0 193.9 %collective-permute-start.23 = (f32[2,512,640]{2,1,0:T(8,128)}, f32[2,512,640]{2,1,0:T(8,128)S(1)}, u32[]{:S(2)}, u32[]{:S(2)}) collective-permute-start(f32[2,512,640]{2,1,0:T(8,128)} %get-tuple-element.80), channel_id=1, source_target_pairs={{0,1},{1,0},{2,3},{3,2},{4,5},{5,4},{6,7},{7,6}} | collective-permute-start | bytes 7864328 | tf_op jit(solution)/shard_map/ppermute | solution.py:451
  357.9 142.4 %collective-permute-start.20 = (f32[2,512,640]{2,1,0:T(8,128)}, f32[2,512,640]{2,1,0:T(8,128)}, u32[]{:S(2)}, u32[]{:S(2)}) collective-permute-start(f32[2,512,640]{2,1,0:T(8,128)} %get-tuple-element.77), channel_id=1, source_target_pairs={{0,1},{1,0},{2,3},{3,2},{4,5},{5,4},{6,7},{7,6}} | collective-permute-start | bytes 7864328 | tf_op jit(solution)/shard_map/ppermute | solution.py:451
  495.5 154.6 %collective-permute-start.19 = (f32[2,512]{1,0:T(2,128)S(1)}, f32[2,512]{1,0:T(2,128)S(1)}, u32[]{:S(2)}, u32[]{:S(2)}) collective-permute-start(f32[2,512]{1,0:T(2,128)S(1)} %fusion.23), channel_id=1, source_target_pairs={{0,2},{2,0},{1,3},{3,1},{4,6},{6,4},{5,7},{7,5}} | collective-permute-start | bytes 12296 | tf_op jit(solution)/shard_map/ppermute | solution.py:454
  499.9 109.0 %collective-permute-start.40 = (f32[128,4096]{1,0:T(8,128)S(1)}, f32[128,4096]{1,0:T(8,128)S(1)}, u32[]{:S(2)}, u32[]{:S(2)}) collective-permute-start(f32[128,4096]{1,0:T(8,128)S(1)} %fusion), channel_id=1, source_target_pairs={{0,2},{2,0},{1,3},{3,1},{4,6},{6,4},{5,7},{7,5}} | collective-permute-start | bytes 6291464 | tf_op jit(solution)/shard_map/ppermute | solution.py:454
  500.3 76.2 %collective-permute-start.24 = (f32[512,640]{1,0:T(8,128)S(1)}, f32[512,640]{1,0:T(8,128)S(1)}, u32[]{:S(2)}, u32[]{:S(2)}) collective-permute-start(f32[512,640]{1,0:T(8,128)S(1)} %fusion.3), channel_id=1, source_target_pairs={{0,2},{2,0},{1,3},{3,1},{4,6},{6,4},{5,7},{7,5}} | collective-permute-start | bytes 3932168 | tf_op jit(solution)/shard_map/ppermute | solution.py:454
  503.6 101.0 %collective-permute-start.21 = (f32[512,640]{1,0:T(8,128)S(1)}, f32[512,640]{1,0:T(8,128)S(1)}, u32[]{:S(2)}, u32[]{:S(2)}) collective-permute-start(f32[512,640]{1,0:T(8,128)S(1)} %fusion.6), channel_id=1, source_target_pairs={{0,2},{2,0},{1,3},{3,1},{4,6},{6,4},{5,7},{7,5}} | collective-permute-start | bytes 3932168 | tf_op jit(solution)/shard_map/ppermute | solution.py:454
  504.1 123.0 %collective-permute-start.34 = (f32[128,2048]{1,0:T(8,128)S(1)}, f32[128,2048]{1,0:T(8,128)S(1)}, u32[]{:S(2)}, u32[]{:S(2)}) collective-permute-start(f32[128,2048]{1,0:T(8,128)S(1)} %fusion.9), channel_id=1, source_target_pairs={{0,2},{2,0},{1,3},{3,1},{4,6},{6,4},{5,7},{7,5}} | collective-permute-start | bytes 3145736 | tf_op jit(solution)/shard_map/ppermute | solution.py:454
  576.5 72.1 %collective-permute-start.31 = (f32[128,2048]{1,0:T(8,128)S(1)}, f32[128,2048]{1,0:T(8,128)S(1)}, u32[]{:S(2)}, u32[]{:S(2)}) collective-permute-start(f32[128,2048]{1,0:T(8,128)S(1)} %fusion.12), channel_id=1, source_target_pairs={{0,2},{2,0},{1,3},{3,1},{4,6},{6,4},{5,7},{7,5}} | collective-permute-start | bytes 3145736 | tf_op jit(solution)/shard_map/ppermute | solution.py:454
  604.6 56.1 %collective-permute-start.25 = (f32[512,640]{1,0:T(8,128)S(1)}, f32[512,640]{1,0:T(8,128)S(1)}, u32[]{:S(2)}, u32[]{:S(2)}) collective-permute-start(f32[512,640]{1,0:T(8,128)S(1)} %fusion.5.a_ref), channel_id=1, source_target_pairs={{0,4},{4,0},{1,5},{5,1},{2,6},{6,2},{3,7},{7,3}} | collective-permute-start | bytes 3932168 | tf_op jit(solution)/shard_map/ppermute | solution.py:457
  608.9 57.7 %collective-permute-start.22 = (f32[512,640]{1,0:T(8,128)}, f32[512,640]{1,0:T(8,128)}, u32[]{:S(2)}, u32[]{:S(2)}) collective-permute-start(f32[512,640]{1,0:T(8,128)} %fusion.8.a_ref), channel_id=1, source_target_pairs={{0,4},{4,0},{1,5},{5,1},{2,6},{6,2},{3,7},{7,3}} | collective-permute-start | bytes 3932168 | tf_op jit(solution)/shard_map/ppermute | solution.py:457
  627.1 133.7 %collective-permute-start.41 = (f32[128,4096]{1,0:T(8,128)S(1)}, f32[128,4096]{1,0:T(8,128)}, u32[]{:S(2)}, u32[]{:S(2)}) collective-permute-start(f32[128,4096]{1,0:T(8,128)S(1)} %fusion.2.refs_2_), channel_id=1, source_target_pairs={{0,4},{4,0},{1,5},{5,1},{2,6},{6,2},{3,7},{7,3}} | collective-permute-start | bytes 6291464 | tf_op jit(solution)/shard_map/ppermute | solution.py:457
  659.2 107.9 %collective-permute-start.35 = (f32[128,2048]{1,0:T(8,128)}, f32[128,2048]{1,0:T(8,128)}, u32[]{:S(2)}, u32[]{:S(2)}) collective-permute-start(f32[128,2048]{1,0:T(8,128)} %fusion.11.refs_4_), channel_id=1, source_target_pairs={{0,4},{4,0},{1,5},{5,1},{2,6},{6,2},{3,7},{7,3}} | collective-permute-start | bytes 3145736 | tf_op jit(solution)/shard_map/ppermute | solution.py:457
  660.7 106.4 %collective-permute-start.32 = (f32[128,2048]{1,0:T(8,128)}, f32[128,2048]{1,0:T(8,128)}, u32[]{:S(2)}, u32[]{:S(2)}) collective-permute-start(f32[128,2048]{1,0:T(8,128)} %fusion.14.refs_2_), channel_id=1, source_target_pairs={{0,4},{4,0},{1,5},{5,1},{2,6},{6,2},{3,7},{7,3}} | collective-permute-start | bytes 3145736 | tf_op jit(solution)/shard_map/ppermute | solution.py:457
  666.6 94.2 %collective-permute-start.38 = (f32[128,640]{1,0:T(8,128)S(1)}, f32[128,640]{1,0:T(8,128)}, u32[]{:S(2)}, u32[]{:S(2)}) collective-permute-start(f32[128,640]{1,0:T(8,128)S(1)} %fusion.18.refs_0_), channel_id=1, source_target_pairs={{0,4},{4,0},{1,5},{5,1},{2,6},{6,2},{3,7},{7,3}} | collective-permute-start | bytes 983048 | tf_op jit(solution)/shard_map/ppermute | solution.py:457
  672.1 86.5 %collective-permute-start.26 = (f32[2,512]{1,0:T(2,128)S(1)}, f32[2,512]{1,0:T(2,128)S(1)}, u32[]{:S(2)}, u32[]{:S(2)}) collective-permute-start(f32[2,512]{1,0:T(2,128)S(1)} %fusion.25), channel_id=1, source_target_pairs={{0,4},{4,0},{1,5},{5,1},{2,6},{6,2},{3,7},{7,3}} | collective-permute-start | bytes 12296 | tf_op jit(solution)/shard_map/ppermute | solution.py:457
  (55 other events, 952.7 us)
